TPU v7x, 32 devices: a whole 2x2x4 slice. The times are simulated.
32 devices in a mesh: field: 2 (over core), dom: 16 (over z, y, x).
Axes of the slice: x: 2, y: 2, z: 4, core: 2. Of those that a mesh axis runs over, the one named last changes fastest.
Arguments:
- modes: float32 [2, 40, 131072], P('field', None, 'dom'), may hold values from -6 to 6
- previous: float32 [2, 40, 131072], P('field', None, 'dom'), may hold values from -6 to 6
- kinds: int32 [2, 3, 256], P('field'), may hold values from 0 to 3
- scales: float32 [2, 3, 256], P('field'), may hold values from 0.5 to 4
- tables: bfloat16 [2, 3, 4, 512, 512], P('field'), may hold values from -2 to 6, as said below
- wet_rows: int32 [2, 49152], P('field', 'dom'), may hold values from 0 to 8191, as said below
- wet_counts: int32 [16], P('dom'), may hold values from 768 to 3072, as said below
- coupling: float32 [49152], P('dom'), may hold values from -6 to 6
Outputs:
- basis: float32 [2, 120, 131072], P('field', None, 'dom')
- projected: float32 [120, 120], replicated
Inputs may be any that keep to these rules, and one draw needn't show every extreme that they name: `tables`: tables of offset 0 are symmetric. `wet_rows`: within each subdomain and field the 3072 row numbers are distinct. `wet_counts`: some subdomain uses all 3072 slots.
All inputs are finite; a program needn't handle non-finite values.
Results may differ from a plain program's by a relative error of at most 0.00045.
The roundings to bfloat16 on the way count: a program that leaves them out, or rounds other values in their place, can miss the bound.
Values may be sent and summed in bfloat16 or wider, within the bound.
A program may use at most 192 MiB of HBM per device.

v0:
```python
import functools

import jax
import jax.numpy as jnp
from jax import lax
from jax.experimental import pallas as pl
from jax.experimental.pallas import tpu as pltpu
from jax.sharding import PartitionSpec as P

BS = 512
LANES = 128
SHIFT = 16


def swapped(shard, axis, apart):
    return lax.ppermute(shard, axis, [(i, i ^ 1 << apart) for i in range(lax.axis_size(axis))])


def halos(cells, axis, dim, width):
    count = lax.axis_size(axis)
    ends = count - 1
    head = lax.slice_in_dim(cells, 0, width, axis=dim)
    tail = lax.slice_in_dim(cells, cells.shape[dim] - width, cells.shape[dim], axis=dim)
    return (
        lax.ppermute(tail, axis, [(i, i + 1) for i in range(ends)]),
        lax.ppermute(head, axis, [(i + 1, i) for i in range(ends)]),
    )


def sum_kernel(rounds, split, x_ref, o_ref, held, landed, across, send_sem, recv_sem, side_send, side_recv):
    field = lax.axis_index("field")
    dom = lax.axis_index("dom")
    groups = []
    for step, members in rounds:
        low = (1 - 2 * ((dom // step) % 2)) * step
        high = (1 - 2 * ((dom // (2 * step)) % 2)) * 2 * step
        groups.append([dom + (e % 2) * low + (e // 2) * high for e in range(1, members)])
    barrier = pltpu.get_barrier_semaphore()
    peers = [(1 - field, dom)] + [(field, peer) for group in groups for peer in group]
    for peer in peers:
        pl.semaphore_signal(barrier, inc=1, device_id=peer, device_id_type=pl.DeviceIdType.MESH)
    pl.semaphore_wait(barrier, len(peers))

    def send(source, target, sems, peer):
        copy = pltpu.make_async_remote_copy(
            src_ref=source,
            dst_ref=target,
            send_sem=sems[0],
            recv_sem=sems[1],
            device_id=peer,
            device_id_type=pl.DeviceIdType.MESH,
        )
        copy.start()
        return copy

    mine, theirs = (field, 1 - field) if split else (0, 0)
    copy = send(
        x_ref.at[theirs], across.at[0], (side_send.at[0], side_recv.at[0]), (1 - field, dom)
    )
    copy.wait()
    total = x_ref[mine] + across[0]
    for turn, group in enumerate(groups):
        held[turn] = total
        copies = [
            send(
                held.at[turn],
                landed.at[turn, e],
                (send_sem.at[turn, e], recv_sem.at[turn, e]),
                (field, peer),
            )
            for e, peer in enumerate(group)
        ]
        for copy in copies:
            copy.wait()
        total = total + landed[turn, 0]
        if len(group) == 3:
            total = total + (landed[turn, 1] + landed[turn, 2])
    o_ref[mine] = total
    if split:
        held[len(groups)] = total
        copy = send(
            held.at[len(groups)],
            across.at[1],
            (side_send.at[1], side_recv.at[1]),
            (1 - field, dom),
        )
        copy.wait()
        o_ref[theirs] = across[1]


def summed_everywhere(x, collective_id):
    bits = (lax.axis_size("dom") - 1).bit_length()
    rounds = [(1 << bit, 4 if bit + 1 < bits else 2) for bit in range(0, bits, 2)]
    cell = x.shape[1:]
    slots = len(rounds)
    return pl.pallas_call(
        functools.partial(sum_kernel, rounds, x.shape[0] == 2),
        out_shape=jax.ShapeDtypeStruct(x.shape, x.dtype),
        in_specs=[pl.BlockSpec(memory_space=pltpu.VMEM)],
        out_specs=pl.BlockSpec(memory_space=pltpu.VMEM),
        scratch_shapes=[
            pltpu.VMEM((slots + 1,) + cell, x.dtype),
            pltpu.VMEM((slots, 3) + cell, x.dtype),
            pltpu.VMEM((2,) + cell, x.dtype),
            pltpu.SemaphoreType.DMA((slots, 3)),
            pltpu.SemaphoreType.DMA((slots, 3)),
            pltpu.SemaphoreType.DMA((2,)),
            pltpu.SemaphoreType.DMA((2,)),
        ],
        compiler_params=pltpu.CompilerParams(
            collective_id=collective_id, has_side_effects=True
        ),
    )(x)


NN = (((1,), (0,)), ((), ()))
NT = (((1,), (1,)), ((), ()))


def operator_kernel(
    kinds, scales, places, weights, x_ref, before, after, other, tables, o_ref, window, rows_in, rows_out
):
    columns, wide = x_ref.shape
    nbr = wide // BS
    share = places.shape[0] // nbr
    window[:, : 2 * BS] = before[...]
    window[:, 2 * BS : 2 * BS + wide] = x_ref[...].astype(jnp.bfloat16)
    window[:, 2 * BS + wide :] = after[...]
    blank = jnp.zeros((LANES - columns, LANES), jnp.float32)

    def turn_in(tile, carry):
        span = pl.ds(pl.multiple_of(tile * LANES, LANES), LANES)
        cell = jnp.concatenate([other[:, span].astype(jnp.float32), blank], axis=0)
        rows_in[span, :] = cell.T
        rows_out[span, :] = jnp.zeros((LANES, LANES), jnp.float32)
        return carry

    lax.fori_loop(0, wide // LANES, turn_in, 0, unroll=16)

    def term(n, shift, offset, at, dims):
        block = window[:, pl.ds(pl.multiple_of((n + 2 + shift) * BS, BS), BS)]
        product = lax.dot_general(
            block, tables[offset, kinds[offset, at]], dims, preferred_element_type=jnp.float32
        )
        return scales[offset, at] * product

    def step(n, carry):
        total = term(n, 0, 0, n + 2, NN)
        for offset in (1, 2):
            total = total + term(n, offset, offset, n + 2, NT)
            total = total + term(n, -offset, offset, n + 2 - offset, NN)
        o_ref[:, pl.ds(pl.multiple_of(n * BS, BS), BS)] = total
        for slot in range(share):
            place = places[n * share + slot]
            source = lax.shift_right_logical(place, SHIFT)
            target = lax.bitwise_and(place, (1 << SHIFT) - 1)
            rows_out[pl.ds(target, 1), :] = rows_in[pl.ds(source, 1), :] * weights[n * share + slot]
        return carry

    lax.fori_loop(0, nbr, step, 0)

    def turn_out(tile, carry):
        span = pl.ds(pl.multiple_of(tile * LANES, LANES), LANES)
        o_ref[:, span] = o_ref[:, span] + rows_out[span, :].T[:columns]
        return carry

    lax.fori_loop(0, wide // LANES, turn_out, 0, unroll=16)


def operate(vectors, kinds, scales, tables, places, weights):
    columns, wide = vectors.shape
    rounded = vectors.astype(jnp.bfloat16)
    other = swapped(rounded, "field", 0)
    before, after = halos(rounded, "dom", 1, 2 * BS)
    smem = pl.BlockSpec(memory_space=pltpu.SMEM)
    vmem = pl.BlockSpec(memory_space=pltpu.VMEM)
    return pl.pallas_call(
        operator_kernel,
        out_shape=jax.ShapeDtypeStruct((columns, wide), jnp.float32),
        in_specs=[smem, smem, smem, smem, vmem, vmem, vmem, vmem, vmem],
        out_specs=vmem,
        scratch_shapes=[
            pltpu.VMEM((columns, wide + 4 * BS), jnp.bfloat16),
            pltpu.VMEM((wide, LANES), jnp.float32),
            pltpu.VMEM((wide, LANES), jnp.float32),
        ],
        cost_estimate=pl.CostEstimate(
            flops=10 * columns * wide * BS, bytes_accessed=16 * columns * wide, transcendentals=0
        ),
        compiler_params=pltpu.CompilerParams(vmem_limit_bytes=40 * 1024 * 1024),
    )(kinds, scales, places, weights, vectors, before, after, other, tables)


def shards(modes, previous, kinds, scales, tables, wet_rows, wet_counts, coupling):
    high = lax.Precision.HIGH
    domain = lax.axis_index("dom")
    vec_modes = modes[0]
    vec_prev = previous[0]
    columns, wide = vec_modes.shape
    nbr = wide // BS
    field_tables = tables[0]
    types = field_tables.shape[1]
    kinds_pad = jnp.pad(kinds[0], ((0, 0), (2, 0)))
    scales_pad = jnp.pad(scales[0], ((0, 0), (2, 0)))
    local_kinds = lax.dynamic_slice_in_dim(kinds_pad, domain * nbr, nbr + 2, 1)
    local_scales = lax.dynamic_slice_in_dim(scales_pad, domain * nbr, nbr + 2, 1)
    rows = wet_rows[0]
    slots = coupling.shape[0]
    used = jnp.arange(slots, dtype=jnp.int32) < wet_counts[0]
    weights = jnp.where(used, coupling, jnp.float32(0.0))
    places = (swapped(rows, "field", 0) << SHIFT) | rows
    operands = (local_kinds, local_scales, field_tables, places, weights)
    first_pair = jnp.concatenate([vec_modes, vec_prev], axis=0)
    image_pair = operate(first_pair, *operands)
    image_x, image_p = image_pair[:columns], image_pair[columns:]
    partial_sums = jnp.stack(
        [jnp.sum(vec_modes * vec_modes, axis=1), jnp.sum(vec_modes * image_x, axis=1)]
    )
    sums = summed_everywhere(jnp.pad(partial_sums, ((0, 6), (0, LANES - columns)))[None], 1)[0]
    quotient = sums[1, :columns] / sums[0, :columns]
    eye = jnp.eye(BS, dtype=jnp.bool_)
    diag_table = jnp.sum(
        jnp.where(eye[None], field_tables[0].astype(jnp.float32), jnp.float32(0.0)), axis=1
    )
    row_diag = jnp.zeros((nbr, BS), jnp.float32)
    for type_id in range(types):
        row_diag = jnp.where(
            (local_kinds[0, 2:] == type_id)[:, None], diag_table[type_id][None, :], row_diag
        )
    jacobi = (local_scales[0, 2:][:, None] * row_diag).reshape(wide)
    residual_dir = (image_x - vec_modes * quotient[:, None]) / jacobi[None, :]
    image_r = operate(residual_dir, *operands)
    search = jnp.concatenate([vec_modes, residual_dir, vec_prev], axis=0)
    image_all = jnp.concatenate([image_x, image_r, image_p], axis=0)
    ndof = 2.0 * lax.axis_size("dom") * wide
    part_b = jnp.dot(search, search.T, precision=high)
    part_a = jnp.dot(search, image_all.T, precision=high)
    part_a = part_a + part_a.T
    size = 3 * columns
    row = lax.broadcasted_iota(jnp.int32, (size, size + 8), 0)
    col = lax.broadcasted_iota(jnp.int32, (size, size + 8), 1)
    packed = jnp.where(
        col <= row,
        jnp.pad(part_b, ((0, 0), (0, 8))),
        jnp.pad(part_a, ((0, 0), (1, 7))),
    )
    half = -(-size // 16) * 8
    packed = jnp.pad(packed, ((0, 2 * half - size), (0, 0))).reshape(2, half, size + 8)
    packed = summed_everywhere(packed, 2).reshape(2 * half, size + 8)[:size]
    low = jnp.where(col <= row, packed, 0.0)[:, :size]
    high_part = packed[:, 1 : size + 1]
    square_row, square_col = row[:, :size], col[:, :size]
    gram_b = jnp.where(square_col <= square_row, low, low.T) / ndof
    gram_a = jnp.where(square_col >= square_row, high_part, high_part.T) / (2.0 * ndof)
    chol = jnp.linalg.cholesky(gram_b, symmetrize_input=False)
    leading = jax.scipy.linalg.solve_triangular(chol, gram_a, lower=True)
    projected = jax.scipy.linalg.solve_triangular(chol, leading.T, lower=True)
    basis = jax.scipy.linalg.solve_triangular(chol, search, lower=True)
    return (basis[None], projected)


def solution(mesh):
    return jax.shard_map(
        shards,
        mesh=mesh,
        in_specs=(
            P("field", None, "dom"),
            P("field", None, "dom"),
            P("field", None, None),
            P("field", None, None),
            P("field", None, None, None, None),
            P("field", "dom"),
            P("dom"),
            P("dom"),
        ),
        out_specs=(P("field", None, "dom"), P()),
        check_vma=False,
    )
```

profile of v0, /device:TPU:0, one launch (start us, length us, event | category | flops | bytes accessed | tf_op | source)
XLA Modules:
  0.0 138.1 jit_solution(14779984837490329827)
XLA Ops:
  0.6 0.0 copy-start.9
  0.6 0.0 copy-start.10
  0.7 0.0 copy-start.11
  0.7 0.0 slice-start
  0.7 3.1 %fusion.27 = bf16[80,8192]{1,0:T(8,128)(2,1)} fusion(f32[40,8192]{1,0:T(8,128)} %bitcast.85, f32[40,8192]{1,0:T(8,128)} %bitcast.80), kind=kLoop, calls=%fused_computation.65 | loop fusion | flops 2621440 | bytes 3932160 | tf_op jit(solution)/shard_map/convert_element_type | solution.py:172
  3.7 0.5 collective-permute-start.3
  4.2 1.7 %fusion.29 = (bf16[80,1024]{1,0:T(8,128)(2,1)}, bf16[80,1024]{1,0:T(8,128)(2,1)}) fusion(bf16[80,8192]{1,0:T(8,128)(2,1)} %fusion.27), kind=kLoop, calls=%fused_computation.67 | loop fusion | bytes 655360 | tf_op jit(solution)/shard_map/slice | solution.py:22
  6.0 5.0 %collective-permute-start.1 = (bf16[80,1024]{1,0:T(8,128)(2,1)}, bf16[80,1024]{1,0:T(8,128)(2,1)}, u32[]{:S(2)}, u32[]{:S(2)}) collective-permute-start(bf16[80,1024]{1,0:T(8,128)(2,1)} %get-tuple-element.10), channel_id=1, source_target_pairs={{0,1},{1,2},{2,3},{3,4},{4,5},{5,6},{6,7},{7,8},{8,9},{9,10},{10,1... | collective-permute-start | bytes 491528 | tf_op jit(solution)/shard_map/ppermute | solution.py:25
  11.0 1.3 collective-permute-start.2
  12.3 0.0 copy-done.9
  12.3 0.3 collective-permute-start
  12.6 0.8 iota_compare_fusion
  13.4 0.0 copy-start.1
  13.4 0.1 pad_dynamic-slice_fusion.scales
  13.5 0.1 pad_dynamic-slice_fusion.1.kinds
  14.3 0.1 compare_bitcast_fusion.3
  14.4 0.1 slice_bitcast_fusion
  14.4 2.2 %fusion = f32[4,512]{1,0:T(4,128)S(1)} fusion(bf16[1,3,4,512,512]{4,3,2,1,0:T(8,128)(2,1)} %param.14, pred[512,512]{1,0:T(8,128)(4,1)} %iota_compare_fusion), kind=kLoop, calls=%fused_computation.2 | loop fusion | flops 3143680 | bytes 2367488 | tf_op jit(solution)/shard_map/reduce_sum | solution.py:222
  16.7 0.1 multiply_bitcast_fusion
  16.8 0.0 copy-done.1
  16.8 0.0 copy-start.8
  16.8 1.5 %pad_maximum_fusion.1.x_ref = f32[80,8192]{1,0:T(8,128)S(1)} fusion(f32[40,8192]{1,0:T(8,128)} %bitcast.86, f32[40,8192]{1,0:T(8,128)S(1)} %bitcast.82), kind=kLoop, calls=%fused_computation.10 | loop fusion | flops 655360 | bytes 5242880 | tf_op jit(solution)/shard_map/concatenate | solution.py:213
  18.4 0.0 collective-permute-done
  18.4 0.0 collective-permute-done.1.before
  18.4 1.8 %collective-permute-done.2.after = bf16[80,1024]{1,0:T(8,128)(2,1)} collective-permute-done((bf16[80,1024]{1,0:T(8,128)(2,1)}, bf16[80,1024]{1,0:T(8,128)(2,1)}, u32[]{:S(2)}, u32[]{:S(2)}) %collective-permute-start.2) | collective-permute-done | bytes 163872 | tf_op jit(solution)/shard_map/ppermute | solution.py:26
  20.2 0.0 collective-permute-done.3.other
  20.3 19.9 %shard_map.95 = f32[80,8192]{1,0:T(8,128)S(1)} custom-call(s32[3,18]{1,0:T(4,128)S(1)} %pad_dynamic-slice_fusion.1.kinds, f32[3,18]{1,0:T(4,128)S(1)} %pad_dynamic-slice_fusion.scales, s32[3072]{0:T(1024)S(1)} %shift-left_or_fusion.places, f32[3072]{0:T(1024)S(1)} %fusion.18.weights, f32[80,8192]{1,0:T(8,128)S(1)} %pad_maximum_fusion.1.x_ref, ...), custom_call_target="tpu_custom_call" | custom-call | flops 3355443200 | bytes 10485760 | tf_op jit(solution)/shard_map/pallas_call | solution.py:177
  40.2 0.0 copy-start
  40.2 0.0 slice-start.2
  40.2 1.8 %multiply_reduce_fusion.1 = (f32[40]{0:T(128)S(1)}, f32[40]{0:T(128)S(1)}, f32[40,8192]{1,0:T(8,128)}, f32[40,8192]{1,0:T(8,128)}) fusion(f32[1,40,8192]{2,1,0:T(8,128)S(1)} %copy-done.1, f32[80,8192]{1,0:T(8,128)S(1)} %shard_map.95), kind=kLoop, calls=%fused_computation.14 | loop fusion | flops 1310640 | bytes 6553920 | tf_op jit(solution)/shard_map/reduce_sum | solution.py:217
  42.0 0.7 copy-done
  42.7 0.6 fusion.19.x_ref
  43.3 12.5 %shard_map.96 = f32[1,8,128]{2,1,0:T(8,128)} custom-call(f32[1,8,128]{2,1,0:T(8,128)} %fusion.19.x_ref), custom_call_target="tpu_custom_call" | custom-call | tf_op jit(solution)/shard_map/pallas_call | solution.py:96
  55.8 0.8 fusion.20
  56.6 2.1 %fusion.28 = (bf16[40,8192]{1,0:T(8,128)(2,1)S(1)}, f32[40,8192]{1,0:T(8,128)S(1)}) fusion(f32[8192]{0:T(1024)S(1)} %bitcast.93, f32[40]{0:T(128)S(1)} %fusion.20, f32[1,40,8192]{2,1,0:T(8,128)} %param.10, f32[80,8192]{1,0:T(8,128)} %copy-done), kind=kLoop, calls=%fused_computation.66 | loop fusion | flops 1310720 | bytes 4620448 | tf_op jit(solution)/shard_map/convert_element_type | solution.py:172
  58.7 0.1 collective-permute-start.6
  58.8 3.0 %collective-permute-start.4 = (bf16[40,1024]{1,0:T(8,128)(2,1)S(1)}, bf16[40,1024]{1,0:T(8,128)(2,1)S(1)}, u32[]{:S(2)}, u32[]{:S(2)}) collective-permute-start(bf16[40,1024]{1,0:T(8,128)(2,1)S(1)} %get-tuple-element.12), channel_id=1, source_target_pairs={{0,1},{1,2},{2,3},{3,4},{4,5},{5,6},{6,7},{7,8},{8,9},{9,10},{10,1... | collective-permute-start | bytes 245768 | tf_op jit(solution)/shard_map/ppermute | solution.py:25
  61.8 1.3 collective-permute-start.5
  63.1 4.2 %fusion.7 = f32[120,120]{0,1:T(8,128)S(1)} fusion(f32[40,8192]{1,0:T(8,128)} %bitcast.87, f32[40,8192]{1,0:T(8,128)S(1)} %get-tuple-element.6.x_ref, f32[40,8192]{1,0:T(8,128)} %bitcast.81), kind=kOutput, calls=%fused_computation.11 | convolution fusion | flops 709754880 | bytes 3989760 | tf_op jit(solution)/shard_map/dot_general | solution.py:236
  67.3 0.0 copy-start.2
  67.3 0.0 copy-start.4
  67.4 0.0 collective-permute-done.4.before
  67.4 0.9 collective-permute-done.5.after
  68.3 0.0 collective-permute-done.6.other
  68.3 19.7 %shard_map.97 = f32[40,8192]{1,0:T(8,128)S(1)} custom-call(s32[3,18]{1,0:T(4,128)S(1)} %pad_dynamic-slice_fusion.1.kinds, f32[3,18]{1,0:T(4,128)S(1)} %pad_dynamic-slice_fusion.scales, s32[3072]{0:T(1024)S(1)} %shift-left_or_fusion.places, f32[3072]{0:T(1024)S(1)} %fusion.18.weights, f32[40,8192]{1,0:T(8,128)S(1)} %get-tuple-element.6.x_ref, ...), custom_call_target="tpu_custom_call" | custom-call | flops 1677721600 | bytes 5242880 | tf_op jit(solution)/shard_map/pallas_call | solution.py:177
  88.1 1.8 %fusion.1 = f32[120,120]{1,0:T(8,128)S(1)} fusion(f32[40,8192]{1,0:T(8,128)S(1)} %copy-done.6, f32[40,8192]{1,0:T(8,128)S(1)} %shard_map.97, f32[40,8192]{1,0:T(8,128)S(1)} %copy-done.5, f32[40,8192]{1,0:T(8,128)S(1)} %bitcast.89, f32[40,8192]{1,0:T(8,128)S(1)} %get-tuple-element.6.x_ref, f32[40,8192]{1,0:T(8,128)S(1)} %bitcast.83), kind=kOutput, calls=%fused_computation.4 | convolution fusion | flops 711720960 | bytes 7921920 | tf_op jit(solution)/shard_map/dot_general | solution.py:237
  89.9 0.0 copy-start.3
  89.9 0.1 copy.18
  90.0 0.1 copy.29
  90.1 0.6 pad.29.clone
  90.7 16.5 %shard_map.98 = f32[2,64,128]{2,1,0:T(8,128)} custom-call(f32[2,64,128]{2,1,0:T(8,128)} %bitcast.92), custom_call_target="tpu_custom_call" | custom-call | tf_op jit(solution)/shard_map/pallas_call | solution.py:96
  107.2 1.0 fusion.31
  108.2 0.1 copy.30
  108.3 0.1 copy.21
  108.4 11.0 %cholesky.16 = f32[120,120]{1,0:T(8,128)S(1)} custom-call(f32[120,120]{1,0:T(8,128)S(1)} %fusion.15), custom_call_target="Cholesky" | custom-call | tf_op jit(solution)/shard_map/jit(cholesky)/cholesky | solution.py:255
  119.5 0.6 compare_reduce_fusion
  120.1 0.7 fusion.8
  120.8 9.2 %custom-call.10 = f32[1,120,120]{1,2,0:T(8,128)S(1)} custom-call(f32[1,120,120]{2,1,0:T(8,128)S(1)} %fusion.8), custom_call_target="InvertDiagBlocksLowerTriangular" | custom-call | tf_op jit(solution)/shard_map/jit(_solve_triangular)/triangular_solve | solution.py:258
  130.0 0.1 copy.28
  130.1 0.0 copy-done.3
  130.1 0.0 copy-start.7
  130.1 6.7 %convolution_bitcast_fusion = f32[1,120,8192]{2,1,0:T(8,128)} fusion(f32[40,8192]{1,0:T(8,128)} %bitcast.88, f32[40,8192]{1,0:T(8,128)S(1)} %get-tuple-element.6.x_ref, f32[40,8192]{1,0:T(8,128)S(1)} %bitcast.84, f32[1,120,120]{1,2,0:T(8,128)S(1)} %custom-call.10), kind=kOutput, calls=%fused_computation | convolution fusion | flops 1417543680 | bytes 7921920 | tf_op jit(solution)/shard_map/jit(_solve_triangular)/triangular_solve | solution.py:258
  136.8 0.3 convolution_bitcast_fusion.1
  137.2 0.9 fusion.12
  (31 shorter events, 0.2 us)
Async XLA Ops:
  0.6 11.7 %copy-start.9 = (s32[1,3072]{1,0:T(1,128)S(1)}, s32[1,3072]{1,0:T(1,128)}, u32[]{:S(2)}) copy-start(s32[1,3072]{1,0:T(1,128)} %param.15) | copy-start | bytes 36868
  0.6 12.7 %copy-start.10 = (f32[1,3,256]{2,0,1:T(1,128)S(1)}, f32[1,3,256]{2,0,1:T(1,128)}, u32[]{:S(2)}) copy-start(f32[1,3,256]{2,0,1:T(1,128)} %param.13) | copy-start | bytes 9220
  0.7 12.7 %copy-start.11 = (s32[1,3,256]{2,0,1:T(1,128)S(1)}, s32[1,3,256]{2,0,1:T(1,128)}, u32[]{:S(2)}) copy-start(s32[1,3,256]{2,0,1:T(1,128)} %param.12) | copy-start | bytes 9220
  0.7 19.6 %slice-start = ((s8[6291456]{0:T(1024)(128)(4,1)}), s8[2097152]{0:T(1024)(128)(4,1)S(1)}, s32[]{:S(2)}) async-start(s8[6291456]{0:T(1024)(128)(4,1)} %bitcast.74), calls=%async_computation | async-start | bytes 4194304
  3.7 16.5 %collective-permute-start.3 = (bf16[80,8192]{1,0:T(8,128)(2,1)}, bf16[80,8192]{1,0:T(8,128)(2,1)S(1)}, u32[]{:S(2)}, u32[]{:S(2)}) collective-permute-start(bf16[80,8192]{1,0:T(8,128)(2,1)} %fusion.27), channel_id=1, source_target_pairs={{0,16},{16,0},{1,17},{17,1},{2,18},{18,2},{3,19},{19,3},{4,20},{20... | collective-permute-start | bytes 3932168 | tf_op jit(solution)/shard_map/ppermute | solution.py:16
  6.0 12.4 %collective-permute-start.1 = (bf16[80,1024]{1,0:T(8,128)(2,1)}, bf16[80,1024]{1,0:T(8,128)(2,1)}, u32[]{:S(2)}, u32[]{:S(2)}) collective-permute-start(bf16[80,1024]{1,0:T(8,128)(2,1)} %get-tuple-element.10), channel_id=1, source_target_pairs={{0,1},{1,2},{2,3},{3,4},{4,5},{5,6},{6,7},{7,8},{8,9},{9,10},{10,1... | collective-permute-start | bytes 491528 | tf_op jit(solution)/shard_map/ppermute | solution.py:25
  11.0 9.2 %collective-permute-start.2 = (bf16[80,1024]{1,0:T(8,128)(2,1)}, bf16[80,1024]{1,0:T(8,128)(2,1)}, u32[]{:S(2)}, u32[]{:S(2)}) collective-permute-start(bf16[80,1024]{1,0:T(8,128)(2,1)} %get-tuple-element.9), channel_id=1, source_target_pairs={{1,0},{2,1},{3,2},{4,3},{5,4},{6,5},{7,6},{8,7},{9,8},{10,9},{11,1... | collective-permute-start | bytes 491528 | tf_op jit(solution)/shard_map/ppermute | solution.py:26
  12.3 6.1 %collective-permute-start = (s32[3072]{0:T(1024)S(1)}, s32[3072]{0:T(1024)S(1)}, u32[]{:S(2)}, u32[]{:S(2)}) collective-permute-start(s32[3072]{0:T(1024)S(1)} %bitcast.96), channel_id=1, source_target_pairs={{0,16},{16,0},{1,17},{17,1},{2,18},{18,2},{3,19},{19,3},{4,20},{20... | collective-permute-start | bytes 36872 | tf_op jit(solution)/shard_map/ppermute | solution.py:16
  13.4 3.4 %copy-start.1 = (f32[1,40,8192]{2,1,0:T(8,128)S(1)}, f32[1,40,8192]{2,1,0:T(8,128)}, u32[]{:S(2)}) copy-start(f32[1,40,8192]{2,1,0:T(8,128)} %param.10) | copy-start | bytes 3932164
  14.4 5.8 %slice-start.1 = ((s8[6291456]{0:T(1024)(128)(4,1)}), s8[4194304]{0:T(1024)(128)(4,1)S(1)}, s32[]{:S(2)}) async-start(s8[6291456]{0:T(1024)(128)(4,1)} %bitcast.74), calls=%async_computation.1 | async-start | bytes 8388608
  16.8 1.5 %copy-start.8 = (f32[3072]{0:T(1024)S(1)}, f32[3072]{0:T(1024)}, u32[]{:S(2)}) copy-start(f32[3072]{0:T(1024)} %param.17) | copy-start | bytes 36868
  40.2 2.5 %copy-start = (f32[80,8192]{1,0:T(8,128)}, f32[80,8192]{1,0:T(8,128)S(1)}, u32[]{:S(2)}) copy-start(f32[80,8192]{1,0:T(8,128)S(1)} %shard_map.95) | copy-start | bytes 7864324
  40.2 28.1 %slice-start.2 = ((s8[6291456]{0:T(1024)(128)(4,1)}), s8[2097152]{0:T(1024)(128)(4,1)S(1)}, s32[]{:S(2)}) async-start(s8[6291456]{0:T(1024)(128)(4,1)} %bitcast.77), calls=%async_computation.2 | async-start | bytes 4194304
  56.6 11.7 %slice-start.3 = ((s8[6291456]{0:T(1024)(128)(4,1)}), s8[4194304]{0:T(1024)(128)(4,1)S(1)}, s32[]{:S(2)}) async-start(s8[6291456]{0:T(1024)(128)(4,1)} %bitcast.77), calls=%async_computation.3 | async-start | bytes 8388608
  58.7 9.6 %collective-permute-start.6 = (bf16[40,8192]{1,0:T(8,128)(2,1)S(1)}, bf16[40,8192]{1,0:T(8,128)(2,1)S(1)}, u32[]{:S(2)}, u32[]{:S(2)}) collective-permute-start(bf16[40,8192]{1,0:T(8,128)(2,1)S(1)} %get-tuple-element.5), channel_id=1, source_target_pairs={{0,16},{16,0},{1,17},{17,1},{2,18},{18,2},{3,19},{19,3},{4,20},{20... | collective-permute-start | bytes 1966088 | tf_op jit(solution)/shard_map/ppermute | solution.py:16
  58.8 8.5 %collective-permute-start.4 = (bf16[40,1024]{1,0:T(8,128)(2,1)S(1)}, bf16[40,1024]{1,0:T(8,128)(2,1)S(1)}, u32[]{:S(2)}, u32[]{:S(2)}) collective-permute-start(bf16[40,1024]{1,0:T(8,128)(2,1)S(1)} %get-tuple-element.12), channel_id=1, source_target_pairs={{0,1},{1,2},{2,3},{3,4},{4,5},{5,6},{6,7},{7,8},{8,9},{9,10},{10,1... | collective-permute-start | bytes 245768 | tf_op jit(solution)/shard_map/ppermute | solution.py:25
  61.8 6.5 %collective-permute-start.5 = (bf16[40,1024]{1,0:T(8,128)(2,1)S(1)}, bf16[40,1024]{1,0:T(8,128)(2,1)S(1)}, u32[]{:S(2)}, u32[]{:S(2)}) collective-permute-start(bf16[40,1024]{1,0:T(8,128)(2,1)S(1)} %get-tuple-element.11), channel_id=1, source_target_pairs={{1,0},{2,1},{3,2},{4,3},{5,4},{6,5},{7,6},{8,7},{9,8},{10,9},{11,1... | collective-permute-start | bytes 245768 | tf_op jit(solution)/shard_map/ppermute | solution.py:26
  67.3 20.7 %copy-start.2 = (f32[1,40,8192]{2,1,0:T(8,128)S(1)}, f32[1,40,8192]{2,1,0:T(8,128)}, u32[]{:S(2)}) copy-start(f32[1,40,8192]{2,1,0:T(8,128)} %param.10) | copy-start | bytes 3932164
  67.3 20.7 %copy-start.4 = (f32[1,40,8192]{2,1,0:T(8,128)S(1)}, f32[1,40,8192]{2,1,0:T(8,128)}, u32[]{:S(2)}) copy-start(f32[1,40,8192]{2,1,0:T(8,128)} %param.11) | copy-start | bytes 3932164
  67.3 20.7 %copy-start.5 = (f32[40,8192]{1,0:T(8,128)S(1)}, f32[40,8192]{1,0:T(8,128)}, u32[]{:S(2)}) copy-start(f32[40,8192]{1,0:T(8,128)} %get-tuple-element.7) | copy-start | bytes 3932164
  67.3 20.7 %copy-start.6 = (f32[40,8192]{1,0:T(8,128)S(1)}, f32[40,8192]{1,0:T(8,128)}, u32[]{:S(2)}) copy-start(f32[40,8192]{1,0:T(8,128)} %get-tuple-element.8) | copy-start | bytes 3932164
  89.9 40.2 %copy-start.3 = (f32[1,40,8192]{2,1,0:T(8,128)S(1)}, f32[1,40,8192]{2,1,0:T(8,128)}, u32[]{:S(2)}) copy-start(f32[1,40,8192]{2,1,0:T(8,128)} %param.10) | copy-start | bytes 3932164
  130.1 6.8 %copy-start.7 = (f32[2,64,128]{2,1,0:T(8,128)S(1)}, f32[2,64,128]{2,1,0:T(8,128)}, u32[]{:S(2)}) copy-start(f32[2,64,128]{2,1,0:T(8,128)} %shard_map.98) | copy-start | bytes 196612
where the time goes:
time: 139 us; the launch traced here: 138 us
  Pallas kernels  68.6 us (49%)
  other arithmetic  34.6 us (25%)
  matrix products  14 us (10%)
  starting transfers between devices  11.4 us (8%)
  local copies, waits for them, and re-layouts  4.82 us (3%)
  waiting for transfers between devices  2.74 us (2%)
  between operations  1.85 us (1%)
    pallas_call x2, Pallas kernels, operate(): pl.pallas_call(operator_kernel, out_shape=jax.ShapeDtypeStruct((columns,...  39.7 us
    pallas_call x2, Pallas kernels, summed_everywhere(): pl.pallas_call(functools.partial(sum_kernel, rounds, x.shape[0] == 2), ou...  29 us
    another operation x3, other arithmetic, shards(): chol = jnp.linalg.cholesky(gram_b, symmetrize_input=False)  11.6 us
    another operation x2, other arithmetic, shards(): basis = jax.scipy.linalg.solve_triangular(chol, search, lower=True)  9.85 us
    ppermute x2, starting transfers between devices, halos(): lax.ppermute(tail, axis, [(i, i + 1) for i in range(ends)])  8.01 us
    another operation x1, matrix products, shards(): basis = jax.scipy.linalg.solve_triangular(chol, search, lower=True)  6.74 us
    convert_element_type x2, other arithmetic, operate(): rounded = vectors.astype(jnp.bfloat16)  5.18 us
    dot_general x1, matrix products, shards(): part_b = jnp.dot(search, search.T, precision=high)  4.2 us
  transfers between devices with their start and end apart: 7, of which 2 were waited for; matrix products, arithmetic and copies ran while one was open for 8% of the time, Pallas kernels for 0%

commit v1 on v0

--- a/solution.py
+++ b/solution.py
@@ -191,6 +191,130 @@
     )(kinds, scales, places, weights, vectors, before, after, other, tables)
 
 
+SUB = 8
+
+
+def split_dot(left, right, dims):
+    lh = left.astype(jnp.bfloat16)
+    ll = (left - lh.astype(jnp.float32)).astype(jnp.bfloat16)
+    rh = right.astype(jnp.bfloat16)
+    rl = (right - rh.astype(jnp.float32)).astype(jnp.bfloat16)
+
+    def dot(a, b):
+        return lax.dot_general(a, b, dims, preferred_element_type=jnp.float32)
+
+    return dot(lh, rh) + (dot(lh, rl) + dot(ll, rh))
+
+
+def eliminate(gram, size, inverse_ref):
+    panels = size // SUB
+    sub = lax.broadcasted_iota(jnp.int32, (SUB, LANES), 0)
+    lane = lax.broadcasted_iota(jnp.int32, (SUB, LANES), 1)
+    left = [gram[SUB * i : SUB * (i + 1)] for i in range(panels)]
+    right = [(lane == sub + SUB * i).astype(jnp.float32) for i in range(panels)]
+
+    def over_lanes(cell, column):
+        return jnp.broadcast_to(cell[:, column : column + 1], (SUB, LANES))
+
+    def over_rows(cell, row):
+        return jnp.broadcast_to(cell[row : row + 1], (SUB, LANES))
+
+    for k in range(panels):
+        columns = [over_lanes(left[k], SUB * k + c) for c in range(SUB)]
+        cells = [left[k], right[k]]
+        for c in range(SUB):
+            pivot = over_rows(columns[c], c)
+            inverse = 1.0 / pivot
+            inverse_ref[SUB * k + c : SUB * k + c + 1] = (cells[1] * lax.rsqrt(pivot))[c : c + 1]
+            here = sub == c
+            factor = columns[c]
+
+            def reduced(cell):
+                row = over_rows(cell, c) * inverse
+                return jnp.where(here, row, cell - factor * row)
+
+            for later in range(c + 1, SUB):
+                columns[later] = reduced(columns[later])
+            cells = [reduced(cell) for cell in cells]
+        rows = [[over_rows(cell, c) for c in range(SUB)] for cell in cells]
+        for i in range(k + 1, panels):
+            source = left[i]
+            for c in range(SUB):
+                factor = over_lanes(source, SUB * k + c)
+                left[i] = left[i] - factor * rows[0][c]
+                right[i] = right[i] - factor * rows[1][c]
+
+
+def finish_kernel(chunk, scale, packed_ref, x_ref, r_ref, p_ref, basis_ref, projected_ref, inverse_ref, held, sems):
+    columns, wide = x_ref.shape
+    size = 3 * columns
+    packed = packed_ref[...] * scale
+    row = lax.broadcasted_iota(jnp.int32, packed.shape, 0)
+    col = lax.broadcasted_iota(jnp.int32, packed.shape, 1)
+    gram_b = jnp.where(col <= row, packed, packed.T)
+    inverse_ref[...] = jnp.zeros_like(inverse_ref)
+    eliminate(gram_b, size, inverse_ref)
+    high = jnp.concatenate([packed[:, 1:], packed[:, :1]], axis=1)
+    gram_a = jnp.where(col >= row, high, high.T)
+    gram_a = jnp.where(jnp.maximum(row, col) < size, 0.5 * gram_a, 0.0)
+    inverse = inverse_ref[...]
+    projected = split_dot(split_dot(inverse, gram_a, NN), inverse, NT)
+    projected_ref[...] = projected[:size, :size]
+    ih = inverse.astype(jnp.bfloat16)
+    il = (inverse - ih.astype(jnp.float32)).astype(jnp.bfloat16)
+    twice = jnp.concatenate([ih, ih], axis=1)
+    blank = jnp.zeros((LANES - size, chunk), jnp.float32)
+
+    def copy(n):
+        span = pl.ds(pl.multiple_of(n * chunk, chunk), chunk)
+        return pltpu.make_async_copy(held.at[n], basis_ref.at[0, :, span], sems.at[n])
+
+    def step(n, carry):
+        span = pl.ds(pl.multiple_of(n * chunk, chunk), chunk)
+        search = jnp.concatenate([x_ref[:, span], r_ref[:, span], p_ref[:, span], blank], axis=0)
+        sh = search.astype(jnp.bfloat16)
+        sl = (search - sh.astype(jnp.float32)).astype(jnp.bfloat16)
+        both = jnp.concatenate([sh, sl], axis=0)
+        out = lax.dot_general(twice, both, NN, preferred_element_type=jnp.float32)
+        out = out + lax.dot_general(il, sh, NN, preferred_element_type=jnp.float32)
+        held[n] = out[:size]
+        copy(n).start()
+        return carry
+
+    lax.fori_loop(0, wide // chunk, step, 0)
+
+    def close(n, carry):
+        copy(n).wait()
+        return carry
+
+    lax.fori_loop(0, wide // chunk, close, 0)
+
+
+def finish(packed, vec_modes, residual_dir, vec_prev, ndof):
+    columns, wide = vec_modes.shape
+    size = 3 * columns
+    chunk = min(512, wide)
+    vmem = pl.BlockSpec(memory_space=pltpu.VMEM)
+    return pl.pallas_call(
+        functools.partial(finish_kernel, chunk, 1.0 / ndof),
+        out_shape=(
+            jax.ShapeDtypeStruct((1, size, wide), jnp.float32),
+            jax.ShapeDtypeStruct((size, size), jnp.float32),
+        ),
+        in_specs=[vmem, vmem, vmem, vmem],
+        out_specs=(pl.BlockSpec(memory_space=pl.ANY), vmem),
+        scratch_shapes=[
+            pltpu.VMEM((LANES, LANES), jnp.float32),
+            pltpu.VMEM((wide // chunk, size, chunk), jnp.float32),
+            pltpu.SemaphoreType.DMA((wide // chunk,)),
+        ],
+        cost_estimate=pl.CostEstimate(
+            flops=6 * size * size * wide, bytes_accessed=8 * size * wide, transcendentals=0
+        ),
+        compiler_params=pltpu.CompilerParams(vmem_limit_bytes=24 * 1024 * 1024),
+    )(packed, vec_modes, residual_dir, vec_prev)
+
+
 def shards(modes, previous, kinds, scales, tables, wet_rows, wet_counts, coupling):
     high = lax.Precision.HIGH
     domain = lax.axis_index("dom")
@@ -246,17 +370,8 @@
     )
     half = -(-size // 16) * 8
     packed = jnp.pad(packed, ((0, 2 * half - size), (0, 0))).reshape(2, half, size + 8)
-    packed = summed_everywhere(packed, 2).reshape(2 * half, size + 8)[:size]
-    low = jnp.where(col <= row, packed, 0.0)[:, :size]
-    high_part = packed[:, 1 : size + 1]
-    square_row, square_col = row[:, :size], col[:, :size]
-    gram_b = jnp.where(square_col <= square_row, low, low.T) / ndof
-    gram_a = jnp.where(square_col >= square_row, high_part, high_part.T) / (2.0 * ndof)
-    chol = jnp.linalg.cholesky(gram_b, symmetrize_input=False)
-    leading = jax.scipy.linalg.solve_triangular(chol, gram_a, lower=True)
-    projected = jax.scipy.linalg.solve_triangular(chol, leading.T, lower=True)
-    basis = jax.scipy.linalg.solve_triangular(chol, search, lower=True)
-    return (basis[None], projected)
+    packed = summed_everywhere(packed, 2).reshape(2 * half, size + 8)
+    return finish(packed, vec_modes, residual_dir, vec_prev, ndof)
 
 
 def solution(mesh):

time: 139 us -> 121 us (0.87)
  other arithmetic: 34.6 us -> 12.7 us
  Pallas kernels: 68.6 us -> 80.7 us
  matrix products: 14 us -> 3.55 us
  starting transfers between devices: 11.4 us -> 14.2 us
  waiting for transfers between devices: 2.74 us -> 0.95 us
  local copies, waits for them, and re-layouts: 4.82 us -> 6.44 us
    another operation x5 -> x0, other arithmetic: 21.5 us -> none  [the longest x3 11.6 us: shards(): chol = jnp.linalg.cholesky(gram_b, symmetrize_input=False)]
    pallas_call x0 -> x1, Pallas kernels: none -> 9.7 us  [finish(): pl.pallas_call(functools.partial(finish_kernel, chunk, 1.0 / ndof), out_s...]
    another operation x3 -> x0, matrix products: 8.02 us -> none  [the longest x1 6.74 us: shards(): basis = jax.scipy.linalg.solve_triangular(chol, search, lower=True)]
    ppermute x2, starting transfers between devices: 8.01 us -> 10.9 us  [halos(): lax.ppermute(tail, axis, [(i, i + 1) for i in range(ends)])]
    ppermute x2, waiting for transfers between devices: 2.72 us -> 0.01 us  [halos(): lax.ppermute(head, axis, [(i + 1, i) for i in range(ends)])]
    unnamed x38 -> x35, local copies, waits for them, and re-layouts: 1.03 us -> 3.71 us
    dot_general x1, matrix products: 4.2 us -> 1.76 us  [shards(): part_b = jnp.dot(search, search.T, precision=high)]
    pallas_call x2, Pallas kernels: 29 us -> 31 us  [summed_everywhere(): pl.pallas_call(functools.partial(sum_kernel, rounds, x.shape[0] == 2), ou...]
  transfers between devices with their start and end apart: 7 -> 7, of which waited for: 2 -> 2; matrix products, arithmetic and copies ran while one was open for 8% -> 10% of each run, Pallas kernels for 0% -> 0%
where the time goes in v1:
time: 121 us; the launch traced here: 120 us
  Pallas kernels  80.7 us (67%)
  starting transfers between devices  14.2 us (12%)
  other arithmetic  12.7 us (10%)
  local copies, waits for them, and re-layouts  6.44 us (5%)
  matrix products  3.55 us (3%)
  between operations  1.88 us (2%)
    pallas_call x2, Pallas kernels, operate(): pl.pallas_call(operator_kernel, out_shape=jax.ShapeDtypeStruct((columns,...  40 us
    pallas_call x2, Pallas kernels, summed_everywhere(): pl.pallas_call(functools.partial(sum_kernel, rounds, x.shape[0] == 2), ou...  31 us
    ppermute x2, starting transfers between devices, halos(): lax.ppermute(tail, axis, [(i, i + 1) for i in range(ends)])  10.9 us
    pallas_call x1, Pallas kernels, finish(): pl.pallas_call(functools.partial(finish_kernel, chunk, 1.0 / ndof), out_s...  9.7 us
    convert_element_type x2, other arithmetic, operate(): rounded = vectors.astype(jnp.bfloat16)  5.22 us
    unnamed x35, local copies, waits for them, and re-layouts  3.71 us
    ppermute x2, starting transfers between devices, halos(): lax.ppermute(head, axis, [(i + 1, i) for i in range(ends)])  2.7 us
  transfers between devices with their start and end apart: 7, of which 2 were waited for; matrix products, arithmetic and copies ran while one was open for 10% of the time, Pallas kernels for 0%

profile of v1, /device:TPU:0, one launch (start us, length us, event | category | flops | bytes accessed | tf_op | source)
XLA Modules:
  0.0 120.4 jit_solution(1559290787541285623)
XLA Ops:
  0.6 0.6 collective-permute-start
  1.2 0.0 copy-start.10
  1.2 0.0 copy-start.11
  1.2 0.0 slice-start
  1.2 3.1 %fusion.13 = bf16[80,8192]{1,0:T(8,128)(2,1)} fusion(f32[40,8192]{1,0:T(8,128)} %bitcast.58, f32[40,8192]{1,0:T(8,128)} %bitcast.53), kind=kLoop, calls=%fused_computation.39 | loop fusion | flops 2621440 | bytes 3932160 | tf_op jit(solution)/shard_map/convert_element_type | solution.py:172
  4.3 0.0 collective-permute-start.3
  4.3 1.8 %fusion.15 = (bf16[80,1024]{1,0:T(8,128)(2,1)}, bf16[80,1024]{1,0:T(8,128)(2,1)}) fusion(bf16[80,8192]{1,0:T(8,128)(2,1)} %fusion.13), kind=kLoop, calls=%fused_computation.41 | loop fusion | bytes 655360 | tf_op jit(solution)/shard_map/slice | solution.py:22
  6.0 1.3 %collective-permute-start.2 = (bf16[80,1024]{1,0:T(8,128)(2,1)}, bf16[80,1024]{1,0:T(8,128)(2,1)}, u32[]{:S(2)}, u32[]{:S(2)}) collective-permute-start(bf16[80,1024]{1,0:T(8,128)(2,1)} %get-tuple-element.8), channel_id=1, source_target_pairs={{1,0},{2,1},{3,2},{4,3},{5,4},{6,5},{7,6},{8,7},{9,8},{10,9},{11,1... | collective-permute-start | bytes 491528 | tf_op jit(solution)/shard_map/ppermute | solution.py:26
  7.3 6.1 %collective-permute-start.1 = (bf16[80,1024]{1,0:T(8,128)(2,1)}, bf16[80,1024]{1,0:T(8,128)(2,1)}, u32[]{:S(2)}, u32[]{:S(2)}) collective-permute-start(bf16[80,1024]{1,0:T(8,128)(2,1)} %get-tuple-element.9), channel_id=1, source_target_pairs={{0,1},{1,2},{2,3},{3,4},{4,5},{5,6},{6,7},{7,8},{8,9},{9,10},{10,1... | collective-permute-start | bytes 491528 | tf_op jit(solution)/shard_map/ppermute | solution.py:25
  13.5 0.8 iota_compare_fusion
  15.0 0.0 copy-done.10
  15.0 0.1 pad_dynamic-slice_fusion.1.kinds
  15.1 0.1 compare_bitcast_fusion.3
  15.2 0.0 copy-done.11
  15.2 0.1 pad_dynamic-slice_fusion.scales
  15.3 0.1 slice_bitcast_fusion
  15.3 2.2 %fusion = f32[4,512]{1,0:T(4,128)S(1)} fusion(bf16[1,3,4,512,512]{4,3,2,1,0:T(8,128)(2,1)} %param.12, pred[512,512]{1,0:T(8,128)(4,1)} %iota_compare_fusion), kind=kLoop, calls=%fused_computation.1 | loop fusion | flops 3143680 | bytes 2367488 | tf_op jit(solution)/shard_map/reduce_sum | solution.py:346
  17.6 0.1 multiply_bitcast_fusion
  17.7 0.0 copy-done
  17.7 0.0 copy-start.8
  17.7 0.0 copy-start.9
  17.7 1.5 %pad_maximum_fusion.3.x_ref = f32[80,8192]{1,0:T(8,128)S(1)} fusion(f32[40,8192]{1,0:T(8,128)} %bitcast.59, f32[40,8192]{1,0:T(8,128)S(1)} %bitcast.54), kind=kLoop, calls=%fused_computation.10 | loop fusion | flops 655360 | bytes 5242880 | tf_op jit(solution)/shard_map/concatenate | solution.py:337
  19.3 0.0 copy-done.8
  19.3 0.0 collective-permute-done
  19.3 0.0 copy-done.9
  19.3 0.0 collective-permute-done.2.after
  19.3 0.9 collective-permute-done.1.before
  20.2 0.0 collective-permute-done.3.other
  20.2 0.0 slice-done
  20.2 0.0 slice-done.1
  20.2 20.4 %shard_map.95 = f32[80,8192]{1,0:T(8,128)S(1)} custom-call(s32[3,18]{1,0:T(4,128)S(1)} %pad_dynamic-slice_fusion.1.kinds, f32[3,18]{1,0:T(4,128)S(1)} %pad_dynamic-slice_fusion.scales, s32[3072]{0:T(1024)S(1)} %shift-left_or_fusion.places, f32[3072]{0:T(1024)S(1)} %fusion.8.weights, f32[80,8192]{1,0:T(8,128)S(1)} %pad_maximum_fusion.3.x_ref, ...), custom_call_target="tpu_custom_call" | custom-call | flops 3355443200 | bytes 10485760 | tf_op jit(solution)/shard_map/pallas_call | solution.py:177
  40.7 0.0 copy-start.1
  40.7 1.5 %copy-done.1 = f32[80,8192]{1,0:T(8,128)} copy-done((f32[80,8192]{1,0:T(8,128)}, f32[80,8192]{1,0:T(8,128)S(1)}, u32[]{:S(2)}) %copy-start.1) | copy-done | bytes 2621464
  42.2 1.3 %multiply_reduce_fusion.1 = (f32[40]{0:T(128)S(1)}, f32[40]{0:T(128)S(1)}, f32[40,8192]{1,0:T(8,128)}) fusion(f32[1,40,8192]{2,1,0:T(8,128)S(1)} %copy-done, f32[80,8192]{1,0:T(8,128)S(1)} %shard_map.95), kind=kLoop, calls=%fused_computation.13 | loop fusion | flops 1310640 | bytes 3932480 | tf_op jit(solution)/shard_map/reduce_sum | solution.py:341
  43.5 0.6 fusion.9.x_ref
  44.1 13.5 %shard_map.96 = f32[1,8,128]{2,1,0:T(8,128)} custom-call(f32[1,8,128]{2,1,0:T(8,128)} %fusion.9.x_ref), custom_call_target="tpu_custom_call" | custom-call | tf_op jit(solution)/shard_map/pallas_call | solution.py:96
  57.6 0.8 fusion.10
  58.3 2.2 %fusion.14 = (bf16[40,8192]{1,0:T(8,128)(2,1)S(1)}, f32[40,8192]{1,0:T(8,128)S(1)}, f32[40,8192]{1,0:T(8,128)S(1)}) fusion(f32[8192]{0:T(1024)S(1)} %bitcast.65, f32[40]{0:T(128)S(1)} %fusion.10, f32[1,40,8192]{2,1,0:T(8,128)S(1)} %copy-done, f32[80,8192]{1,0:T(8,128)} %copy-done.1), kind=kLoop, calls=%fused_computation.40 | loop fusion | flops 1310720 | bytes 7241888 | tf_op jit(solution)/shard_map/convert_element_type | solution.py:172
  60.5 0.0 copy-start.2
  60.5 0.1 collective-permute-start.6
  60.6 1.4 %collective-permute-start.5 = (bf16[40,1024]{1,0:T(8,128)(2,1)S(1)}, bf16[40,1024]{1,0:T(8,128)(2,1)S(1)}, u32[]{:S(2)}, u32[]{:S(2)}) collective-permute-start(bf16[40,1024]{1,0:T(8,128)(2,1)S(1)} %get-tuple-element.10), channel_id=1, source_target_pairs={{1,0},{2,1},{3,2},{4,3},{5,4},{6,5},{7,6},{8,7},{9,8},{10,9},{11,1... | collective-permute-start | bytes 245768 | tf_op jit(solution)/shard_map/ppermute | solution.py:26
  62.0 4.7 %collective-permute-start.4 = (bf16[40,1024]{1,0:T(8,128)(2,1)S(1)}, bf16[40,1024]{1,0:T(8,128)(2,1)S(1)}, u32[]{:S(2)}, u32[]{:S(2)}) collective-permute-start(bf16[40,1024]{1,0:T(8,128)(2,1)S(1)} %get-tuple-element.11), channel_id=1, source_target_pairs={{0,1},{1,2},{2,3},{3,4},{4,5},{5,6},{6,7},{7,8},{8,9},{9,10},{10,1... | collective-permute-start | bytes 245768 | tf_op jit(solution)/shard_map/ppermute | solution.py:25
  66.8 0.0 copy-done.4
  66.8 1.8 %fusion.7 = f32[120,120]{1,0:T(8,128)S(1)} fusion(f32[40,8192]{1,0:T(8,128)S(1)} %bitcast.60, f32[40,8192]{1,0:T(8,128)S(1)} %get-tuple-element.5.x_ref.r_ref, f32[40,8192]{1,0:T(8,128)S(1)} %bitcast.55), kind=kOutput, calls=%fused_computation.9 | convolution fusion | flops 709754880 | bytes 3989760 | tf_op jit(solution)/shard_map/dot_general | solution.py:360
  68.6 0.0 copy-start.7
  68.6 0.0 collective-permute-done.5.after
  68.6 0.1 collective-permute-done.4.before
  68.6 0.0 collective-permute-done.6.other
  68.6 0.0 slice-done.2
  68.6 0.0 slice-done.3
  68.6 19.6 %shard_map.97 = f32[40,8192]{1,0:T(8,128)S(1)} custom-call(s32[3,18]{1,0:T(4,128)S(1)} %pad_dynamic-slice_fusion.1.kinds, f32[3,18]{1,0:T(4,128)S(1)} %pad_dynamic-slice_fusion.scales, s32[3072]{0:T(1024)S(1)} %shift-left_or_fusion.places, f32[3072]{0:T(1024)S(1)} %fusion.8.weights, f32[40,8192]{1,0:T(8,128)S(1)} %get-tuple-element.5.x_ref.r_ref, ...), custom_call_target="tpu_custom_call" | custom-call | flops 1677721600 | bytes 5242880 | tf_op jit(solution)/shard_map/pallas_call | solution.py:177
  88.2 0.0 copy-done.2
  88.2 0.0 copy-done.7
  88.2 0.0 copy-start.5
  88.2 1.8 %fusion.1 = f32[120,120]{1,0:T(8,128)S(1)} fusion(f32[40,8192]{1,0:T(8,128)S(1)} %get-tuple-element.7, f32[40,8192]{1,0:T(8,128)S(1)} %shard_map.97, f32[40,8192]{1,0:T(8,128)S(1)} %copy-done.7, f32[40,8192]{1,0:T(8,128)S(1)} %bitcast.61, f32[40,8192]{1,0:T(8,128)S(1)} %get-tuple-element.5.x_ref.r_ref, f32[40,8192]{1,0:T(8,128)S(1)} %bitcast.56), kind=kOutput, calls=%fused_computation.3 | convolution fusion | flops 711720960 | bytes 7921920 | tf_op jit(solution)/shard_map/dot_general | solution.py:361
  90.0 0.1 copy.10
  90.1 0.1 pad_select_fusion
  90.2 0.6 pad.29
  90.9 17.5 %shard_map.98 = f32[2,64,128]{2,1,0:T(8,128)} custom-call(f32[2,64,128]{2,1,0:T(8,128)} %bitcast.64), custom_call_target="tpu_custom_call" | custom-call | tf_op jit(solution)/shard_map/pallas_call | solution.py:96
  108.4 0.0 copy-done.5
  108.4 0.0 copy-start.3
  108.4 1.3 %copy-done.3 = f32[40,8192]{1,0:T(8,128)S(1)} copy-done((f32[40,8192]{1,0:T(8,128)S(1)}, f32[40,8192]{1,0:T(8,128)}, u32[]{:S(2)}) %copy-start.3) | copy-done | bytes 1310744
  109.7 0.8 copy-done.6
  110.6 9.7 %shard_map.99 = (f32[1,120,8192]{2,1,0:T(8,128)}, f32[120,120]{1,0:T(8,128)}) custom-call(f32[128,128]{1,0:T(8,128)S(1)} %bitcast.63, f32[40,8192]{1,0:T(8,128)S(1)} %bitcast.57, f32[40,8192]{1,0:T(8,128)S(1)} %copy-done.3, f32[40,8192]{1,0:T(8,128)S(1)} %bitcast.62), custom_call_target="tpu_custom_call" | custom-call | flops 707788800 | bytes 7864320 | tf_op jit(solution)/shard_map/pallas_call | solution.py:298
  (16 shorter events, 0.1 us)
Async XLA Ops:
  0.6 18.7 %collective-permute-start = (s32[3072]{0:T(1024)}, s32[3072]{0:T(1024)S(1)}, u32[]{:S(2)}, u32[]{:S(2)}) collective-permute-start(s32[3072]{0:T(1024)} %bitcast.68), channel_id=1, source_target_pairs={{0,16},{16,0},{1,17},{17,1},{2,18},{18,2},{3,19},{19,3},{4,20},{20... | collective-permute-start | bytes 36872 | tf_op jit(solution)/shard_map/ppermute | solution.py:16
  1.2 13.8 %copy-start.10 = (s32[1,3,256]{2,0,1:T(1,128)S(1)}, s32[1,3,256]{2,0,1:T(1,128)}, u32[]{:S(2)}) copy-start(s32[1,3,256]{2,0,1:T(1,128)} %param.10) | copy-start | bytes 9220
  1.2 14.0 %copy-start.11 = (f32[1,3,256]{2,0,1:T(1,128)S(1)}, f32[1,3,256]{2,0,1:T(1,128)}, u32[]{:S(2)}) copy-start(f32[1,3,256]{2,0,1:T(1,128)} %param.11) | copy-start | bytes 9220
  1.2 19.0 %slice-start = ((s8[6291456]{0:T(1024)(128)(4,1)}), s8[2097152]{0:T(1024)(128)(4,1)S(1)}, s32[]{:S(2)}) async-start(s8[6291456]{0:T(1024)(128)(4,1)} %bitcast.47), calls=%async_computation | async-start | bytes 4194304
  4.3 16.0 %collective-permute-start.3 = (bf16[80,8192]{1,0:T(8,128)(2,1)}, bf16[80,8192]{1,0:T(8,128)(2,1)}, u32[]{:S(2)}, u32[]{:S(2)}) collective-permute-start(bf16[80,8192]{1,0:T(8,128)(2,1)} %fusion.13), channel_id=1, source_target_pairs={{0,16},{16,0},{1,17},{17,1},{2,18},{18,2},{3,19},{19,3},{4,20},{20... | collective-permute-start | bytes 3932168 | tf_op jit(solution)/shard_map/ppermute | solution.py:16
  6.0 13.3 %collective-permute-start.2 = (bf16[80,1024]{1,0:T(8,128)(2,1)}, bf16[80,1024]{1,0:T(8,128)(2,1)}, u32[]{:S(2)}, u32[]{:S(2)}) collective-permute-start(bf16[80,1024]{1,0:T(8,128)(2,1)} %get-tuple-element.8), channel_id=1, source_target_pairs={{1,0},{2,1},{3,2},{4,3},{5,4},{6,5},{7,6},{8,7},{9,8},{10,9},{11,1... | collective-permute-start | bytes 491528 | tf_op jit(solution)/shard_map/ppermute | solution.py:26
  7.3 12.9 %collective-permute-start.1 = (bf16[80,1024]{1,0:T(8,128)(2,1)}, bf16[80,1024]{1,0:T(8,128)(2,1)}, u32[]{:S(2)}, u32[]{:S(2)}) collective-permute-start(bf16[80,1024]{1,0:T(8,128)(2,1)} %get-tuple-element.9), channel_id=1, source_target_pairs={{0,1},{1,2},{2,3},{3,4},{4,5},{5,6},{6,7},{7,8},{8,9},{9,10},{10,1... | collective-permute-start | bytes 491528 | tf_op jit(solution)/shard_map/ppermute | solution.py:25
  14.2 3.4 %copy-start = (f32[1,40,8192]{2,1,0:T(8,128)S(1)}, f32[1,40,8192]{2,1,0:T(8,128)}, u32[]{:S(2)}) copy-start(f32[1,40,8192]{2,1,0:T(8,128)} %param.8) | copy-start | bytes 3932164
  15.3 4.9 %slice-start.1 = ((s8[6291456]{0:T(1024)(128)(4,1)}), s8[4194304]{0:T(1024)(128)(4,1)S(1)}, s32[]{:S(2)}) async-start(s8[6291456]{0:T(1024)(128)(4,1)} %bitcast.47), calls=%async_computation.1 | async-start | bytes 8388608
  17.7 1.6 %copy-start.8 = (f32[3072]{0:T(1024)S(1)}, f32[3072]{0:T(1024)}, u32[]{:S(2)}) copy-start(f32[3072]{0:T(1024)} %param.15) | copy-start | bytes 36868
  17.7 1.6 %copy-start.9 = (s32[1,3072]{1,0:T(1,128)S(1)}, s32[1,3072]{1,0:T(1,128)}, u32[]{:S(2)}) copy-start(s32[1,3072]{1,0:T(1,128)} %param.13) | copy-start | bytes 36868
  40.7 1.5 %copy-start.1 = (f32[80,8192]{1,0:T(8,128)}, f32[80,8192]{1,0:T(8,128)S(1)}, u32[]{:S(2)}) copy-start(f32[80,8192]{1,0:T(8,128)S(1)} %shard_map.95) | copy-start | bytes 7864324
  42.2 26.5 %slice-start.2 = ((s8[6291456]{0:T(1024)(128)(4,1)}), s8[2097152]{0:T(1024)(128)(4,1)S(1)}, s32[]{:S(2)}) async-start(s8[6291456]{0:T(1024)(128)(4,1)} %bitcast.50), calls=%async_computation.2 | async-start | bytes 4194304
  58.3 8.5 %copy-start.4 = (f32[1,40,8192]{2,1,0:T(8,128)S(1)}, f32[1,40,8192]{2,1,0:T(8,128)}, u32[]{:S(2)}) copy-start(f32[1,40,8192]{2,1,0:T(8,128)} %param.9) | copy-start | bytes 3932164
  58.3 10.3 %slice-start.3 = ((s8[6291456]{0:T(1024)(128)(4,1)}), s8[4194304]{0:T(1024)(128)(4,1)S(1)}, s32[]{:S(2)}) async-start(s8[6291456]{0:T(1024)(128)(4,1)} %bitcast.50), calls=%async_computation.3 | async-start | bytes 8388608
  60.5 27.7 %copy-start.2 = (f32[40,8192]{1,0:T(8,128)}, f32[40,8192]{1,0:T(8,128)S(1)}, u32[]{:S(2)}) copy-start(f32[40,8192]{1,0:T(8,128)S(1)} %get-tuple-element.5.x_ref.r_ref) | copy-start | bytes 3932164
  60.5 8.1 %collective-permute-start.6 = (bf16[40,8192]{1,0:T(8,128)(2,1)S(1)}, bf16[40,8192]{1,0:T(8,128)(2,1)S(1)}, u32[]{:S(2)}, u32[]{:S(2)}) collective-permute-start(bf16[40,8192]{1,0:T(8,128)(2,1)S(1)} %get-tuple-element.4), channel_id=1, source_target_pairs={{0,16},{16,0},{1,17},{17,1},{2,18},{18,2},{3,19},{19,3},{4,20},{20... | collective-permute-start | bytes 1966088 | tf_op jit(solution)/shard_map/ppermute | solution.py:16
  60.6 8.0 %collective-permute-start.5 = (bf16[40,1024]{1,0:T(8,128)(2,1)S(1)}, bf16[40,1024]{1,0:T(8,128)(2,1)S(1)}, u32[]{:S(2)}, u32[]{:S(2)}) collective-permute-start(bf16[40,1024]{1,0:T(8,128)(2,1)S(1)} %get-tuple-element.10), channel_id=1, source_target_pairs={{1,0},{2,1},{3,2},{4,3},{5,4},{6,5},{7,6},{8,7},{9,8},{10,9},{11,1... | collective-permute-start | bytes 245768 | tf_op jit(solution)/shard_map/ppermute | solution.py:26
  62.0 6.6 %collective-permute-start.4 = (bf16[40,1024]{1,0:T(8,128)(2,1)S(1)}, bf16[40,1024]{1,0:T(8,128)(2,1)S(1)}, u32[]{:S(2)}, u32[]{:S(2)}) collective-permute-start(bf16[40,1024]{1,0:T(8,128)(2,1)S(1)} %get-tuple-element.11), channel_id=1, source_target_pairs={{0,1},{1,2},{2,3},{3,4},{4,5},{5,6},{6,7},{7,8},{8,9},{9,10},{10,1... | collective-permute-start | bytes 245768 | tf_op jit(solution)/shard_map/ppermute | solution.py:25
  68.6 19.7 %copy-start.7 = (f32[40,8192]{1,0:T(8,128)S(1)}, f32[40,8192]{1,0:T(8,128)}, u32[]{:S(2)}) copy-start(f32[40,8192]{1,0:T(8,128)} %get-tuple-element.6) | copy-start | bytes 3932164
  88.2 20.2 %copy-start.5 = (f32[1,40,8192]{2,1,0:T(8,128)S(1)}, f32[1,40,8192]{2,1,0:T(8,128)}, u32[]{:S(2)}) copy-start(f32[1,40,8192]{2,1,0:T(8,128)} %param.9) | copy-start | bytes 3932164
  108.4 1.3 %copy-start.3 = (f32[40,8192]{1,0:T(8,128)S(1)}, f32[40,8192]{1,0:T(8,128)}, u32[]{:S(2)}) copy-start(f32[40,8192]{1,0:T(8,128)} %copy-done.2) | copy-start | bytes 3932164
  109.7 0.8 copy-start.6

commit v2 on v1

--- a/solution.py
+++ b/solution.py
@@ -9,22 +9,11 @@
 
 BS = 512
 LANES = 128
-SHIFT = 16
-
-
-def swapped(shard, axis, apart):
-    return lax.ppermute(shard, axis, [(i, i ^ 1 << apart) for i in range(lax.axis_size(axis))])
-
-
-def halos(cells, axis, dim, width):
-    count = lax.axis_size(axis)
-    ends = count - 1
-    head = lax.slice_in_dim(cells, 0, width, axis=dim)
-    tail = lax.slice_in_dim(cells, cells.shape[dim] - width, cells.shape[dim], axis=dim)
-    return (
-        lax.ppermute(tail, axis, [(i, i + 1) for i in range(ends)]),
-        lax.ppermute(head, axis, [(i + 1, i) for i in range(ends)]),
-    )
+GROUP = 4
+UNROLL = 64
+MESH = pl.DeviceIdType.MESH
+NN = (((1,), (0,)), ((), ()))
+NT = (((1,), (1,)), ((), ()))
 
 
 def sum_kernel(rounds, split, x_ref, o_ref, held, landed, across, send_sem, recv_sem, side_send, side_recv):
@@ -113,84 +102,6 @@
     )(x)
 
 
-NN = (((1,), (0,)), ((), ()))
-NT = (((1,), (1,)), ((), ()))
-
-
-def operator_kernel(
-    kinds, scales, places, weights, x_ref, before, after, other, tables, o_ref, window, rows_in, rows_out
-):
-    columns, wide = x_ref.shape
-    nbr = wide // BS
-    share = places.shape[0] // nbr
-    window[:, : 2 * BS] = before[...]
-    window[:, 2 * BS : 2 * BS + wide] = x_ref[...].astype(jnp.bfloat16)
-    window[:, 2 * BS + wide :] = after[...]
-    blank = jnp.zeros((LANES - columns, LANES), jnp.float32)
-
-    def turn_in(tile, carry):
-        span = pl.ds(pl.multiple_of(tile * LANES, LANES), LANES)
-        cell = jnp.concatenate([other[:, span].astype(jnp.float32), blank], axis=0)
-        rows_in[span, :] = cell.T
-        rows_out[span, :] = jnp.zeros((LANES, LANES), jnp.float32)
-        return carry
-
-    lax.fori_loop(0, wide // LANES, turn_in, 0, unroll=16)
-
-    def term(n, shift, offset, at, dims):
-        block = window[:, pl.ds(pl.multiple_of((n + 2 + shift) * BS, BS), BS)]
-        product = lax.dot_general(
-            block, tables[offset, kinds[offset, at]], dims, preferred_element_type=jnp.float32
-        )
-        return scales[offset, at] * product
-
-    def step(n, carry):
-        total = term(n, 0, 0, n + 2, NN)
-        for offset in (1, 2):
-            total = total + term(n, offset, offset, n + 2, NT)
-            total = total + term(n, -offset, offset, n + 2 - offset, NN)
-        o_ref[:, pl.ds(pl.multiple_of(n * BS, BS), BS)] = total
-        for slot in range(share):
-            place = places[n * share + slot]
-            source = lax.shift_right_logical(place, SHIFT)
-            target = lax.bitwise_and(place, (1 << SHIFT) - 1)
-            rows_out[pl.ds(target, 1), :] = rows_in[pl.ds(source, 1), :] * weights[n * share + slot]
-        return carry
-
-    lax.fori_loop(0, nbr, step, 0)
-
-    def turn_out(tile, carry):
-        span = pl.ds(pl.multiple_of(tile * LANES, LANES), LANES)
-        o_ref[:, span] = o_ref[:, span] + rows_out[span, :].T[:columns]
-        return carry
-
-    lax.fori_loop(0, wide // LANES, turn_out, 0, unroll=16)
-
-
-def operate(vectors, kinds, scales, tables, places, weights):
-    columns, wide = vectors.shape
-    rounded = vectors.astype(jnp.bfloat16)
-    other = swapped(rounded, "field", 0)
-    before, after = halos(rounded, "dom", 1, 2 * BS)
-    smem = pl.BlockSpec(memory_space=pltpu.SMEM)
-    vmem = pl.BlockSpec(memory_space=pltpu.VMEM)
-    return pl.pallas_call(
-        operator_kernel,
-        out_shape=jax.ShapeDtypeStruct((columns, wide), jnp.float32),
-        in_specs=[smem, smem, smem, smem, vmem, vmem, vmem, vmem, vmem],
-        out_specs=vmem,
-        scratch_shapes=[
-            pltpu.VMEM((columns, wide + 4 * BS), jnp.bfloat16),
-            pltpu.VMEM((wide, LANES), jnp.float32),
-            pltpu.VMEM((wide, LANES), jnp.float32),
-        ],
-        cost_estimate=pl.CostEstimate(
-            flops=10 * columns * wide * BS, bytes_accessed=16 * columns * wide, transcendentals=0
-        ),
-        compiler_params=pltpu.CompilerParams(vmem_limit_bytes=40 * 1024 * 1024),
-    )(kinds, scales, places, weights, vectors, before, after, other, tables)
-
-
 SUB = 8
 
 
@@ -315,45 +226,440 @@
     )(packed, vec_modes, residual_dir, vec_prev)
 
 
+def remote(source, target, sems, peer):
+    return pltpu.make_async_remote_copy(
+        src_ref=source,
+        dst_ref=target,
+        send_sem=sems[0],
+        recv_sem=sems[1],
+        device_id=peer,
+        device_id_type=MESH,
+    )
+
+
+def greet(peers):
+    barrier = pltpu.get_barrier_semaphore()
+    for peer in peers:
+        pl.semaphore_signal(barrier, inc=1, device_id=peer, device_id_type=MESH)
+
+
+def greet_ends(field, dom, ends):
+    barrier = pltpu.get_barrier_semaphore()
+
+    @pl.when(dom > 0)
+    def _():
+        pl.semaphore_signal(barrier, inc=1, device_id=(field, dom - 1), device_id_type=MESH)
+
+    @pl.when(dom < ends)
+    def _():
+        pl.semaphore_signal(barrier, inc=1, device_id=(field, dom + 1), device_id_type=MESH)
+
+
+def meet(dom, ends, count):
+    left = (dom + ends - 1) // ends
+    right = (2 * ends - dom - 1) // ends
+    pl.semaphore_wait(pltpu.get_barrier_semaphore(), count + left + right)
+
+
+def clear_ends(window, nbr):
+    empty = jnp.zeros((2,) + window.shape[1:], window.dtype)
+    window[:2] = empty
+    window[nbr + 2 : nbr + 4] = empty
+
+
+def halo_copies(window, nbr, sems, field, dom):
+    send, recv = sems
+    left = remote(
+        window.at[pl.ds(2, 2)], window.at[pl.ds(nbr + 2, 2)], (send.at[0], recv.at[0]), (field, dom - 1)
+    )
+    right = remote(
+        window.at[pl.ds(nbr, 2)], window.at[pl.ds(0, 2)], (send.at[1], recv.at[1]), (field, dom + 1)
+    )
+    return left, right
+
+
+def start_halos(copies, dom, ends):
+    left, right = copies
+
+    @pl.when(dom > 0)
+    def _():
+        left.start()
+
+    @pl.when(dom < ends)
+    def _():
+        right.start()
+
+
+def finish_halos(copies, dom, ends):
+    left, right = copies
+
+    @pl.when(dom > 0)
+    def _():
+        left.wait_send()
+        right.wait_recv()
+
+    @pl.when(dom < ends)
+    def _():
+        right.wait_send()
+        left.wait_recv()
+
+
+def send_wet(read, columns, wide, rows, count, coupling, rows_in, picked, outgoing, wet, sems, peer):
+    slots = picked.shape[0]
+    blank = jnp.zeros((LANES - columns, LANES), jnp.float32)
+
+    def turn_in(tile, carry):
+        span = pl.ds(pl.multiple_of(tile * LANES, LANES), LANES)
+        rows_in[span, :] = jnp.concatenate([read(span), blank], axis=0).T
+        return carry
+
+    lax.fori_loop(0, wide // LANES, turn_in, 0, unroll=16)
+
+    def gather(i, carry):
+        for slot in range(UNROLL):
+            at = i * UNROLL + slot
+            picked[pl.ds(at, 1), :] = rows_in[pl.ds(rows[0, at], 1), :]
+        return carry
+
+    lax.fori_loop(0, slots // UNROLL, gather, 0)
+
+    def weigh(i, carry):
+        span = pl.ds(pl.multiple_of(i * LANES, LANES), LANES)
+        used = i * LANES + lax.broadcasted_iota(jnp.int32, (1, LANES), 1) < count
+        weights = jnp.where(used, coupling[pl.ds(i, 1), :], 0.0)
+        spread = jnp.broadcast_to(weights, (LANES, LANES)).T
+        outgoing[span, :] = (picked[span, :] * spread).astype(jnp.bfloat16)
+        return carry
+
+    lax.fori_loop(0, slots // LANES, weigh, 0, unroll=4)
+    copy = remote(outgoing, wet, (sems[0].at[0], sems[1].at[0]), peer)
+    copy.start()
+    return copy
+
+
+def first_kernel(
+    rows, counts, coupling, x_ref, p_ref, window, wet, rows_in, picked, outgoing, side_send, side_recv, end_send, end_recv
+):
+    field = lax.axis_index("field")
+    dom = lax.axis_index("dom")
+    ends = lax.axis_size("dom") - 1
+    columns, wide = x_ref.shape
+    nbr = wide // BS
+    clear_ends(window, nbr)
+    greet([(1 - field, dom)])
+    greet_ends(field, dom, ends)
+
+    def read(span):
+        return jnp.concatenate([x_ref[:, span], p_ref[:, span]], axis=0)
+
+    def fill(n, carry):
+        span = pl.ds(pl.multiple_of(n * BS, BS), BS)
+        window[n + 2] = read(span).astype(jnp.bfloat16)
+        return carry
+
+    lax.fori_loop(0, nbr, fill, 0, unroll=2)
+    meet(dom, ends, 1)
+    halos = halo_copies(window, nbr, (end_send, end_recv), field, dom)
+    start_halos(halos, dom, ends)
+    copy = send_wet(
+        read, 2 * columns, wide, rows, counts[0], coupling, rows_in, picked, outgoing, wet,
+        (side_send, side_recv), (1 - field, dom),
+    )
+    finish_halos(halos, dom, ends)
+    copy.wait()
+
+
+def exchange_scratch(wide, slots):
+    return [
+        pltpu.VMEM((wide, LANES), jnp.float32),
+        pltpu.VMEM((slots, LANES), jnp.float32),
+        pltpu.VMEM((slots, LANES), jnp.bfloat16),
+        pltpu.SemaphoreType.DMA((1,)),
+        pltpu.SemaphoreType.DMA((1,)),
+        pltpu.SemaphoreType.DMA((2,)),
+        pltpu.SemaphoreType.DMA((2,)),
+    ]
+
+
+def rows_deep(columns):
+    return -(-columns // 16) * 16
+
+
+SMEM = pl.BlockSpec(memory_space=pltpu.SMEM)
+VMEM = pl.BlockSpec(memory_space=pltpu.VMEM)
+
+
+def exchange_first(vec_modes, vec_prev, wet_rows, wet_counts, coupling):
+    columns, wide = vec_modes.shape
+    slots = wet_rows.shape[1]
+    return pl.pallas_call(
+        first_kernel,
+        out_shape=(
+            jax.ShapeDtypeStruct((wide // BS + 5, rows_deep(2 * columns), BS), jnp.bfloat16),
+            jax.ShapeDtypeStruct((slots, LANES), jnp.bfloat16),
+        ),
+        in_specs=[SMEM, SMEM, VMEM, VMEM, VMEM],
+        out_specs=(VMEM, VMEM),
+        scratch_shapes=exchange_scratch(wide, slots),
+        compiler_params=pltpu.CompilerParams(
+            collective_id=1, has_side_effects=True, vmem_limit_bytes=32 * 1024 * 1024
+        ),
+    )(wet_rows, wet_counts, coupling, vec_modes, vec_prev)
+
+
+def second_kernel(
+    rounds, rows, counts, coupling, x_ref, image, jacobi, window, wet, r_ref,
+    rows_in, picked, outgoing, side_send, side_recv, end_send, end_recv, held, landed, sum_send, sum_recv,
+):
+    field = lax.axis_index("field")
+    dom = lax.axis_index("dom")
+    ends = lax.axis_size("dom") - 1
+    columns, wide = x_ref.shape
+    nbr = wide // BS
+    deep = window.shape[1]
+    groups = []
+    for turn, (step, members) in enumerate(rounds):
+        low = (1 - 2 * ((dom // step) % 2)) * step
+        high = (1 - 2 * ((dom // (2 * step)) % 2)) * 2 * step
+        group = [(field, dom + (e % 2) * low + (e // 2) * high) for e in range(members)]
+        across = [(1 - field, there) for _, there in group] if turn == 0 else []
+        groups.append(group[1:] + across)
+    clear_ends(window, nbr)
+    peers = [peer for group in groups for peer in group]
+    greet(peers)
+    greet_ends(field, dom, ends)
+
+    def add(n, carry):
+        span = pl.ds(pl.multiple_of(n * LANES, LANES), LANES)
+        x = x_ref[:, span]
+        return carry[0] + x * x, carry[1] + x * image[:columns, span]
+
+    zero = jnp.zeros((columns, LANES), jnp.float32)
+    squares, products = lax.fori_loop(0, wide // LANES, add, (zero, zero), unroll=8)
+    lane = lax.broadcasted_iota(jnp.int32, (columns, LANES), 1)
+    total = jnp.where(
+        lane == 0,
+        jnp.sum(squares, axis=1, keepdims=True),
+        jnp.where(lane == 1, jnp.sum(products, axis=1, keepdims=True), 0.0),
+    )
+    meet(dom, ends, len(peers))
+    for turn, group in enumerate(groups):
+        held[turn] = total
+        copies = [
+            remote(held.at[turn], landed.at[turn, e], (sum_send.at[turn, e], sum_recv.at[turn, e]), peer)
+            for e, peer in enumerate(group)
+        ]
+        for copy in copies:
+            copy.start()
+        for copy in copies:
+            copy.wait()
+
+        def four(parts):
+            return (parts[0] + parts[1]) + (parts[2] + parts[3]) if len(parts) == 4 else parts[0] + parts[1]
+
+        members = rounds[turn][1]
+        parts = [total] + [landed[turn, e] for e in range(len(group))]
+        total = four(parts[:members])
+        if len(parts) > members:
+            total = total + four(parts[members:])
+    quotient = total[:, 1:2] / total[:, 0:1]
+    extra = jnp.zeros((deep - columns, BS), jnp.float32)
+
+    def fill(n, carry):
+        span = pl.ds(pl.multiple_of(n * BS, BS), BS)
+        r = (image[:columns, span] - x_ref[:, span] * quotient) / jacobi[:, span]
+        r_ref[:, span] = r
+        window[n + 2] = jnp.concatenate([r, extra], axis=0).astype(jnp.bfloat16)
+        return carry
+
+    lax.fori_loop(0, nbr, fill, 0, unroll=2)
+    halos = halo_copies(window, nbr, (end_send, end_recv), field, dom)
+    start_halos(halos, dom, ends)
+    copy = send_wet(
+        lambda span: r_ref[:, span], columns, wide, rows, counts[0], coupling, rows_in, picked, outgoing, wet,
+        (side_send, side_recv), (1 - field, dom),
+    )
+    finish_halos(halos, dom, ends)
+    copy.wait()
+
+
+def exchange_second(vec_modes, image, jacobi, wet_rows, wet_counts, coupling):
+    columns, wide = vec_modes.shape
+    slots = wet_rows.shape[1]
+    bits = (lax.axis_size("dom") - 1).bit_length()
+    rounds = [(1 << bit, 4 if bit + 1 < bits else 2) for bit in range(0, bits, 2)]
+    most = 2 * rounds[0][1] - 1
+    return pl.pallas_call(
+        functools.partial(second_kernel, rounds),
+        out_shape=(
+            jax.ShapeDtypeStruct((wide // BS + 5, rows_deep(columns), BS), jnp.bfloat16),
+            jax.ShapeDtypeStruct((slots, LANES), jnp.bfloat16),
+            jax.ShapeDtypeStruct((columns, wide), jnp.float32),
+        ),
+        in_specs=[SMEM, SMEM, VMEM, VMEM, VMEM, VMEM],
+        out_specs=(VMEM, VMEM, VMEM),
+        scratch_shapes=exchange_scratch(wide, slots)
+        + [
+            pltpu.VMEM((len(rounds), columns, LANES), jnp.float32),
+            pltpu.VMEM((len(rounds), most, columns, LANES), jnp.float32),
+            pltpu.SemaphoreType.DMA((len(rounds), most)),
+            pltpu.SemaphoreType.DMA((len(rounds), most)),
+        ],
+        compiler_params=pltpu.CompilerParams(
+            collective_id=3, has_side_effects=True, vmem_limit_bytes=32 * 1024 * 1024
+        ),
+    )(wet_rows, wet_counts, coupling, vec_modes, image, jacobi)
+
+
+def group_rows(kind_of, lists, nbr, types, cells):
+    spare = nbr + 2
+    for offset in range(3):
+        for slot in range((cells + 1) * GROUP):
+            lists[offset, slot] = spare
+        known = [kind_of(offset, row) for row in range(2 - offset, nbr + 2)]
+        place = jnp.int32(0)
+        for kind in range(types):
+            for row, found in enumerate(known):
+                lists[offset, place] = row + 2 - offset
+                place = place + (found == kind).astype(jnp.int32)
+            for slot in range(GROUP):
+                lists[offset, place + slot] = spare
+            place = ((place + (GROUP - 1)) // GROUP) * GROUP
+
+
+def operator_kernel(cells, with_diagonal, kinds, scales, rows, window, wet, tables, o_ref, *rest):
+    if with_diagonal:
+        jacobi, diagonal, total, rows_in, rows_out, lists = rest
+    else:
+        total, rows_in, rows_out, lists = rest
+    columns, wide = o_ref.shape
+    nbr = wide // BS
+    types = tables.shape[1]
+    deep = window.shape[1]
+    slots = wet.shape[0]
+    base = lax.axis_index("dom") * nbr - 2
+
+    def kind_of(offset, row):
+        return kinds[offset, jnp.maximum(base + row, 0)]
+
+    def scale_of(offset, row):
+        return scales[offset, jnp.maximum(base + row, 0)]
+
+    group_rows(kind_of, lists, nbr, types, cells)
+
+    def clear(n, carry):
+        total[n] = jnp.zeros(total.shape[1:], jnp.float32)
+        span = pl.ds(pl.multiple_of(n * BS, BS), BS)
+        rows_out[span, :] = jnp.zeros((BS, LANES), jnp.float32)
+        return carry
+
+    lax.fori_loop(0, nbr, clear, 0)
+
+    def widen(i, carry):
+        span = pl.ds(pl.multiple_of(i * LANES, LANES), LANES)
+        rows_in[span, :] = wet[span, :].astype(jnp.float32)
+        return carry
+
+    lax.fori_loop(0, slots // LANES, widen, 0, unroll=4)
+
+    def scatter(i, carry):
+        for slot in range(UNROLL):
+            at = i * UNROLL + slot
+            rows_out[pl.ds(rows[0, at], 1), :] = rows_in[pl.ds(at, 1), :]
+        return carry
+
+    lax.fori_loop(0, slots // UNROLL, scatter, 0)
+    if with_diagonal:
+        eye = lax.broadcasted_iota(jnp.int32, (LANES, LANES), 0) == lax.broadcasted_iota(
+            jnp.int32, (LANES, LANES), 1
+        )
+        for kind in range(types):
+            for part in range(BS // LANES):
+                span = slice(part * LANES, (part + 1) * LANES)
+                cell = tables[0, kind, span, span].astype(jnp.float32)
+                diagonal[kind, :, span] = jnp.sum(jnp.where(eye, cell, 0.0), axis=0, keepdims=True)
+        for n in range(nbr):
+            jacobi[:, n * BS : (n + 1) * BS] = scale_of(0, n + 2) * diagonal[kind_of(0, n + 2)]
+
+    def step(i, carry):
+        for offset in range(3):
+            found = [lists[offset, i * GROUP + u] for u in range(GROUP)]
+            held = [jnp.minimum(row, nbr + 1) for row in found]
+            kind = kind_of(offset, held[0])
+            factors = [scale_of(offset, row) for row in held]
+            for ahead in (True, False) if offset else (True,):
+                if ahead:
+                    sources = [row + offset for row in found]
+                    targets = [jnp.where(row < 2, nbr, row - 2) for row in found]
+                else:
+                    sources = found
+                    targets = [jnp.minimum(row - 2 + offset, nbr) for row in found]
+                left = jnp.concatenate([window[source] for source in sources], axis=0)
+                product = lax.dot_general(
+                    left,
+                    tables[offset, kind],
+                    NT if ahead and offset else NN,
+                    preferred_element_type=jnp.float32,
+                )
+                for u in range(GROUP):
+                    total[targets[u]] += factors[u] * product[u * deep : (u + 1) * deep]
+        return carry
+
+    lax.fori_loop(0, cells, step, 0)
+    parts = BS // LANES
+
+    def turn_out(n, carry):
+        for part in range(parts):
+            span = pl.ds(pl.multiple_of(n * BS + part * LANES, LANES), LANES)
+            inner = slice(part * LANES, (part + 1) * LANES)
+            o_ref[:, span] = total[n, :columns, inner] + rows_out[span, :].T[:columns]
+        return carry
+
+    lax.fori_loop(0, nbr, turn_out, 0, unroll=4)
+
+
+def operate(columns, window, wet, kinds, scales, rows, tables, with_diagonal):
+    nbr = window.shape[0] - 5
+    wide = nbr * BS
+    deep = window.shape[1]
+    slots = wet.shape[0]
+    types = tables.shape[1]
+    cells = (nbr + 2 + types * (GROUP - 1)) // GROUP
+    outs = [jax.ShapeDtypeStruct((columns, wide), jnp.float32)]
+    scratch = [
+        pltpu.VMEM((nbr + 1, deep, BS), jnp.float32),
+        pltpu.VMEM((slots, LANES), jnp.float32),
+        pltpu.VMEM((wide, LANES), jnp.float32),
+        pltpu.SMEM((3, (cells + 1) * GROUP), jnp.int32),
+    ]
+    if with_diagonal:
+        outs.append(jax.ShapeDtypeStruct((1, wide), jnp.float32))
+        scratch = [pltpu.VMEM((types, 1, BS), jnp.float32)] + scratch
+    return pl.pallas_call(
+        functools.partial(operator_kernel, cells, with_diagonal),
+        out_shape=tuple(outs),
+        in_specs=[SMEM, SMEM, SMEM, VMEM, VMEM, VMEM],
+        out_specs=(VMEM,) * len(outs),
+        scratch_shapes=scratch,
+        cost_estimate=pl.CostEstimate(
+            flops=10 * columns * wide * BS, bytes_accessed=16 * columns * wide, transcendentals=0
+        ),
+        compiler_params=pltpu.CompilerParams(vmem_limit_bytes=32 * 1024 * 1024),
+    )(kinds, scales, rows, window, wet, tables)
+
+
 def shards(modes, previous, kinds, scales, tables, wet_rows, wet_counts, coupling):
     high = lax.Precision.HIGH
-    domain = lax.axis_index("dom")
     vec_modes = modes[0]
     vec_prev = previous[0]
     columns, wide = vec_modes.shape
-    nbr = wide // BS
-    field_tables = tables[0]
-    types = field_tables.shape[1]
-    kinds_pad = jnp.pad(kinds[0], ((0, 0), (2, 0)))
-    scales_pad = jnp.pad(scales[0], ((0, 0), (2, 0)))
-    local_kinds = lax.dynamic_slice_in_dim(kinds_pad, domain * nbr, nbr + 2, 1)
-    local_scales = lax.dynamic_slice_in_dim(scales_pad, domain * nbr, nbr + 2, 1)
-    rows = wet_rows[0]
-    slots = coupling.shape[0]
-    used = jnp.arange(slots, dtype=jnp.int32) < wet_counts[0]
-    weights = jnp.where(used, coupling, jnp.float32(0.0))
-    places = (swapped(rows, "field", 0) << SHIFT) | rows
-    operands = (local_kinds, local_scales, field_tables, places, weights)
-    first_pair = jnp.concatenate([vec_modes, vec_prev], axis=0)
-    image_pair = operate(first_pair, *operands)
+    shared = (kinds[0], scales[0], wet_rows, tables[0])
+    weights = coupling.reshape(-1, LANES)
+    window, wet = exchange_first(vec_modes, vec_prev, wet_rows, wet_counts, weights)
+    image_pair, jacobi = operate(2 * columns, window, wet, *shared, True)
     image_x, image_p = image_pair[:columns], image_pair[columns:]
-    partial_sums = jnp.stack(
-        [jnp.sum(vec_modes * vec_modes, axis=1), jnp.sum(vec_modes * image_x, axis=1)]
-    )
-    sums = summed_everywhere(jnp.pad(partial_sums, ((0, 6), (0, LANES - columns)))[None], 1)[0]
-    quotient = sums[1, :columns] / sums[0, :columns]
-    eye = jnp.eye(BS, dtype=jnp.bool_)
-    diag_table = jnp.sum(
-        jnp.where(eye[None], field_tables[0].astype(jnp.float32), jnp.float32(0.0)), axis=1
-    )
-    row_diag = jnp.zeros((nbr, BS), jnp.float32)
-    for type_id in range(types):
-        row_diag = jnp.where(
-            (local_kinds[0, 2:] == type_id)[:, None], diag_table[type_id][None, :], row_diag
-        )
-    jacobi = (local_scales[0, 2:][:, None] * row_diag).reshape(wide)
-    residual_dir = (image_x - vec_modes * quotient[:, None]) / jacobi[None, :]
-    image_r = operate(residual_dir, *operands)
+    window, wet, residual_dir = exchange_second(vec_modes, image_pair, jacobi, wet_rows, wet_counts, weights)
+    (image_r,) = operate(columns, window, wet, *shared, False)
     search = jnp.concatenate([vec_modes, residual_dir, vec_prev], axis=0)
     image_all = jnp.concatenate([image_x, image_r, image_p], axis=0)
     ndof = 2.0 * lax.axis_size("dom") * wide

time: 121 us -> 101 us (0.83)
  starting transfers between devices: 14.2 us -> 0 us
  other arithmetic: 12.7 us -> 0.1 us
  local copies, waits for them, and re-layouts: 6.44 us -> 11 us
  matrix products: 3.55 us -> 5.4 us
    pallas_call x2 -> x4, Pallas kernels: 40 us -> 58.2 us  [the longest x2 25.6 us: operate(): pl.pallas_call(functools.partial(operator_kernel, cells, with_diagonal),...]
    pallas_call x2 -> x1, Pallas kernels: 31 us -> 14 us  [summed_everywhere(): pl.pallas_call(functools.partial(sum_kernel, rounds, x.shape[0] == 2), ou...]
    ppermute x7 -> x0, starting transfers between devices: 14.2 us -> none  [the longest x2 10.9 us: halos(): lax.ppermute(tail, axis, [(i, i + 1) for i in range(ends)])]
    unnamed x35 -> x32, local copies, waits for them, and re-layouts: 3.71 us -> 10.1 us
    convert_element_type x2 -> x0, other arithmetic: 5.22 us -> none  [operate(): rounded = vectors.astype(jnp.bfloat16)]
    reduce_sum x2 -> x0, other arithmetic: 3.55 us -> none  [the longest x1 2.24 us: shards(): jnp.sum(jnp.where(eye[None], field_tables[0].astype(jnp.float32), jnp.flo...]
    dot_general x1, matrix products: 1.76 us -> 3.58 us  [shards(): part_b = jnp.dot(search, search.T, precision=high)]
    slice x3 -> x1, local copies, waits for them, and re-layouts: 1.78 us -> 0.18 us  [shards(): image_x, image_p = (image_pair[:columns], image_pair[columns:])]
  transfers between devices with their start and end apart: 7 -> 0, of which waited for: 2 -> 0; matrix products, arithmetic and copies ran while one was open for 10% -> 0% of each run, Pallas kernels for 0% -> 0%
where the time goes in v2:
time: 101 us; the launch traced here: 100 us
  Pallas kernels  81.9 us (81%)
  local copies, waits for them, and re-layouts  11 us (11%)
  matrix products  5.4 us (5%)
  between operations  1.64 us (2%)
    pallas_call x2, Pallas kernels, operate(): pl.pallas_call(functools.partial(operator_kernel, cells, with_diagonal),...  25.6 us
    pallas_call x1, Pallas kernels, exchange_second(): pl.pallas_call(functools.partial(second_kernel, rounds), out_shape=(jax.S...  21.9 us
    pallas_call x1, Pallas kernels, summed_everywhere(): pl.pallas_call(functools.partial(sum_kernel, rounds, x.shape[0] == 2), ou...  14 us
    pallas_call x1, Pallas kernels, exchange_first(): pl.pallas_call(first_kernel, out_shape=(jax.ShapeDtypeStruct((wide // BS...  10.8 us
    unnamed x32, local copies, waits for them, and re-layouts  10.1 us
    pallas_call x1, Pallas kernels, finish(): pl.pallas_call(functools.partial(finish_kernel, chunk, 1.0 / ndof), out_s...  9.7 us
    dot_general x1, matrix products, shards(): part_b = jnp.dot(search, search.T, precision=high)  3.58 us

profile of v2, /device:TPU:0, one launch (start us, length us, event | category | flops | bytes accessed | tf_op | source)
XLA Modules:
  0.0 100.1 jit_solution(7855005046241808343)
XLA Ops:
  1.3 0.0 copy-start
  1.3 1.3 %copy-done = f32[1,40,8192]{2,1,0:T(8,128)S(1)} copy-done((f32[1,40,8192]{2,1,0:T(8,128)S(1)}, f32[1,40,8192]{2,1,0:T(8,128)}, u32[]{:S(2)}) %copy-start) | copy-done | bytes 1310744
  2.6 0.0 copy-start.4
  2.6 1.3 %copy-done.4 = f32[1,40,8192]{2,1,0:T(8,128)S(1)} copy-done((f32[1,40,8192]{2,1,0:T(8,128)S(1)}, f32[1,40,8192]{2,1,0:T(8,128)}, u32[]{:S(2)}) %copy-start.4) | copy-done | bytes 1310744
  3.9 0.0 copy-start.9
  3.9 0.7 copy-done.9
  4.6 0.0 copy-start.11
  4.6 0.7 copy-done.11
  5.3 0.0 copy-start.13
  5.3 0.0 copy-start.14
  5.3 0.0 copy-start.10
  5.3 10.8 %shard_map.95 = (bf16[21,80,512]{2,1,0:T(8,128)(2,1)S(1)}, bf16[3072,128]{1,0:T(8,128)(2,1)S(1)}) custom-call(s32[1,3072]{1,0:T(1,128)S(1)} %copy-done.9, s32[1]{0:T(128)S(6)} %copy.17.counts, f32[24,128]{1,0:T(8,128)S(1)} %bitcast.26, f32[40,8192]{1,0:T(8,128)S(1)} %bitcast.14, f32[40,8192]{1,0:T(8,128)S(1)} %bitcast.21), custom_call_target="tpu_custom_call" | custom-call | tf_op jit(solution)/shard_map/pallas_call | solution.py:395
  16.1 0.0 copy-done.13
  16.1 0.0 copy-done.14
  16.1 0.0 copy-done.10
  16.2 0.0 copy-start.2
  16.2 2.8 %copy-done.2 = bf16[1,3,4,512,512]{4,3,2,1,0:T(8,128)(2,1)S(1)} copy-done((bf16[1,3,4,512,512]{4,3,2,1,0:T(8,128)(2,1)S(1)}, bf16[1,3,4,512,512]{4,3,2,1,0:T(8,128)(2,1)}, u32[]{:S(2)}) %copy-start.2) | copy-done | bytes 6291480
  18.9 0.0 copy-start.1
  18.9 0.0 copy-start.12
  18.9 0.0 copy-start.3
  18.9 13.6 %shard_map.96 = (f32[80,8192]{1,0:T(8,128)S(1)}, f32[1,8192]{1,0:T(1,128)S(1)}) custom-call(s32[3,256]{1,0:T(4,128)S(1)} %bitcast.30, f32[3,256]{1,0:T(4,128)S(1)} %bitcast.28, s32[1,3072]{1,0:T(1,128)S(1)} %copy-done.10, bf16[21,80,512]{2,1,0:T(8,128)(2,1)S(1)} %get-tuple-element.9.window, bf16[3072,128]{1,0:T(8,128)(2,1)S(1)} %get-tuple-element.10.wet, ...), custom_call_target="tpu_custom_call" | custom-call | flops 3355443200 | bytes 10485760 | tf_op jit(solution)/shard_map/pallas_call | solution.py:638
  32.5 0.0 copy-done.1
  32.6 0.0 copy-done.12
  32.6 21.9 %shard_map.97 = (bf16[21,48,512]{2,1,0:T(8,128)(2,1)S(1)}, bf16[3072,128]{1,0:T(8,128)(2,1)S(1)}, f32[40,8192]{1,0:T(8,128)S(1)}) custom-call(s32[1,3072]{1,0:T(1,128)S(1)} %copy-done.10, s32[1]{0:T(128)S(6)} %copy.17.counts, f32[24,128]{1,0:T(8,128)S(1)} %bitcast.27, f32[40,8192]{1,0:T(8,128)S(1)} %bitcast.15, f32[80,8192]{1,0:T(8,128)S(1)} %get-tuple-element.11.image, ...), custom_call_target="tpu_custom_call" | custom-call | tf_op jit(solution)/shard_map/pallas_call | solution.py:492
  54.5 0.0 copy-start.6
  54.5 0.0 copy-done.3
  54.5 12.0 %shard_map.98 = f32[40,8192]{1,0:T(8,128)S(1)} custom-call(s32[3,256]{1,0:T(4,128)S(1)} %bitcast.31, f32[3,256]{1,0:T(4,128)S(1)} %bitcast.29, s32[1,3072]{1,0:T(1,128)S(1)} %copy-done.10, bf16[21,48,512]{2,1,0:T(8,128)(2,1)S(1)} %get-tuple-element.14.window, bf16[3072,128]{1,0:T(8,128)(2,1)S(1)} %get-tuple-element.15.wet, bf16[3,4,512,512]{3,2,1,0:T(8,128)(2,1)S(1)} %bitcast.20), custom_call_target="tpu_custom_call" | custom-call | flops 1677721600 | bytes 5242880 | tf_op jit(solution)/shard_map/pallas_call | solution.py:638
  66.5 0.0 copy-start.5
  66.5 0.2 fusion.9
  66.7 0.0 copy-done.6
  66.7 1.1 %copy-done.5 = f32[1,40,8192]{2,1,0:T(8,128)S(1)} copy-done((f32[1,40,8192]{2,1,0:T(8,128)S(1)}, f32[1,40,8192]{2,1,0:T(8,128)}, u32[]{:S(2)}) %copy-start.5) | copy-done | bytes 1310744
  67.8 1.8 %fusion = f32[120,120]{1,0:T(8,128)S(1)} fusion(f32[40,8192]{1,0:T(8,128)S(1)} %get-tuple-element.17, f32[40,8192]{1,0:T(8,128)S(1)} %shard_map.98, f32[40,8192]{1,0:T(8,128)S(1)} %get-tuple-element.16, f32[40,8192]{1,0:T(8,128)S(1)} %bitcast.22, f32[40,8192]{1,0:T(8,128)S(1)} %get-tuple-element.13.r_ref, f32[40,8192]{1,0:T(8,128)S(1)} %bitcast.16), kind=kOutput, calls=%fused_computation.1 | convolution fusion | flops 711720960 | bytes 7921920 | tf_op jit(solution)/shard_map/dot_general | solution.py:667
  69.7 0.1 copy.10
  69.8 3.6 %fusion.6 = f32[120,120]{1,0:T(8,128)S(1)} fusion(f32[40,8192]{1,0:T(8,128)S(1)} %bitcast.23, f32[40,8192]{1,0:T(8,128)} %copy-done.6, f32[40,8192]{1,0:T(8,128)S(1)} %bitcast.17), kind=kOutput, calls=%fused_computation.7 | convolution fusion | flops 709754880 | bytes 3989760 | tf_op jit(solution)/shard_map/dot_general | solution.py:666
  73.3 0.1 pad_select_fusion
  73.4 0.6 pad.14
  74.1 14.0 %shard_map.99 = f32[2,64,128]{2,1,0:T(8,128)} custom-call(f32[2,64,128]{2,1,0:T(8,128)} %bitcast.32), custom_call_target="tpu_custom_call" | custom-call | tf_op jit(solution)/shard_map/pallas_call | solution.py:85
  88.1 0.0 copy-start.7
  88.1 1.3 %copy-done.7 = f32[40,8192]{1,0:T(8,128)S(1)} copy-done((f32[40,8192]{1,0:T(8,128)S(1)}, f32[40,8192]{1,0:T(8,128)}, u32[]{:S(2)}) %copy-start.7) | copy-done | bytes 1310744
  89.4 0.0 copy-start.8
  89.4 0.8 copy-done.8
  90.2 9.7 %shard_map.100 = (f32[1,120,8192]{2,1,0:T(8,128)}, f32[120,120]{1,0:T(8,128)}) custom-call(f32[128,128]{1,0:T(8,128)S(1)} %bitcast.25, f32[40,8192]{1,0:T(8,128)S(1)} %bitcast.18, f32[40,8192]{1,0:T(8,128)S(1)} %copy-done.7, f32[40,8192]{1,0:T(8,128)S(1)} %bitcast.24), custom_call_target="tpu_custom_call" | custom-call | flops 707788800 | bytes 7864320 | tf_op jit(solution)/shard_map/pallas_call | solution.py:209
  (3 shorter events, 0.0 us)
Async XLA Ops:
  1.3 1.3 %copy-start = (f32[1,40,8192]{2,1,0:T(8,128)S(1)}, f32[1,40,8192]{2,1,0:T(8,128)}, u32[]{:S(2)}) copy-start(f32[1,40,8192]{2,1,0:T(8,128)} %param.8) | copy-start | bytes 3932164
  2.6 1.3 %copy-start.4 = (f32[1,40,8192]{2,1,0:T(8,128)S(1)}, f32[1,40,8192]{2,1,0:T(8,128)}, u32[]{:S(2)}) copy-start(f32[1,40,8192]{2,1,0:T(8,128)} %param.9) | copy-start | bytes 3932164
  3.9 0.7 copy-start.9
  4.6 0.7 copy-start.11
  5.3 10.8 %copy-start.13 = (f32[1,3,256]{2,0,1:T(1,128)S(1)}, f32[1,3,256]{2,0,1:T(1,128)}, u32[]{:S(2)}) copy-start(f32[1,3,256]{2,0,1:T(1,128)} %param.11) | copy-start | bytes 9220
  5.3 10.8 %copy-start.14 = (s32[1,3,256]{2,0,1:T(1,128)S(1)}, s32[1,3,256]{2,0,1:T(1,128)}, u32[]{:S(2)}) copy-start(s32[1,3,256]{2,0,1:T(1,128)} %param.10) | copy-start | bytes 9220
  5.3 10.8 %copy-start.10 = (s32[1,3072]{1,0:T(1,128)S(1)}, s32[1,3072]{1,0:T(1,128)}, u32[]{:S(2)}) copy-start(s32[1,3072]{1,0:T(1,128)} %rows.7) | copy-start | bytes 36868
  16.2 2.8 %copy-start.2 = (bf16[1,3,4,512,512]{4,3,2,1,0:T(8,128)(2,1)S(1)}, bf16[1,3,4,512,512]{4,3,2,1,0:T(8,128)(2,1)}, u32[]{:S(2)}) copy-start(bf16[1,3,4,512,512]{4,3,2,1,0:T(8,128)(2,1)} %param.12) | copy-start | bytes 18874372
  18.9 13.6 %copy-start.1 = (f32[1,40,8192]{2,1,0:T(8,128)S(1)}, f32[1,40,8192]{2,1,0:T(8,128)}, u32[]{:S(2)}) copy-start(f32[1,40,8192]{2,1,0:T(8,128)} %param.8) | copy-start | bytes 3932164
  18.9 13.6 %copy-start.12 = (f32[3072]{0:T(1024)S(1)}, f32[3072]{0:T(1024)}, u32[]{:S(2)}) copy-start(f32[3072]{0:T(1024)} %param.15) | copy-start | bytes 36868
  18.9 35.6 %copy-start.3 = (bf16[1,3,4,512,512]{4,3,2,1,0:T(8,128)(2,1)S(1)}, bf16[1,3,4,512,512]{4,3,2,1,0:T(8,128)(2,1)}, u32[]{:S(2)}) copy-start(bf16[1,3,4,512,512]{4,3,2,1,0:T(8,128)(2,1)} %param.12) | copy-start | bytes 18874372
  54.5 12.2 %copy-start.6 = (f32[40,8192]{1,0:T(8,128)}, f32[40,8192]{1,0:T(8,128)S(1)}, u32[]{:S(2)}) copy-start(f32[40,8192]{1,0:T(8,128)S(1)} %get-tuple-element.13.r_ref) | copy-start | bytes 3932164
  66.5 1.3 %copy-start.5 = (f32[1,40,8192]{2,1,0:T(8,128)S(1)}, f32[1,40,8192]{2,1,0:T(8,128)}, u32[]{:S(2)}) copy-start(f32[1,40,8192]{2,1,0:T(8,128)} %param.9) | copy-start | bytes 3932164
  88.1 1.3 %copy-start.7 = (f32[40,8192]{1,0:T(8,128)S(1)}, f32[40,8192]{1,0:T(8,128)}, u32[]{:S(2)}) copy-start(f32[40,8192]{1,0:T(8,128)} %copy-done.6) | copy-start | bytes 3932164
  89.4 0.8 copy-start.8

commit v3 on v2

--- a/solution.py
+++ b/solution.py
@@ -11,95 +11,11 @@
 LANES = 128
 GROUP = 4
 UNROLL = 64
+PARTS = 4
+SPAN = 2048
 MESH = pl.DeviceIdType.MESH
 NN = (((1,), (0,)), ((), ()))
 NT = (((1,), (1,)), ((), ()))
-
-
-def sum_kernel(rounds, split, x_ref, o_ref, held, landed, across, send_sem, recv_sem, side_send, side_recv):
-    field = lax.axis_index("field")
-    dom = lax.axis_index("dom")
-    groups = []
-    for step, members in rounds:
-        low = (1 - 2 * ((dom // step) % 2)) * step
-        high = (1 - 2 * ((dom // (2 * step)) % 2)) * 2 * step
-        groups.append([dom + (e % 2) * low + (e // 2) * high for e in range(1, members)])
-    barrier = pltpu.get_barrier_semaphore()
-    peers = [(1 - field, dom)] + [(field, peer) for group in groups for peer in group]
-    for peer in peers:
-        pl.semaphore_signal(barrier, inc=1, device_id=peer, device_id_type=pl.DeviceIdType.MESH)
-    pl.semaphore_wait(barrier, len(peers))
-
-    def send(source, target, sems, peer):
-        copy = pltpu.make_async_remote_copy(
-            src_ref=source,
-            dst_ref=target,
-            send_sem=sems[0],
-            recv_sem=sems[1],
-            device_id=peer,
-            device_id_type=pl.DeviceIdType.MESH,
-        )
-        copy.start()
-        return copy
-
-    mine, theirs = (field, 1 - field) if split else (0, 0)
-    copy = send(
-        x_ref.at[theirs], across.at[0], (side_send.at[0], side_recv.at[0]), (1 - field, dom)
-    )
-    copy.wait()
-    total = x_ref[mine] + across[0]
-    for turn, group in enumerate(groups):
-        held[turn] = total
-        copies = [
-            send(
-                held.at[turn],
-                landed.at[turn, e],
-                (send_sem.at[turn, e], recv_sem.at[turn, e]),
-                (field, peer),
-            )
-            for e, peer in enumerate(group)
-        ]
-        for copy in copies:
-            copy.wait()
-        total = total + landed[turn, 0]
-        if len(group) == 3:
-            total = total + (landed[turn, 1] + landed[turn, 2])
-    o_ref[mine] = total
-    if split:
-        held[len(groups)] = total
-        copy = send(
-            held.at[len(groups)],
-            across.at[1],
-            (side_send.at[1], side_recv.at[1]),
-            (1 - field, dom),
-        )
-        copy.wait()
-        o_ref[theirs] = across[1]
-
-
-def summed_everywhere(x, collective_id):
-    bits = (lax.axis_size("dom") - 1).bit_length()
-    rounds = [(1 << bit, 4 if bit + 1 < bits else 2) for bit in range(0, bits, 2)]
-    cell = x.shape[1:]
-    slots = len(rounds)
-    return pl.pallas_call(
-        functools.partial(sum_kernel, rounds, x.shape[0] == 2),
-        out_shape=jax.ShapeDtypeStruct(x.shape, x.dtype),
-        in_specs=[pl.BlockSpec(memory_space=pltpu.VMEM)],
-        out_specs=pl.BlockSpec(memory_space=pltpu.VMEM),
-        scratch_shapes=[
-            pltpu.VMEM((slots + 1,) + cell, x.dtype),
-            pltpu.VMEM((slots, 3) + cell, x.dtype),
-            pltpu.VMEM((2,) + cell, x.dtype),
-            pltpu.SemaphoreType.DMA((slots, 3)),
-            pltpu.SemaphoreType.DMA((slots, 3)),
-            pltpu.SemaphoreType.DMA((2,)),
-            pltpu.SemaphoreType.DMA((2,)),
-        ],
-        compiler_params=pltpu.CompilerParams(
-            collective_id=collective_id, has_side_effects=True
-        ),
-    )(x)
 
 
 SUB = 8
@@ -331,20 +247,31 @@
         outgoing[span, :] = (picked[span, :] * spread).astype(jnp.bfloat16)
         return carry
 
-    lax.fori_loop(0, slots // LANES, weigh, 0, unroll=4)
-    copy = remote(outgoing, wet, (sems[0].at[0], sems[1].at[0]), peer)
-    copy.start()
-    return copy
+    cells = slots // LANES
+    copies = []
+    for part in range(PARTS):
+        low, high = cells * part // PARTS, cells * (part + 1) // PARTS
+        lax.fori_loop(low, high, weigh, 0, unroll=2)
+        span = pl.ds(low * LANES, (high - low) * LANES)
+        copy = remote(outgoing.at[span], wet.at[span], (sems[0].at[part], sems[1].at[part]), peer)
+        copy.start()
+        copies.append(copy)
+    return copies
 
 
 def first_kernel(
-    rows, counts, coupling, x_ref, p_ref, window, wet, rows_in, picked, outgoing, side_send, side_recv, end_send, end_recv
+    counts, rows_in_hbm, coupling_in, x_in, p_in, tables_in, window, wet, x_ref, p_ref, tables, coupling,
+    rows_in, picked, outgoing, side_send, side_recv, end_send, end_recv, rows, loads,
 ):
     field = lax.axis_index("field")
     dom = lax.axis_index("dom")
     ends = lax.axis_size("dom") - 1
     columns, wide = x_ref.shape
     nbr = wide // BS
+    pairs = [(x_in.at[0], x_ref), (p_in.at[0], p_ref), (rows_in_hbm, rows), (coupling_in, coupling), (tables_in.at[0], tables)]
+    arrivals = [pltpu.make_async_copy(source, target, loads.at[n]) for n, (source, target) in enumerate(pairs)]
+    for arrival in arrivals:
+        arrival.start()
     clear_ends(window, nbr)
     greet([(1 - field, dom)])
     greet_ends(field, dom, ends)
@@ -357,16 +284,22 @@
         window[n + 2] = read(span).astype(jnp.bfloat16)
         return carry
 
+    arrivals[0].wait()
+    arrivals[1].wait()
     lax.fori_loop(0, nbr, fill, 0, unroll=2)
     meet(dom, ends, 1)
     halos = halo_copies(window, nbr, (end_send, end_recv), field, dom)
     start_halos(halos, dom, ends)
-    copy = send_wet(
+    arrivals[2].wait()
+    arrivals[3].wait()
+    copies = send_wet(
         read, 2 * columns, wide, rows, counts[0], coupling, rows_in, picked, outgoing, wet,
         (side_send, side_recv), (1 - field, dom),
     )
+    arrivals[4].wait()
     finish_halos(halos, dom, ends)
-    copy.wait()
+    for copy in copies:
+        copy.wait()
 
 
 def exchange_scratch(wide, slots):
@@ -374,8 +307,8 @@
         pltpu.VMEM((wide, LANES), jnp.float32),
         pltpu.VMEM((slots, LANES), jnp.float32),
         pltpu.VMEM((slots, LANES), jnp.bfloat16),
-        pltpu.SemaphoreType.DMA((1,)),
-        pltpu.SemaphoreType.DMA((1,)),
+        pltpu.SemaphoreType.DMA((PARTS,)),
+        pltpu.SemaphoreType.DMA((PARTS,)),
         pltpu.SemaphoreType.DMA((2,)),
         pltpu.SemaphoreType.DMA((2,)),
     ]
@@ -387,28 +320,84 @@
 
 SMEM = pl.BlockSpec(memory_space=pltpu.SMEM)
 VMEM = pl.BlockSpec(memory_space=pltpu.VMEM)
-
-
-def exchange_first(vec_modes, vec_prev, wet_rows, wet_counts, coupling):
-    columns, wide = vec_modes.shape
+HBM = pl.BlockSpec(memory_space=pltpu.HBM)
+
+
+def exchange_first(modes, previous, wet_rows, wet_counts, coupling, tables):
+    _, columns, wide = modes.shape
     slots = wet_rows.shape[1]
+    held = jax.ShapeDtypeStruct((columns, wide), jnp.float32)
     return pl.pallas_call(
         first_kernel,
         out_shape=(
             jax.ShapeDtypeStruct((wide // BS + 5, rows_deep(2 * columns), BS), jnp.bfloat16),
             jax.ShapeDtypeStruct((slots, LANES), jnp.bfloat16),
-        ),
-        in_specs=[SMEM, SMEM, VMEM, VMEM, VMEM],
-        out_specs=(VMEM, VMEM),
-        scratch_shapes=exchange_scratch(wide, slots),
+            held,
+            held,
+            jax.ShapeDtypeStruct(tables.shape[1:], tables.dtype),
+            jax.ShapeDtypeStruct(coupling.shape, coupling.dtype),
+        ),
+        in_specs=[SMEM, HBM, HBM, HBM, HBM, HBM],
+        out_specs=(VMEM,) * 6,
+        scratch_shapes=exchange_scratch(wide, slots)
+        + [pltpu.SMEM(wet_rows.shape, jnp.int32), pltpu.SemaphoreType.DMA((5,))],
         compiler_params=pltpu.CompilerParams(
-            collective_id=1, has_side_effects=True, vmem_limit_bytes=32 * 1024 * 1024
-        ),
-    )(wet_rows, wet_counts, coupling, vec_modes, vec_prev)
+            collective_id=1, has_side_effects=True, vmem_limit_bytes=24 * 1024 * 1024
+        ),
+    )(wet_counts, wet_rows, coupling, modes, previous, tables)
+
+
+def gram_part(left, right):
+    lh = left.astype(jnp.bfloat16)
+    ll = (left - lh.astype(jnp.float32)).astype(jnp.bfloat16)
+    rh = right.astype(jnp.bfloat16)
+    rl = (right - rh.astype(jnp.float32)).astype(jnp.bfloat16)
+    rows = left.shape[0]
+    both = lax.dot_general(
+        jnp.concatenate([lh, ll], axis=0), rh, NT, preferred_element_type=jnp.float32
+    )
+    cross = lax.dot_general(lh, rl, NT, preferred_element_type=jnp.float32)
+    return both[:rows] + (both[rows:] + cross)
+
+
+def gram_over(low, high, step, read_left, read_right, out):
+    def add(n, carry):
+        span = pl.ds(pl.multiple_of(n * step, step), step)
+        out[...] += gram_part(read_left(span), read_right(span))
+        return carry
+
+    lax.fori_loop(low, high, add, 0)
+
+
+def neighbours(rounds, field, dom):
+    groups = []
+    for turn, (step, members) in enumerate(rounds):
+        low = (1 - 2 * ((dom // step) % 2)) * step
+        high = (1 - 2 * ((dom // (2 * step)) % 2)) * 2 * step
+        group = [(field, dom + (e % 2) * low + (e // 2) * high) for e in range(members)]
+        across = [(1 - field, there) for _, there in group] if turn == 0 else []
+        groups.append(group[1:] + across)
+    return groups
+
+
+def gathered(total, landed, members):
+    def fold(parts):
+        if len(parts) == 4:
+            return (parts[0] + parts[1]) + (parts[2] + parts[3])
+        return parts[0] + parts[1]
+
+    parts = [total] + landed
+    total = fold(parts[:members])
+    return total + fold(parts[members:]) if len(parts) > members else total
+
+
+def sum_rounds():
+    bits = (lax.axis_size("dom") - 1).bit_length()
+    return [(1 << bit, 4 if bit + 1 < bits else 2) for bit in range(0, bits, 2)]
 
 
 def second_kernel(
-    rounds, rows, counts, coupling, x_ref, image, jacobi, window, wet, r_ref,
+    rounds, rows, counts, coupling, x_ref, p_ref, image, jacobi, window, wet, r_ref, gram,
     rows_in, picked, outgoing, side_send, side_recv, end_send, end_recv, held, landed, sum_send, sum_recv,
 ):
     field = lax.axis_index("field")
@@ -417,13 +406,7 @@
     columns, wide = x_ref.shape
     nbr = wide // BS
     deep = window.shape[1]
-    groups = []
-    for turn, (step, members) in enumerate(rounds):
-        low = (1 - 2 * ((dom // step) % 2)) * step
-        high = (1 - 2 * ((dom // (2 * step)) % 2)) * 2 * step
-        group = [(field, dom + (e % 2) * low + (e // 2) * high) for e in range(members)]
-        across = [(1 - field, there) for _, there in group] if turn == 0 else []
-        groups.append(group[1:] + across)
+    groups = neighbours(rounds, field, dom)
     clear_ends(window, nbr)
     peers = [peer for group in groups for peer in group]
     greet(peers)
@@ -442,7 +425,10 @@
         jnp.sum(squares, axis=1, keepdims=True),
         jnp.where(lane == 1, jnp.sum(products, axis=1, keepdims=True), 0.0),
     )
+    total = jnp.concatenate([total, jnp.zeros((LANES - columns, LANES), jnp.float32)], axis=0).T[:SUB]
+    gram[...] = jnp.zeros_like(gram)
     meet(dom, ends, len(peers))
+    pieces = wide // SPAN
     for turn, group in enumerate(groups):
         held[turn] = total
         copies = [
@@ -451,17 +437,19 @@
         ]
         for copy in copies:
             copy.start()
+        gram_over(
+            pieces * turn // len(groups),
+            pieces * (turn + 1) // len(groups),
+            SPAN,
+            lambda span: jnp.concatenate([x_ref[:, span], p_ref[:, span]], axis=0),
+            lambda span: jnp.concatenate([x_ref[:, span], p_ref[:, span], image[:, span]], axis=0),
+            gram,
+        )
         for copy in copies:
             copy.wait()
-
-        def four(parts):
-            return (parts[0] + parts[1]) + (parts[2] + parts[3]) if len(parts) == 4 else parts[0] + parts[1]
-
         members = rounds[turn][1]
-        parts = [total] + [landed[turn, e] for e in range(len(group))]
-        total = four(parts[:members])
-        if len(parts) > members:
-            total = total + four(parts[members:])
+        total = gathered(total, [landed[turn, e] for e in range(len(group))], members)
+    total = jnp.concatenate([total, jnp.zeros((LANES - SUB, LANES), jnp.float32)], axis=0).T[:columns]
     quotient = total[:, 1:2] / total[:, 0:1]
     extra = jnp.zeros((deep - columns, BS), jnp.float32)
 
@@ -475,19 +463,19 @@
     lax.fori_loop(0, nbr, fill, 0, unroll=2)
     halos = halo_copies(window, nbr, (end_send, end_recv), field, dom)
     start_halos(halos, dom, ends)
-    copy = send_wet(
+    copies = send_wet(
         lambda span: r_ref[:, span], columns, wide, rows, counts[0], coupling, rows_in, picked, outgoing, wet,
         (side_send, side_recv), (1 - field, dom),
     )
     finish_halos(halos, dom, ends)
-    copy.wait()
-
-
-def exchange_second(vec_modes, image, jacobi, wet_rows, wet_counts, coupling):
+    for copy in copies:
+        copy.wait()
+
+
+def exchange_second(vec_modes, vec_prev, image, jacobi, wet_rows, wet_counts, coupling):
     columns, wide = vec_modes.shape
     slots = wet_rows.shape[1]
-    bits = (lax.axis_size("dom") - 1).bit_length()
-    rounds = [(1 << bit, 4 if bit + 1 < bits else 2) for bit in range(0, bits, 2)]
+    rounds = sum_rounds()
     most = 2 * rounds[0][1] - 1
     return pl.pallas_call(
         functools.partial(second_kernel, rounds),
@@ -495,36 +483,158 @@
             jax.ShapeDtypeStruct((wide // BS + 5, rows_deep(columns), BS), jnp.bfloat16),
             jax.ShapeDtypeStruct((slots, LANES), jnp.bfloat16),
             jax.ShapeDtypeStruct((columns, wide), jnp.float32),
-        ),
-        in_specs=[SMEM, SMEM, VMEM, VMEM, VMEM, VMEM],
-        out_specs=(VMEM, VMEM, VMEM),
+            jax.ShapeDtypeStruct((2 * columns, 4 * columns), jnp.float32),
+        ),
+        in_specs=[SMEM, SMEM, VMEM, VMEM, VMEM, VMEM, VMEM],
+        out_specs=(VMEM,) * 4,
         scratch_shapes=exchange_scratch(wide, slots)
         + [
-            pltpu.VMEM((len(rounds), columns, LANES), jnp.float32),
-            pltpu.VMEM((len(rounds), most, columns, LANES), jnp.float32),
+            pltpu.VMEM((len(rounds), SUB, LANES), jnp.float32),
+            pltpu.VMEM((len(rounds), most, SUB, LANES), jnp.float32),
             pltpu.SemaphoreType.DMA((len(rounds), most)),
             pltpu.SemaphoreType.DMA((len(rounds), most)),
         ],
         compiler_params=pltpu.CompilerParams(
-            collective_id=3, has_side_effects=True, vmem_limit_bytes=32 * 1024 * 1024
-        ),
-    )(wet_rows, wet_counts, coupling, vec_modes, image, jacobi)
+            collective_id=3, has_side_effects=True, vmem_limit_bytes=20 * 1024 * 1024
+        ),
+    )(wet_rows, wet_counts, coupling, vec_modes, vec_prev, image, jacobi)
+
+
+def gram_kernel(
+    rounds, x_ref, p_ref, r_ref, image, image_r, known, o_ref,
+    fresh, gram_b, gram_a, packed, held, landed, across, send_sem, recv_sem, side_send, side_recv,
+):
+    field = lax.axis_index("field")
+    dom = lax.axis_index("dom")
+    columns, wide = x_ref.shape
+    groups = []
+    for step, members in rounds:
+        low = (1 - 2 * ((dom // step) % 2)) * step
+        high = (1 - 2 * ((dom // (2 * step)) % 2)) * 2 * step
+        groups.append([dom + (e % 2) * low + (e // 2) * high for e in range(1, members)])
+    peers = [(1 - field, dom)] + [(field, peer) for group in groups for peer in group]
+    greet(peers)
+    fresh[...] = jnp.zeros_like(fresh)
+    gram_over(
+        0,
+        wide // SPAN,
+        SPAN,
+        lambda span: jnp.concatenate([r_ref[:, span], image_r[:, span]], axis=0),
+        lambda span: jnp.concatenate(
+            [x_ref[:, span], p_ref[:, span], r_ref[:, span], image[:, span], image_r[:, span]], axis=0
+        ),
+        fresh,
+    )
+    n = columns
+    new = fresh[...]
+    old = known[...]
+    turned = jnp.concatenate(
+        [new[:, : 2 * n], jnp.zeros((2 * n, LANES - 2 * n), jnp.float32)], axis=1
+    )
+    turned = jnp.concatenate([turned, jnp.zeros((LANES - 2 * n, LANES), jnp.float32)], axis=0).T
+    gram_b[...] = jnp.zeros_like(gram_b)
+    gram_a[...] = jnp.zeros_like(gram_a)
+    x, r, p = slice(0, n), slice(n, 2 * n), slice(2 * n, 3 * n)
+    gram_b[x, x] = old[:n, :n]
+    gram_b[r, x] = new[:n, :n]
+    gram_b[r, r] = new[:n, 2 * n : 3 * n]
+    gram_b[p, x] = old[n:, :n]
+    gram_b[p, r] = turned[n : 2 * n, :n]
+    gram_b[p, p] = old[n:, n : 2 * n]
+    gram_a[x, x] = old[:n, 2 * n : 3 * n]
+    gram_a[x, r] = turned[:n, n : 2 * n]
+    gram_a[x, p] = old[:n, 3 * n :]
+    gram_a[r, x] = new[:n, 3 * n : 4 * n]
+    gram_a[r, r] = new[:n, 5 * n :]
+    gram_a[r, p] = new[:n, 4 * n : 5 * n]
+    gram_a[p, x] = old[n:, 2 * n : 3 * n]
+    gram_a[p, r] = turned[n : 2 * n, n : 2 * n]
+    gram_a[p, p] = old[n:, 3 * n :]
+    both = gram_a[...] + gram_a[...].T
+    both = jnp.concatenate([both[:, LANES - 1 :], both[:, : LANES - 1]], axis=1)
+    row = lax.broadcasted_iota(jnp.int32, (LANES, LANES), 0)
+    col = lax.broadcasted_iota(jnp.int32, (LANES, LANES), 1)
+    half = LANES // 2
+    whole = jnp.where(col <= row, gram_b[...], both)
+    packed[0] = whole[:half]
+    packed[1] = whole[half:]
+    pl.semaphore_wait(pltpu.get_barrier_semaphore(), len(peers))
+    copy = remote(packed.at[1 - field], across.at[0], (side_send.at[0], side_recv.at[0]), (1 - field, dom))
+    copy.start()
+    copy.wait()
+    total = packed[field] + across[0]
+    for turn, group in enumerate(groups):
+        held[turn] = total
+        copies = [
+            remote(
+                held.at[turn], landed.at[turn, e], (send_sem.at[turn, e], recv_sem.at[turn, e]), (field, peer)
+            )
+            for e, peer in enumerate(group)
+        ]
+        for copy in copies:
+            copy.start()
+        for copy in copies:
+            copy.wait()
+        total = gathered(total, [landed[turn, e] for e in range(len(group))], rounds[turn][1])
+    o_ref[field] = total
+    held[len(groups)] = total
+    copy = remote(held.at[len(groups)], across.at[1], (side_send.at[1], side_recv.at[1]), (1 - field, dom))
+    copy.start()
+    copy.wait()
+    o_ref[1 - field] = across[1]
+
+
+def gram_everywhere(vec_modes, vec_prev, residual_dir, image, image_r, known):
+    columns = vec_modes.shape[0]
+    rounds = sum_rounds()
+    slots = len(rounds)
+    cell = (LANES // 2, LANES)
+    return pl.pallas_call(
+        functools.partial(gram_kernel, rounds),
+        out_shape=jax.ShapeDtypeStruct((2,) + cell, jnp.float32),
+        in_specs=[VMEM] * 6,
+        out_specs=VMEM,
+        scratch_shapes=[
+            pltpu.VMEM((2 * columns, 6 * columns), jnp.float32),
+            pltpu.VMEM((LANES, LANES), jnp.float32),
+            pltpu.VMEM((LANES, LANES), jnp.float32),
+            pltpu.VMEM((2,) + cell, jnp.float32),
+            pltpu.VMEM((slots + 1,) + cell, jnp.float32),
+            pltpu.VMEM((slots, 3) + cell, jnp.float32),
+            pltpu.VMEM((2,) + cell, jnp.float32),
+            pltpu.SemaphoreType.DMA((slots, 3)),
+            pltpu.SemaphoreType.DMA((slots, 3)),
+            pltpu.SemaphoreType.DMA((2,)),
+            pltpu.SemaphoreType.DMA((2,)),
+        ],
+        compiler_params=pltpu.CompilerParams(
+            collective_id=2, has_side_effects=True, vmem_limit_bytes=16 * 1024 * 1024
+        ),
+    )(vec_modes, vec_prev, residual_dir, image, image_r, known)
 
 
 def group_rows(kind_of, lists, nbr, types, cells):
     spare = nbr + 2
+    bits = 32 // types
+    mask = (1 << bits) - 1
     for offset in range(3):
-        for slot in range((cells + 1) * GROUP):
+        for slot in range(cells * GROUP):
             lists[offset, slot] = spare
-        known = [kind_of(offset, row) for row in range(2 - offset, nbr + 2)]
+        first = 2 - offset
+        shifts = [kind_of(offset, row) * bits for row in range(first, nbr + 2)]
+        count = jnp.int32(0)
+        ranks = []
+        for shift in shifts:
+            ranks.append(lax.shift_right_logical(count, shift) & mask)
+            count = count + lax.shift_left(jnp.int32(1), shift)
+        starts = jnp.int32(0)
         place = jnp.int32(0)
         for kind in range(types):
-            for row, found in enumerate(known):
-                lists[offset, place] = row + 2 - offset
-                place = place + (found == kind).astype(jnp.int32)
-            for slot in range(GROUP):
-                lists[offset, place + slot] = spare
-            place = ((place + (GROUP - 1)) // GROUP) * GROUP
+            starts = starts + place * (1 << bits * kind)
+            here = lax.shift_right_logical(count, jnp.int32(bits * kind)) & mask
+            place = place + ((here + (GROUP - 1)) & -GROUP)
+        for n, (shift, rank) in enumerate(zip(shifts, ranks)):
+            lists[offset, (lax.shift_right_logical(starts, shift) & mask) + rank] = n + first
 
 
 def operator_kernel(cells, with_diagonal, kinds, scales, rows, window, wet, tables, o_ref, *rest):
@@ -630,7 +740,7 @@
         pltpu.VMEM((nbr + 1, deep, BS), jnp.float32),
         pltpu.VMEM((slots, LANES), jnp.float32),
         pltpu.VMEM((wide, LANES), jnp.float32),
-        pltpu.SMEM((3, (cells + 1) * GROUP), jnp.int32),
+        pltpu.SMEM((3, cells * GROUP), jnp.int32),
     ]
     if with_diagonal:
         outs.append(jax.ShapeDtypeStruct((1, wide), jnp.float32))
@@ -644,40 +754,24 @@
         cost_estimate=pl.CostEstimate(
             flops=10 * columns * wide * BS, bytes_accessed=16 * columns * wide, transcendentals=0
         ),
-        compiler_params=pltpu.CompilerParams(vmem_limit_bytes=32 * 1024 * 1024),
+        compiler_params=pltpu.CompilerParams(vmem_limit_bytes=24 * 1024 * 1024),
     )(kinds, scales, rows, window, wet, tables)
 
 
 def shards(modes, previous, kinds, scales, tables, wet_rows, wet_counts, coupling):
-    high = lax.Precision.HIGH
-    vec_modes = modes[0]
-    vec_prev = previous[0]
-    columns, wide = vec_modes.shape
-    shared = (kinds[0], scales[0], wet_rows, tables[0])
-    weights = coupling.reshape(-1, LANES)
-    window, wet = exchange_first(vec_modes, vec_prev, wet_rows, wet_counts, weights)
-    image_pair, jacobi = operate(2 * columns, window, wet, *shared, True)
-    image_x, image_p = image_pair[:columns], image_pair[columns:]
-    window, wet, residual_dir = exchange_second(vec_modes, image_pair, jacobi, wet_rows, wet_counts, weights)
+    _, columns, wide = modes.shape
+    window, wet, vec_modes, vec_prev, field_tables, weights = exchange_first(
+        modes, previous, wet_rows, wet_counts, coupling.reshape(-1, LANES), tables
+    )
+    shared = (kinds[0], scales[0], wet_rows, field_tables)
+    image, jacobi = operate(2 * columns, window, wet, *shared, True)
+    window, wet, residual_dir, known = exchange_second(
+        vec_modes, vec_prev, image, jacobi, wet_rows, wet_counts, weights
+    )
     (image_r,) = operate(columns, window, wet, *shared, False)
-    search = jnp.concatenate([vec_modes, residual_dir, vec_prev], axis=0)
-    image_all = jnp.concatenate([image_x, image_r, image_p], axis=0)
+    packed = gram_everywhere(vec_modes, vec_prev, residual_dir, image, image_r, known)
     ndof = 2.0 * lax.axis_size("dom") * wide
-    part_b = jnp.dot(search, search.T, precision=high)
-    part_a = jnp.dot(search, image_all.T, precision=high)
-    part_a = part_a + part_a.T
-    size = 3 * columns
-    row = lax.broadcasted_iota(jnp.int32, (size, size + 8), 0)
-    col = lax.broadcasted_iota(jnp.int32, (size, size + 8), 1)
-    packed = jnp.where(
-        col <= row,
-        jnp.pad(part_b, ((0, 0), (0, 8))),
-        jnp.pad(part_a, ((0, 0), (1, 7))),
-    )
-    half = -(-size // 16) * 8
-    packed = jnp.pad(packed, ((0, 2 * half - size), (0, 0))).reshape(2, half, size + 8)
-    packed = summed_everywhere(packed, 2).reshape(2 * half, size + 8)
-    return finish(packed, vec_modes, residual_dir, vec_prev, ndof)
+    return finish(packed.reshape(LANES, LANES), vec_modes, residual_dir, vec_prev, ndof)
 
 
 def solution(mesh):

time: 101 us -> 90.3 us (0.89)
  matrix products: 5.4 us -> 0 us
  local copies, waits for them, and re-layouts: 11 us -> 8.2 us
  Pallas kernels: 81.9 us -> 80.4 us
    dot_general x2 -> x0, matrix products: 5.4 us -> none  [the longest x1 3.58 us: shards(): part_b = jnp.dot(search, search.T, precision=high)]
    unnamed x32 -> x12, local copies, waits for them, and re-layouts: 10.1 us -> 8.2 us
    pallas_call x1, Pallas kernels: 21.9 us -> 20.3 us  [exchange_second(): pl.pallas_call(functools.partial(second_kernel, rounds), out_shape=(jax.S...]
where the time goes in v3:
time: 90.3 us; the launch traced here: 90 us
  Pallas kernels  80.4 us (89%)
  local copies, waits for them, and re-layouts  8.2 us (9%)
  between operations  1.32 us (1%)
    pallas_call x2, Pallas kernels, operate(): pl.pallas_call(functools.partial(operator_kernel, cells, with_diagonal),...  25.4 us
    pallas_call x1, Pallas kernels, exchange_second(): pl.pallas_call(functools.partial(second_kernel, rounds), out_shape=(jax.S...  20.3 us
    pallas_call x1, Pallas kernels, gram_everywhere(): pl.pallas_call(functools.partial(gram_kernel, rounds), out_shape=jax.Shap...  14.3 us
    pallas_call x1, Pallas kernels, exchange_first(): pl.pallas_call(first_kernel, out_shape=(jax.ShapeDtypeStruct((wide // BS...  10.7 us
    pallas_call x1, Pallas kernels, finish(): pl.pallas_call(functools.partial(finish_kernel, chunk, 1.0 / ndof), out_s...  9.72 us
    unnamed x12, local copies, waits for them, and re-layouts  8.2 us

profile of v3, /device:TPU:0, one launch (start us, length us, event | category | flops | bytes accessed | tf_op | source)
XLA Modules:
  0.0 90.0 jit_solution(6988537793710184307)
XLA Ops:
  1.3 0.7 copy.15
  2.0 0.7 copy.14
  2.6 0.0 copy-start
  2.7 2.8 %copy-done = bf16[1,3,4,512,512]{4,3,2,1,0:T(8,128)(2,1)S(1)} copy-done((bf16[1,3,4,512,512]{4,3,2,1,0:T(8,128)(2,1)S(1)}, bf16[1,3,4,512,512]{4,3,2,1,0:T(8,128)(2,1)}, u32[]{:S(2)}) %copy-start) | copy-done | bytes 6291480
  5.4 0.0 copy-start.1
  5.4 1.3 %copy-done.1 = f32[1,40,8192]{2,1,0:T(8,128)S(1)} copy-done((f32[1,40,8192]{2,1,0:T(8,128)S(1)}, f32[1,40,8192]{2,1,0:T(8,128)}, u32[]{:S(2)}) %copy-start.1) | copy-done | bytes 1310744
  6.8 0.0 copy-start.2
  6.8 1.3 %copy-done.2 = f32[1,40,8192]{2,1,0:T(8,128)S(1)} copy-done((f32[1,40,8192]{2,1,0:T(8,128)S(1)}, f32[1,40,8192]{2,1,0:T(8,128)}, u32[]{:S(2)}) %copy-start.2) | copy-done | bytes 1310744
  8.1 0.0 copy-start.3
  8.1 0.7 copy-done.3
  8.8 0.0 copy-start.4
  8.8 0.7 copy-done.4
  9.5 10.7 %shard_map.95 = (bf16[21,80,512]{2,1,0:T(8,128)(2,1)S(1)}, bf16[3072,128]{1,0:T(8,128)(2,1)S(1)}, f32[40,8192]{1,0:T(8,128)S(1)}, f32[40,8192]{1,0:T(8,128)S(1)}...) custom-call(s32[1]{0:T(128)S(6)} %copy.16.counts, s32[1,3072]{1,0:T(1,128)S(1)} %copy-done.3, ...), custom_call_target="tpu_custom_call" | custom-call | tf_op jit(solution)/shard_map/pallas_call | solution.py:330
  20.2 13.6 %shard_map.96 = (f32[80,8192]{1,0:T(8,128)S(1)}, f32[1,8192]{1,0:T(1,128)S(1)}) custom-call(s32[3,256]{1,0:T(4,128)S(1)} %bitcast.9, f32[3,256]{1,0:T(4,128)S(1)} %bitcast.11, s32[1,3072]{1,0:T(1,128)S(1)} %copy-done.3, bf16[21,80,512]{2,1,0:T(8,128)(2,1)S(1)} %get-tuple-element.17.window, bf16[3072,128]{1,0:T(8,128)(2,1)S(1)} %get-tuple-element.18.wet, ...), custom_call_target="tpu_custom_call" | custom-call | flops 3355443200 | bytes 10485760 | tf_op jit(solution)/shard_map/pallas_call | solution.py:748
  33.8 20.3 %shard_map.97 = (bf16[21,48,512]{2,1,0:T(8,128)(2,1)S(1)}, bf16[3072,128]{1,0:T(8,128)(2,1)S(1)}, f32[40,8192]{1,0:T(8,128)S(1)}, f32[80,160]{1,0:T(8,128)S(1)}) custom-call(s32[1,3072]{1,0:T(1,128)S(1)} %copy-done.3, s32[1]{0:T(128)S(6)} %copy.16.counts, f32[24,128]{1,0:T(8,128)S(1)} %get-tuple-element.16.coupling, f32[40,8192]{1,0:T(8,128)S(1)} %get-tuple-element.14.x_ref, ...), custom_call_target="tpu_custom_call" | custom-call | tf_op jit(solution)/shard_map/pallas_call | solution.py:480
  54.1 11.8 %shard_map.98.image_r = f32[40,8192]{1,0:T(8,128)S(1)} custom-call(s32[3,256]{1,0:T(4,128)S(1)} %bitcast.10, f32[3,256]{1,0:T(4,128)S(1)} %bitcast.12, s32[1,3072]{1,0:T(1,128)S(1)} %copy-done.3, bf16[21,48,512]{2,1,0:T(8,128)(2,1)S(1)} %get-tuple-element.23.window, bf16[3072,128]{1,0:T(8,128)(2,1)S(1)} %get-tuple-element.24.wet, ...), custom_call_target="tpu_custom_call" | custom-call | flops 1677721600 | bytes 5242880 | tf_op jit(solution)/shard_map/pallas_call | solution.py:748
  66.0 14.3 %shard_map.99 = f32[2,64,128]{2,1,0:T(8,128)S(1)} custom-call(f32[40,8192]{1,0:T(8,128)S(1)} %get-tuple-element.14.x_ref, f32[40,8192]{1,0:T(8,128)S(1)} %get-tuple-element.15.p_ref, f32[40,8192]{1,0:T(8,128)S(1)} %get-tuple-element.22.r_ref, f32[80,8192]{1,0:T(8,128)S(1)} %get-tuple-element.20.image, f32[40,8192]{1,0:T(8,128)S(1)} %shard_map.98.image_r, ...), custom_call_target="tpu_custom_call" | custom-call | tf_op jit(solution)/shard_map/pallas_call | solution.py:592
  80.2 9.7 %shard_map.100 = (f32[1,120,8192]{2,1,0:T(8,128)}, f32[120,120]{1,0:T(8,128)}) custom-call(f32[128,128]{1,0:T(8,128)S(1)} %bitcast.8, f32[40,8192]{1,0:T(8,128)S(1)} %get-tuple-element.14.x_ref, f32[40,8192]{1,0:T(8,128)S(1)} %get-tuple-element.22.r_ref, f32[40,8192]{1,0:T(8,128)S(1)} %get-tuple-element.15.p_ref), custom_call_target="tpu_custom_call" | custom-call | flops 707788800 | bytes 7864320 | tf_op jit(solution)/shard_map/pallas_call | solution.py:125
Async XLA Ops:
  2.6 2.8 %copy-start = (bf16[1,3,4,512,512]{4,3,2,1,0:T(8,128)(2,1)S(1)}, bf16[1,3,4,512,512]{4,3,2,1,0:T(8,128)(2,1)}, u32[]{:S(2)}) copy-start(bf16[1,3,4,512,512]{4,3,2,1,0:T(8,128)(2,1)} %tables_in.1) | copy-start | bytes 18874372
  5.4 1.3 %copy-start.1 = (f32[1,40,8192]{2,1,0:T(8,128)S(1)}, f32[1,40,8192]{2,1,0:T(8,128)}, u32[]{:S(2)}) copy-start(f32[1,40,8192]{2,1,0:T(8,128)} %x_in.1) | copy-start | bytes 3932164
  6.8 1.3 %copy-start.2 = (f32[1,40,8192]{2,1,0:T(8,128)S(1)}, f32[1,40,8192]{2,1,0:T(8,128)}, u32[]{:S(2)}) copy-start(f32[1,40,8192]{2,1,0:T(8,128)} %p_in.1) | copy-start | bytes 3932164
  8.1 0.7 copy-start.3
  8.8 0.7 copy-start.4

commit v4 on v3

--- a/solution.py
+++ b/solution.py
@@ -51,8 +51,9 @@
         cells = [left[k], right[k]]
         for c in range(SUB):
             pivot = over_rows(columns[c], c)
-            inverse = 1.0 / pivot
-            inverse_ref[SUB * k + c : SUB * k + c + 1] = (cells[1] * lax.rsqrt(pivot))[c : c + 1]
+            root = lax.rsqrt(pivot)
+            inverse = root * root
+            inverse_ref[SUB * k + c : SUB * k + c + 1] = (cells[1] * root)[c : c + 1]
             here = sub == c
             factor = columns[c]
 
@@ -108,7 +109,7 @@
         copy(n).start()
         return carry
 
-    lax.fori_loop(0, wide // chunk, step, 0)
+    lax.fori_loop(0, wide // chunk, step, 0, unroll=2)
 
     def close(n, carry):
         copy(n).wait()
@@ -220,7 +221,7 @@
         left.wait_recv()
 
 
-def send_wet(read, columns, wide, rows, count, coupling, rows_in, picked, outgoing, wet, sems, peer):
+def pick_rows(read, columns, wide, rows, rows_in, picked):
     slots = picked.shape[0]
     blank = jnp.zeros((LANES - columns, LANES), jnp.float32)
 
@@ -238,13 +239,17 @@
         return carry
 
     lax.fori_loop(0, slots // UNROLL, gather, 0)
+
+
+def send_wet(combine, count, coupling, picked, outgoing, wet, sems, peer):
+    slots = picked.shape[0]
 
     def weigh(i, carry):
         span = pl.ds(pl.multiple_of(i * LANES, LANES), LANES)
         used = i * LANES + lax.broadcasted_iota(jnp.int32, (1, LANES), 1) < count
         weights = jnp.where(used, coupling[pl.ds(i, 1), :], 0.0)
         spread = jnp.broadcast_to(weights, (LANES, LANES)).T
-        outgoing[span, :] = (picked[span, :] * spread).astype(jnp.bfloat16)
+        outgoing[span, :] = (combine(picked[span, :]) * spread).astype(jnp.bfloat16)
         return carry
 
     cells = slots // LANES
@@ -292,9 +297,9 @@
     start_halos(halos, dom, ends)
     arrivals[2].wait()
     arrivals[3].wait()
+    pick_rows(read, 2 * columns, wide, rows, rows_in, picked)
     copies = send_wet(
-        read, 2 * columns, wide, rows, counts[0], coupling, rows_in, picked, outgoing, wet,
-        (side_send, side_recv), (1 - field, dom),
+        lambda cell: cell, counts[0], coupling, picked, outgoing, wet, (side_send, side_recv), (1 - field, dom)
     )
     arrivals[4].wait()
     finish_halos(halos, dom, ends)
@@ -347,26 +352,27 @@
     )(wet_counts, wet_rows, coupling, modes, previous, tables)
 
 
-def gram_part(left, right):
-    lh = left.astype(jnp.bfloat16)
-    ll = (left - lh.astype(jnp.float32)).astype(jnp.bfloat16)
-    rh = right.astype(jnp.bfloat16)
-    rl = (right - rh.astype(jnp.float32)).astype(jnp.bfloat16)
-    rows = left.shape[0]
-    both = lax.dot_general(
-        jnp.concatenate([lh, ll], axis=0), rh, NT, preferred_element_type=jnp.float32
-    )
-    cross = lax.dot_general(lh, rl, NT, preferred_element_type=jnp.float32)
-    return both[:rows] + (both[rows:] + cross)
-
-
-def gram_over(low, high, step, read_left, read_right, out):
+def gram_over(wide, read, count, out):
+    out[...] = jnp.zeros_like(out)
+
     def add(n, carry):
-        span = pl.ds(pl.multiple_of(n * step, step), step)
-        out[...] += gram_part(read_left(span), read_right(span))
-        return carry
-
-    lax.fori_loop(low, high, add, 0)
+        span = pl.ds(pl.multiple_of(n * SPAN, SPAN), SPAN)
+        left, right = read(span)
+        rh = right.astype(jnp.bfloat16)
+        rl = (right - rh.astype(jnp.float32)).astype(jnp.bfloat16)
+        if left is None:
+            lh, ll = rh[:count], rl[:count]
+        else:
+            lh = left.astype(jnp.bfloat16)
+            ll = (left - lh.astype(jnp.float32)).astype(jnp.bfloat16)
+        both = lax.dot_general(
+            jnp.concatenate([lh, ll], axis=0), rh, NT, preferred_element_type=jnp.float32
+        )
+        cross = lax.dot_general(lh, rl, NT, preferred_element_type=jnp.float32)
+        out[...] += both[:count] + (both[count:] + cross)
+        return carry
+
+    lax.fori_loop(0, wide // SPAN, add, 0)
 
 
 def neighbours(rounds, field, dom):
@@ -397,8 +403,9 @@
 
 
 def second_kernel(
-    rounds, rows, counts, coupling, x_ref, p_ref, image, jacobi, window, wet, r_ref, gram,
-    rows_in, picked, outgoing, side_send, side_recv, end_send, end_recv, held, landed, sum_send, sum_recv,
+    rounds, counts, rows_hbm, coupling, x_ref, p_ref, image, jacobi, window, wet, r_ref, gram,
+    rows_in, picked, outgoing, side_send, side_recv, end_send, end_recv,
+    rows, loads, held, landed, sum_send, sum_recv,
 ):
     field = lax.axis_index("field")
     dom = lax.axis_index("dom")
@@ -406,6 +413,8 @@
     columns, wide = x_ref.shape
     nbr = wide // BS
     deep = window.shape[1]
+    arrival = pltpu.make_async_copy(rows_hbm, rows, loads.at[0])
+    arrival.start()
     groups = neighbours(rounds, field, dom)
     clear_ends(window, nbr)
     peers = [peer for group in groups for peer in group]
@@ -426,9 +435,8 @@
         jnp.where(lane == 1, jnp.sum(products, axis=1, keepdims=True), 0.0),
     )
     total = jnp.concatenate([total, jnp.zeros((LANES - columns, LANES), jnp.float32)], axis=0).T[:SUB]
-    gram[...] = jnp.zeros_like(gram)
+    arrival.wait()
     meet(dom, ends, len(peers))
-    pieces = wide // SPAN
     for turn, group in enumerate(groups):
         held[turn] = total
         copies = [
@@ -437,18 +445,19 @@
         ]
         for copy in copies:
             copy.start()
-        gram_over(
-            pieces * turn // len(groups),
-            pieces * (turn + 1) // len(groups),
-            SPAN,
-            lambda span: jnp.concatenate([x_ref[:, span], p_ref[:, span]], axis=0),
-            lambda span: jnp.concatenate([x_ref[:, span], p_ref[:, span], image[:, span]], axis=0),
-            gram,
-        )
+        if turn == 0:
+            pick_rows(
+                lambda span: jnp.concatenate(
+                    [image[:columns, span] / jacobi[:, span], x_ref[:, span] / jacobi[:, span]], axis=0
+                ),
+                2 * columns, wide, rows, rows_in, picked,
+            )
         for copy in copies:
             copy.wait()
         members = rounds[turn][1]
         total = gathered(total, [landed[turn, e] for e in range(len(group))], members)
+    lane = lax.broadcasted_iota(jnp.int32, (1, LANES), 1)
+    across = jnp.where(lane < columns, total[1:2] / total[0:1], 0.0)
     total = jnp.concatenate([total, jnp.zeros((LANES - SUB, LANES), jnp.float32)], axis=0).T[:columns]
     quotient = total[:, 1:2] / total[:, 0:1]
     extra = jnp.zeros((deep - columns, BS), jnp.float32)
@@ -460,12 +469,24 @@
         window[n + 2] = jnp.concatenate([r, extra], axis=0).astype(jnp.bfloat16)
         return carry
 
-    lax.fori_loop(0, nbr, fill, 0, unroll=2)
+    for n in (0, 1, nbr - 2, nbr - 1):
+        fill(n, 0)
     halos = halo_copies(window, nbr, (end_send, end_recv), field, dom)
     start_halos(halos, dom, ends)
     copies = send_wet(
-        lambda span: r_ref[:, span], columns, wide, rows, counts[0], coupling, rows_in, picked, outgoing, wet,
-        (side_send, side_recv), (1 - field, dom),
+        lambda cell: cell - pltpu.roll(cell, LANES - columns, 1) * across,
+        counts[0], coupling, picked, outgoing, wet, (side_send, side_recv), (1 - field, dom),
+    )
+    lax.fori_loop(2, nbr - 2, fill, 0)
+    spare = jnp.zeros((gram.shape[1] - 5 * columns, SPAN), jnp.float32)
+    gram_over(
+        wide,
+        lambda span: (
+            None,
+            jnp.concatenate([x_ref[:, span], p_ref[:, span], r_ref[:, span], image[:, span], spare], axis=0),
+        ),
+        gram.shape[0],
+        gram,
     )
     finish_halos(halos, dom, ends)
     for copy in copies:
@@ -483,12 +504,14 @@
             jax.ShapeDtypeStruct((wide // BS + 5, rows_deep(columns), BS), jnp.bfloat16),
             jax.ShapeDtypeStruct((slots, LANES), jnp.bfloat16),
             jax.ShapeDtypeStruct((columns, wide), jnp.float32),
-            jax.ShapeDtypeStruct((2 * columns, 4 * columns), jnp.float32),
-        ),
-        in_specs=[SMEM, SMEM, VMEM, VMEM, VMEM, VMEM, VMEM],
+            jax.ShapeDtypeStruct((LANES, rows_deep(5 * columns)), jnp.float32),
+        ),
+        in_specs=[SMEM, HBM, VMEM, VMEM, VMEM, VMEM, VMEM],
         out_specs=(VMEM,) * 4,
         scratch_shapes=exchange_scratch(wide, slots)
         + [
+            pltpu.SMEM(wet_rows.shape, jnp.int32),
+            pltpu.SemaphoreType.DMA((1,)),
             pltpu.VMEM((len(rounds), SUB, LANES), jnp.float32),
             pltpu.VMEM((len(rounds), most, SUB, LANES), jnp.float32),
             pltpu.SemaphoreType.DMA((len(rounds), most)),
@@ -497,11 +520,11 @@
         compiler_params=pltpu.CompilerParams(
             collective_id=3, has_side_effects=True, vmem_limit_bytes=20 * 1024 * 1024
         ),
-    )(wet_rows, wet_counts, coupling, vec_modes, vec_prev, image, jacobi)
+    )(wet_counts, wet_rows, coupling, vec_modes, vec_prev, image, jacobi)
 
 
 def gram_kernel(
-    rounds, x_ref, p_ref, r_ref, image, image_r, known, o_ref,
+    rounds, x_ref, p_ref, r_ref, image_r, known, o_ref,
     fresh, gram_b, gram_a, packed, held, landed, across, send_sem, recv_sem, side_send, side_recv,
 ):
     field = lax.axis_index("field")
@@ -514,42 +537,35 @@
         groups.append([dom + (e % 2) * low + (e // 2) * high for e in range(1, members)])
     peers = [(1 - field, dom)] + [(field, peer) for group in groups for peer in group]
     greet(peers)
-    fresh[...] = jnp.zeros_like(fresh)
+    n = columns
+    low = jnp.zeros((fresh.shape[0] - n, SPAN), jnp.float32)
+    spare = jnp.zeros((LANES - 3 * n, SPAN), jnp.float32)
     gram_over(
-        0,
-        wide // SPAN,
-        SPAN,
-        lambda span: jnp.concatenate([r_ref[:, span], image_r[:, span]], axis=0),
-        lambda span: jnp.concatenate(
-            [x_ref[:, span], p_ref[:, span], r_ref[:, span], image[:, span], image_r[:, span]], axis=0
-        ),
+        wide,
+        lambda span: (
+            jnp.concatenate([image_r[:, span], low], axis=0),
+            jnp.concatenate([x_ref[:, span], p_ref[:, span], r_ref[:, span], spare], axis=0),
+        ),
+        fresh.shape[0],
         fresh,
     )
-    n = columns
-    new = fresh[...]
     old = known[...]
     turned = jnp.concatenate(
-        [new[:, : 2 * n], jnp.zeros((2 * n, LANES - 2 * n), jnp.float32)], axis=1
-    )
-    turned = jnp.concatenate([turned, jnp.zeros((LANES - 2 * n, LANES), jnp.float32)], axis=0).T
+        [fresh[...], jnp.zeros((LANES - fresh.shape[0], LANES), jnp.float32)], axis=0
+    ).T
     gram_b[...] = jnp.zeros_like(gram_b)
     gram_a[...] = jnp.zeros_like(gram_a)
     x, r, p = slice(0, n), slice(n, 2 * n), slice(2 * n, 3 * n)
-    gram_b[x, x] = old[:n, :n]
-    gram_b[r, x] = new[:n, :n]
-    gram_b[r, r] = new[:n, 2 * n : 3 * n]
-    gram_b[p, x] = old[n:, :n]
-    gram_b[p, r] = turned[n : 2 * n, :n]
-    gram_b[p, p] = old[n:, n : 2 * n]
-    gram_a[x, x] = old[:n, 2 * n : 3 * n]
-    gram_a[x, r] = turned[:n, n : 2 * n]
-    gram_a[x, p] = old[:n, 3 * n :]
-    gram_a[r, x] = new[:n, 3 * n : 4 * n]
-    gram_a[r, r] = new[:n, 5 * n :]
-    gram_a[r, p] = new[:n, 4 * n : 5 * n]
-    gram_a[p, x] = old[n:, 2 * n : 3 * n]
-    gram_a[p, r] = turned[n : 2 * n, n : 2 * n]
-    gram_a[p, p] = old[n:, 3 * n :]
+    kx, kp, kr = slice(0, n), slice(n, 2 * n), slice(2 * n, 3 * n)
+    ax, ap = slice(3 * n, 4 * n), slice(4 * n, 5 * n)
+    for rows, here in ((x, kx), (r, kr), (p, kp)):
+        gram_a[rows, x] = old[here, ax]
+        gram_a[rows, r] = turned[here, :n]
+        gram_a[rows, p] = old[here, ap]
+    for rows, here, cols, there in (
+        (x, kx, x, kx), (r, kr, x, kx), (r, kr, r, kr), (p, kp, x, kx), (p, kp, r, kr), (p, kp, p, kp),
+    ):
+        gram_b[rows, cols] = old[here, there]
     both = gram_a[...] + gram_a[...].T
     both = jnp.concatenate([both[:, LANES - 1 :], both[:, : LANES - 1]], axis=1)
     row = lax.broadcasted_iota(jnp.int32, (LANES, LANES), 0)
@@ -584,7 +600,7 @@
     o_ref[1 - field] = across[1]
 
 
-def gram_everywhere(vec_modes, vec_prev, residual_dir, image, image_r, known):
+def gram_everywhere(vec_modes, vec_prev, residual_dir, image_r, known):
     columns = vec_modes.shape[0]
     rounds = sum_rounds()
     slots = len(rounds)
@@ -592,10 +608,10 @@
     return pl.pallas_call(
         functools.partial(gram_kernel, rounds),
         out_shape=jax.ShapeDtypeStruct((2,) + cell, jnp.float32),
-        in_specs=[VMEM] * 6,
+        in_specs=[VMEM] * 5,
         out_specs=VMEM,
         scratch_shapes=[
-            pltpu.VMEM((2 * columns, 6 * columns), jnp.float32),
+            pltpu.VMEM((rows_deep(columns), LANES), jnp.float32),
             pltpu.VMEM((LANES, LANES), jnp.float32),
             pltpu.VMEM((LANES, LANES), jnp.float32),
             pltpu.VMEM((2,) + cell, jnp.float32),
@@ -610,7 +626,7 @@
         compiler_params=pltpu.CompilerParams(
             collective_id=2, has_side_effects=True, vmem_limit_bytes=16 * 1024 * 1024
         ),
-    )(vec_modes, vec_prev, residual_dir, image, image_r, known)
+    )(vec_modes, vec_prev, residual_dir, image_r, known)
 
 
 def group_rows(kind_of, lists, nbr, types, cells):
@@ -637,23 +653,26 @@
             lists[offset, (lax.shift_right_logical(starts, shift) & mask) + rank] = n + first
 
 
-def operator_kernel(cells, with_diagonal, kinds, scales, rows, window, wet, tables, o_ref, *rest):
+def operator_kernel(cells, with_diagonal, kinds, scales, rows_hbm, window, wet, tables, o_ref, *rest):
     if with_diagonal:
-        jacobi, diagonal, total, rows_in, rows_out, lists = rest
+        jacobi, diagonal, total, rows_in, rows_out, lists, rows, loads = rest
     else:
-        total, rows_in, rows_out, lists = rest
+        total, rows_in, rows_out, lists, rows, loads = rest
     columns, wide = o_ref.shape
     nbr = wide // BS
     types = tables.shape[1]
     deep = window.shape[1]
     slots = wet.shape[0]
+    arrival = pltpu.make_async_copy(rows_hbm, rows, loads.at[0])
+    arrival.start()
     base = lax.axis_index("dom") * nbr - 2
+    every = kinds.shape[0] // 3
 
     def kind_of(offset, row):
-        return kinds[offset, jnp.maximum(base + row, 0)]
+        return kinds[offset * every + jnp.maximum(base + row, 0)]
 
     def scale_of(offset, row):
-        return scales[offset, jnp.maximum(base + row, 0)]
+        return scales[offset * every + jnp.maximum(base + row, 0)]
 
     group_rows(kind_of, lists, nbr, types, cells)
 
@@ -671,6 +690,7 @@
         return carry
 
     lax.fori_loop(0, slots // LANES, widen, 0, unroll=4)
+    arrival.wait()
 
     def scatter(i, carry):
         for slot in range(UNROLL):
@@ -741,6 +761,8 @@
         pltpu.VMEM((slots, LANES), jnp.float32),
         pltpu.VMEM((wide, LANES), jnp.float32),
         pltpu.SMEM((3, cells * GROUP), jnp.int32),
+        pltpu.SMEM(rows.shape, jnp.int32),
+        pltpu.SemaphoreType.DMA((1,)),
     ]
     if with_diagonal:
         outs.append(jax.ShapeDtypeStruct((1, wide), jnp.float32))
@@ -748,7 +770,7 @@
     return pl.pallas_call(
         functools.partial(operator_kernel, cells, with_diagonal),
         out_shape=tuple(outs),
-        in_specs=[SMEM, SMEM, SMEM, VMEM, VMEM, VMEM],
+        in_specs=[SMEM, SMEM, HBM, VMEM, VMEM, VMEM],
         out_specs=(VMEM,) * len(outs),
         scratch_shapes=scratch,
         cost_estimate=pl.CostEstimate(
@@ -759,17 +781,20 @@
 
 
 def shards(modes, previous, kinds, scales, tables, wet_rows, wet_counts, coupling):
+    modes, previous, tables, wet_rows, coupling = [
+        pltpu.with_memory_space_constraint(a, pltpu.HBM) for a in (modes, previous, tables, wet_rows, coupling.reshape(-1, LANES))
+    ]
     _, columns, wide = modes.shape
     window, wet, vec_modes, vec_prev, field_tables, weights = exchange_first(
-        modes, previous, wet_rows, wet_counts, coupling.reshape(-1, LANES), tables
-    )
-    shared = (kinds[0], scales[0], wet_rows, field_tables)
+        modes, previous, wet_rows, wet_counts, coupling, tables
+    )
+    shared = (kinds.reshape(-1), scales.reshape(-1), wet_rows, field_tables)
     image, jacobi = operate(2 * columns, window, wet, *shared, True)
     window, wet, residual_dir, known = exchange_second(
         vec_modes, vec_prev, image, jacobi, wet_rows, wet_counts, weights
     )
     (image_r,) = operate(columns, window, wet, *shared, False)
-    packed = gram_everywhere(vec_modes, vec_prev, residual_dir, image, image_r, known)
+    packed = gram_everywhere(vec_modes, vec_prev, residual_dir, image_r, known)
     ndof = 2.0 * lax.axis_size("dom") * wide
     return finish(packed.reshape(LANES, LANES), vec_modes, residual_dir, vec_prev, ndof)
 

time: 90.3 us -> 79.3 us (0.88)
  local copies, waits for them, and re-layouts: 8.2 us -> 0.02 us
  Pallas kernels: 80.4 us -> 76.2 us
  other arithmetic: 0 us -> 1.41 us
    unnamed x12 -> x0, local copies, waits for them, and re-layouts: 8.2 us -> none
    pallas_call x1, Pallas kernels: 20.3 us -> 18.8 us  [exchange_second(): pl.pallas_call(functools.partial(second_kernel, rounds), out_shape=(jax.S...]
    unnamed x0 -> x2, other arithmetic: none -> 1.41 us
    pallas_call x1, Pallas kernels: 9.72 us -> 8.72 us  [finish(): pl.pallas_call(functools.partial(finish_kernel, chunk, 1.0 / ndof), out_s...]
    pallas_call x2, Pallas kernels: 25.4 us -> 24.4 us  [operate(): pl.pallas_call(functools.partial(operator_kernel, cells, with_diagonal),...]
where the time goes in v4:
time: 79.3 us; the launch traced here: 78.9 us
  Pallas kernels  76.2 us (96%)
  other arithmetic  1.41 us (2%)
  between operations  1.32 us (2%)
    pallas_call x2, Pallas kernels, operate(): pl.pallas_call(functools.partial(operator_kernel, cells, with_diagonal),...  24.4 us
    pallas_call x1, Pallas kernels, exchange_second(): pl.pallas_call(functools.partial(second_kernel, rounds), out_shape=(jax.S...  18.8 us
    pallas_call x1, Pallas kernels, gram_everywhere(): pl.pallas_call(functools.partial(gram_kernel, rounds), out_shape=jax.Shap...  14 us
    pallas_call x1, Pallas kernels, exchange_first(): pl.pallas_call(first_kernel, out_shape=(jax.ShapeDtypeStruct((wide // BS...  10.2 us
    pallas_call x1, Pallas kernels, finish(): pl.pallas_call(functools.partial(finish_kernel, chunk, 1.0 / ndof), out_s...  8.72 us

profile of v4, /device:TPU:0, one launch (start us, length us, event | category | flops | bytes accessed | tf_op | source)
XLA Modules:
  0.0 78.9 jit_solution(498436401634356412)
XLA Ops:
  1.3 0.7 reduce
  2.0 0.7 reduce.1
  2.7 10.2 %shard_map.95 = (bf16[21,80,512]{2,1,0:T(8,128)(2,1)S(1)}, bf16[3072,128]{1,0:T(8,128)(2,1)S(1)}, f32[40,8192]{1,0:T(8,128)S(1)}, f32[40,8192]{1,0:T(8,128)S(1)}...) custom-call(s32[1]{0:T(128)S(6)} %copy.10.counts, s32[1,3072]{1,0:T(1,128)} %rows_hbm.5, f32[24,128]{1,0:T(8,128)} %bitcast.3, ...), custom_call_target="tpu_custom_call" | custom-call | tf_op jit(solution)/shard_map/pallas_call | solution.py:335
  12.9 12.9 %shard_map.96 = (f32[80,8192]{1,0:T(8,128)S(1)}, f32[1,8192]{1,0:T(1,128)S(1)}) custom-call(s32[768]{0:T(1024)S(1)} %reshape.17.kinds, f32[768]{0:T(1024)S(1)} %reshape.18.scales, s32[1,3072]{1,0:T(1,128)} %rows_hbm.5, bf16[21,80,512]{2,1,0:T(8,128)(2,1)S(1)} %get-tuple-element.17.window, bf16[3072,128]{1,0:T(8,128)(2,1)S(1)} %get-tuple-element.18.wet, ...), custom_call_target="tpu_custom_call" | custom-call | flops 3355443200 | bytes 10485760 | tf_op jit(solution)/shard_map/pallas_call | solution.py:770
  25.8 18.8 %shard_map.97 = (bf16[21,48,512]{2,1,0:T(8,128)(2,1)S(1)}, bf16[3072,128]{1,0:T(8,128)(2,1)S(1)}, f32[40,8192]{1,0:T(8,128)S(1)}, f32[128,208]{1,0:T(8,128)S(1)}) custom-call(s32[1]{0:T(128)S(6)} %copy.10.counts, s32[1,3072]{1,0:T(1,128)} %rows_hbm.5, f32[24,128]{1,0:T(8,128)S(1)} %get-tuple-element.16.coupling, f32[40,8192]{1,0:T(8,128)S(1)} %get-tuple-element.14.x_ref, ...), custom_call_target="tpu_custom_call" | custom-call | tf_op jit(solution)/shard_map/pallas_call | solution.py:501
  44.6 11.6 %shard_map.98.image_r = f32[40,8192]{1,0:T(8,128)S(1)} custom-call(s32[768]{0:T(1024)S(1)} %reshape.17.kinds, f32[768]{0:T(1024)S(1)} %reshape.18.scales, s32[1,3072]{1,0:T(1,128)} %rows_hbm.5, bf16[21,48,512]{2,1,0:T(8,128)(2,1)S(1)} %get-tuple-element.23.window, bf16[3072,128]{1,0:T(8,128)(2,1)S(1)} %get-tuple-element.24.wet, ...), custom_call_target="tpu_custom_call" | custom-call | flops 1677721600 | bytes 5242880 | tf_op jit(solution)/shard_map/pallas_call | solution.py:770
  56.2 14.0 %shard_map.99 = f32[2,64,128]{2,1,0:T(8,128)S(1)} custom-call(f32[40,8192]{1,0:T(8,128)S(1)} %get-tuple-element.14.x_ref, f32[40,8192]{1,0:T(8,128)S(1)} %get-tuple-element.15.p_ref, f32[40,8192]{1,0:T(8,128)S(1)} %get-tuple-element.22.r_ref, f32[40,8192]{1,0:T(8,128)S(1)} %shard_map.98.image_r, f32[128,208]{1,0:T(8,128)S(1)} %get-tuple-element.25.known), custom_call_target="tpu_custom_call" | custom-call | tf_op jit(solution)/shard_map/pallas_call | solution.py:608
  70.2 8.7 %shard_map.100 = (f32[1,120,8192]{2,1,0:T(8,128)}, f32[120,120]{1,0:T(8,128)}) custom-call(f32[128,128]{1,0:T(8,128)S(1)} %bitcast.2, f32[40,8192]{1,0:T(8,128)S(1)} %get-tuple-element.14.x_ref, f32[40,8192]{1,0:T(8,128)S(1)} %get-tuple-element.22.r_ref, f32[40,8192]{1,0:T(8,128)S(1)} %get-tuple-element.15.p_ref), custom_call_target="tpu_custom_call" | custom-call | flops 707788800 | bytes 7864320 | tf_op jit(solution)/shard_map/pallas_call | solution.py:126
  (2 shorter events, 0.0 us)

commit v5 on v4

--- a/solution.py
+++ b/solution.py
@@ -10,7 +10,7 @@
 BS = 512
 LANES = 128
 GROUP = 4
-UNROLL = 64
+GROUP_WIDE = 3
 PARTS = 4
 SPAN = 2048
 MESH = pl.DeviceIdType.MESH
@@ -73,8 +73,8 @@
                 right[i] = right[i] - factor * rows[1][c]
 
 
-def finish_kernel(chunk, scale, packed_ref, x_ref, r_ref, p_ref, basis_ref, projected_ref, inverse_ref, held, sems):
-    columns, wide = x_ref.shape
+def finish_kernel(columns, chunk, scale, packed_ref, split, basis_ref, projected_ref, inverse_ref, held, sems):
+    wide = split.shape[1]
     size = 3 * columns
     packed = packed_ref[...] * scale
     row = lax.broadcasted_iota(jnp.int32, packed.shape, 0)
@@ -88,10 +88,18 @@
     inverse = inverse_ref[...]
     projected = split_dot(split_dot(inverse, gram_a, NN), inverse, NT)
     projected_ref[...] = projected[:size, :size]
+    inverse = jnp.concatenate(
+        [
+            inverse[:, :columns],
+            inverse[:, 2 * columns : size],
+            inverse[:, columns : 2 * columns],
+            inverse[:, size:],
+        ],
+        axis=1,
+    )
     ih = inverse.astype(jnp.bfloat16)
     il = (inverse - ih.astype(jnp.float32)).astype(jnp.bfloat16)
     twice = jnp.concatenate([ih, ih], axis=1)
-    blank = jnp.zeros((LANES - size, chunk), jnp.float32)
 
     def copy(n):
         span = pl.ds(pl.multiple_of(n * chunk, chunk), chunk)
@@ -99,12 +107,8 @@
 
     def step(n, carry):
         span = pl.ds(pl.multiple_of(n * chunk, chunk), chunk)
-        search = jnp.concatenate([x_ref[:, span], r_ref[:, span], p_ref[:, span], blank], axis=0)
-        sh = search.astype(jnp.bfloat16)
-        sl = (search - sh.astype(jnp.float32)).astype(jnp.bfloat16)
-        both = jnp.concatenate([sh, sl], axis=0)
-        out = lax.dot_general(twice, both, NN, preferred_element_type=jnp.float32)
-        out = out + lax.dot_general(il, sh, NN, preferred_element_type=jnp.float32)
+        out = lax.dot_general(twice, split[:, span], NN, preferred_element_type=jnp.float32)
+        out = out + lax.dot_general(il, split[:LANES, span], NN, preferred_element_type=jnp.float32)
         held[n] = out[:size]
         copy(n).start()
         return carry
@@ -118,18 +122,18 @@
     lax.fori_loop(0, wide // chunk, close, 0)
 
 
-def finish(packed, vec_modes, residual_dir, vec_prev, ndof):
-    columns, wide = vec_modes.shape
+def finish(columns, packed, split, ndof):
+    wide = split.shape[1]
     size = 3 * columns
     chunk = min(512, wide)
     vmem = pl.BlockSpec(memory_space=pltpu.VMEM)
     return pl.pallas_call(
-        functools.partial(finish_kernel, chunk, 1.0 / ndof),
+        functools.partial(finish_kernel, columns, chunk, 1.0 / ndof),
         out_shape=(
             jax.ShapeDtypeStruct((1, size, wide), jnp.float32),
             jax.ShapeDtypeStruct((size, size), jnp.float32),
         ),
-        in_specs=[vmem, vmem, vmem, vmem],
+        in_specs=[vmem, vmem],
         out_specs=(pl.BlockSpec(memory_space=pl.ANY), vmem),
         scratch_shapes=[
             pltpu.VMEM((LANES, LANES), jnp.float32),
@@ -140,7 +144,7 @@
             flops=6 * size * size * wide, bytes_accessed=8 * size * wide, transcendentals=0
         ),
         compiler_params=pltpu.CompilerParams(vmem_limit_bytes=24 * 1024 * 1024),
-    )(packed, vec_modes, residual_dir, vec_prev)
+    )(packed, split)
 
 
 def remote(source, target, sems, peer):
@@ -221,8 +225,7 @@
         left.wait_recv()
 
 
-def pick_rows(read, columns, wide, rows, rows_in, picked):
-    slots = picked.shape[0]
+def turn_rows(read, columns, wide, rows_in):
     blank = jnp.zeros((LANES - columns, LANES), jnp.float32)
 
     def turn_in(tile, carry):
@@ -232,30 +235,39 @@
 
     lax.fori_loop(0, wide // LANES, turn_in, 0, unroll=16)
 
+
+def pick_rows(low, high, rows, rows_in, picked):
     def gather(i, carry):
-        for slot in range(UNROLL):
-            at = i * UNROLL + slot
-            picked[pl.ds(at, 1), :] = rows_in[pl.ds(rows[0, at], 1), :]
-        return carry
-
-    lax.fori_loop(0, slots // UNROLL, gather, 0)
-
-
-def send_wet(combine, count, coupling, picked, outgoing, wet, sems, peer):
-    slots = picked.shape[0]
-
-    def weigh(i, carry):
+        for slot in range(LANES):
+            picked[pl.ds(i * LANES + slot, 1), :] = rows_in[pl.ds(rows[i, slot], 1), :]
+        return carry
+
+    lax.fori_loop(low, high, gather, 0)
+
+
+def spread_weights(count, coupling, spread):
+    def one(i, carry):
         span = pl.ds(pl.multiple_of(i * LANES, LANES), LANES)
         used = i * LANES + lax.broadcasted_iota(jnp.int32, (1, LANES), 1) < count
         weights = jnp.where(used, coupling[pl.ds(i, 1), :], 0.0)
-        spread = jnp.broadcast_to(weights, (LANES, LANES)).T
-        outgoing[span, :] = (combine(picked[span, :]) * spread).astype(jnp.bfloat16)
-        return carry
-
-    cells = slots // LANES
+        spread[span, :] = jnp.broadcast_to(weights, (LANES, LANES)).T
+        return carry
+
+    lax.fori_loop(0, coupling.shape[0], one, 0, unroll=4)
+
+
+def send_wet(prepare, combine, spread, picked, outgoing, wet, sems, peer):
+    cells = picked.shape[0] // LANES
+
+    def weigh(i, carry):
+        span = pl.ds(pl.multiple_of(i * LANES, LANES), LANES)
+        outgoing[span, :] = (combine(picked[span, :]) * spread[span, :]).astype(jnp.bfloat16)
+        return carry
+
     copies = []
     for part in range(PARTS):
         low, high = cells * part // PARTS, cells * (part + 1) // PARTS
+        prepare(low, high)
         lax.fori_loop(low, high, weigh, 0, unroll=2)
         span = pl.ds(low * LANES, (high - low) * LANES)
         copy = remote(outgoing.at[span], wet.at[span], (sems[0].at[part], sems[1].at[part]), peer)
@@ -266,7 +278,7 @@
 
 def first_kernel(
     counts, rows_in_hbm, coupling_in, x_in, p_in, tables_in, window, wet, x_ref, p_ref, tables, coupling,
-    rows_in, picked, outgoing, side_send, side_recv, end_send, end_recv, rows, loads,
+    rows_in, picked, spread, outgoing, side_send, side_recv, end_send, end_recv, rows, loads,
 ):
     field = lax.axis_index("field")
     dom = lax.axis_index("dom")
@@ -275,7 +287,7 @@
     nbr = wide // BS
     pairs = [(x_in.at[0], x_ref), (p_in.at[0], p_ref), (rows_in_hbm, rows), (coupling_in, coupling), (tables_in.at[0], tables)]
     arrivals = [pltpu.make_async_copy(source, target, loads.at[n]) for n, (source, target) in enumerate(pairs)]
-    for arrival in arrivals:
+    for arrival in arrivals[:4]:
         arrival.start()
     clear_ends(window, nbr)
     greet([(1 - field, dom)])
@@ -289,17 +301,20 @@
         window[n + 2] = read(span).astype(jnp.bfloat16)
         return carry
 
+    arrivals[3].wait()
+    spread_weights(counts[0], coupling, spread)
     arrivals[0].wait()
     arrivals[1].wait()
+    arrivals[4].start()
     lax.fori_loop(0, nbr, fill, 0, unroll=2)
     meet(dom, ends, 1)
     halos = halo_copies(window, nbr, (end_send, end_recv), field, dom)
     start_halos(halos, dom, ends)
     arrivals[2].wait()
-    arrivals[3].wait()
-    pick_rows(read, 2 * columns, wide, rows, rows_in, picked)
+    turn_rows(read, 2 * columns, wide, rows_in)
     copies = send_wet(
-        lambda cell: cell, counts[0], coupling, picked, outgoing, wet, (side_send, side_recv), (1 - field, dom)
+        lambda low, high: pick_rows(low, high, rows, rows_in, picked),
+        lambda cell: cell, spread, picked, outgoing, wet, (side_send, side_recv), (1 - field, dom),
     )
     arrivals[4].wait()
     finish_halos(halos, dom, ends)
@@ -310,6 +325,7 @@
 def exchange_scratch(wide, slots):
     return [
         pltpu.VMEM((wide, LANES), jnp.float32),
+        pltpu.VMEM((slots, LANES), jnp.float32),
         pltpu.VMEM((slots, LANES), jnp.float32),
         pltpu.VMEM((slots, LANES), jnp.bfloat16),
         pltpu.SemaphoreType.DMA((PARTS,)),
@@ -330,7 +346,7 @@
 
 def exchange_first(modes, previous, wet_rows, wet_counts, coupling, tables):
     _, columns, wide = modes.shape
-    slots = wet_rows.shape[1]
+    slots = wet_rows.size
     held = jax.ShapeDtypeStruct((columns, wide), jnp.float32)
     return pl.pallas_call(
         first_kernel,
@@ -352,19 +368,18 @@
     )(wet_counts, wet_rows, coupling, modes, previous, tables)
 
 
-def gram_over(wide, read, count, out):
+def parts_of(cell):
+    high = cell.astype(jnp.bfloat16)
+    return high, (cell - high.astype(jnp.float32)).astype(jnp.bfloat16)
+
+
+def gram_over(wide, read, out):
     out[...] = jnp.zeros_like(out)
+    count = out.shape[0]
 
     def add(n, carry):
         span = pl.ds(pl.multiple_of(n * SPAN, SPAN), SPAN)
-        left, right = read(span)
-        rh = right.astype(jnp.bfloat16)
-        rl = (right - rh.astype(jnp.float32)).astype(jnp.bfloat16)
-        if left is None:
-            lh, ll = rh[:count], rl[:count]
-        else:
-            lh = left.astype(jnp.bfloat16)
-            ll = (left - lh.astype(jnp.float32)).astype(jnp.bfloat16)
+        (lh, ll), (rh, rl) = read(span)
         both = lax.dot_general(
             jnp.concatenate([lh, ll], axis=0), rh, NT, preferred_element_type=jnp.float32
         )
@@ -403,9 +418,9 @@
 
 
 def second_kernel(
-    rounds, counts, rows_hbm, coupling, x_ref, p_ref, image, jacobi, window, wet, r_ref, gram,
-    rows_in, picked, outgoing, side_send, side_recv, end_send, end_recv,
-    rows, loads, held, landed, sum_send, sum_recv,
+    rounds, counts, rows_hbm, coupling, x_ref, p_ref, image, jacobi, window, wet, gram, split,
+    rows_in, picked, spread, outgoing, side_send, side_recv, end_send, end_recv,
+    rows, loads, held, landed, sum_send, sum_recv, r_ref,
 ):
     field = lax.axis_index("field")
     dom = lax.axis_index("dom")
@@ -446,12 +461,15 @@
         for copy in copies:
             copy.start()
         if turn == 0:
-            pick_rows(
+            turn_rows(
                 lambda span: jnp.concatenate(
                     [image[:columns, span] / jacobi[:, span], x_ref[:, span] / jacobi[:, span]], axis=0
                 ),
-                2 * columns, wide, rows, rows_in, picked,
+                2 * columns, wide, rows_in,
             )
+        if turn == len(groups) - 1:
+            pick_rows(0, rows.shape[0], rows, rows_in, picked)
+            spread_weights(counts[0], coupling, spread)
         for copy in copies:
             copy.wait()
         members = rounds[turn][1]
@@ -474,20 +492,21 @@
     halos = halo_copies(window, nbr, (end_send, end_recv), field, dom)
     start_halos(halos, dom, ends)
     copies = send_wet(
+        lambda low, high: None,
         lambda cell: cell - pltpu.roll(cell, LANES - columns, 1) * across,
-        counts[0], coupling, picked, outgoing, wet, (side_send, side_recv), (1 - field, dom),
+        spread, picked, outgoing, wet, (side_send, side_recv), (1 - field, dom),
     )
     lax.fori_loop(2, nbr - 2, fill, 0)
-    spare = jnp.zeros((gram.shape[1] - 5 * columns, SPAN), jnp.float32)
-    gram_over(
-        wide,
-        lambda span: (
-            None,
-            jnp.concatenate([x_ref[:, span], p_ref[:, span], r_ref[:, span], image[:, span], spare], axis=0),
-        ),
-        gram.shape[0],
-        gram,
-    )
+    blank = jnp.zeros((LANES - 3 * columns, SPAN), jnp.float32)
+
+    def read(span):
+        left = parts_of(jnp.concatenate([x_ref[:, span], p_ref[:, span], r_ref[:, span], blank], axis=0))
+        split[:LANES, span] = left[0]
+        split[LANES:, span] = left[1]
+        right = parts_of(image[:, span])
+        return left, tuple(jnp.concatenate(pair, axis=0) for pair in zip(left, right))
+
+    gram_over(wide, read, gram)
     finish_halos(halos, dom, ends)
     for copy in copies:
         copy.wait()
@@ -495,7 +514,7 @@
 
 def exchange_second(vec_modes, vec_prev, image, jacobi, wet_rows, wet_counts, coupling):
     columns, wide = vec_modes.shape
-    slots = wet_rows.shape[1]
+    slots = wet_rows.size
     rounds = sum_rounds()
     most = 2 * rounds[0][1] - 1
     return pl.pallas_call(
@@ -503,8 +522,8 @@
         out_shape=(
             jax.ShapeDtypeStruct((wide // BS + 5, rows_deep(columns), BS), jnp.bfloat16),
             jax.ShapeDtypeStruct((slots, LANES), jnp.bfloat16),
-            jax.ShapeDtypeStruct((columns, wide), jnp.float32),
-            jax.ShapeDtypeStruct((LANES, rows_deep(5 * columns)), jnp.float32),
+            jax.ShapeDtypeStruct((LANES, LANES + 2 * columns), jnp.float32),
+            jax.ShapeDtypeStruct((2 * LANES, wide), jnp.bfloat16),
         ),
         in_specs=[SMEM, HBM, VMEM, VMEM, VMEM, VMEM, VMEM],
         out_specs=(VMEM,) * 4,
@@ -516,20 +535,21 @@
             pltpu.VMEM((len(rounds), most, SUB, LANES), jnp.float32),
             pltpu.SemaphoreType.DMA((len(rounds), most)),
             pltpu.SemaphoreType.DMA((len(rounds), most)),
+            pltpu.VMEM((columns, wide), jnp.float32),
         ],
         compiler_params=pltpu.CompilerParams(
-            collective_id=3, has_side_effects=True, vmem_limit_bytes=20 * 1024 * 1024
+            collective_id=3, has_side_effects=True, vmem_limit_bytes=24 * 1024 * 1024
         ),
     )(wet_counts, wet_rows, coupling, vec_modes, vec_prev, image, jacobi)
 
 
 def gram_kernel(
-    rounds, x_ref, p_ref, r_ref, image_r, known, o_ref,
+    rounds, split, image_r, known, o_ref,
     fresh, gram_b, gram_a, packed, held, landed, across, send_sem, recv_sem, side_send, side_recv,
 ):
     field = lax.axis_index("field")
     dom = lax.axis_index("dom")
-    columns, wide = x_ref.shape
+    columns, wide = image_r.shape
     groups = []
     for step, members in rounds:
         low = (1 - 2 * ((dom // step) % 2)) * step
@@ -539,14 +559,12 @@
     greet(peers)
     n = columns
     low = jnp.zeros((fresh.shape[0] - n, SPAN), jnp.float32)
-    spare = jnp.zeros((LANES - 3 * n, SPAN), jnp.float32)
     gram_over(
         wide,
         lambda span: (
-            jnp.concatenate([image_r[:, span], low], axis=0),
-            jnp.concatenate([x_ref[:, span], p_ref[:, span], r_ref[:, span], spare], axis=0),
-        ),
-        fresh.shape[0],
+            parts_of(jnp.concatenate([image_r[:, span], low], axis=0)),
+            (split[:LANES, span], split[LANES:, span]),
+        ),
         fresh,
     )
     old = known[...]
@@ -557,7 +575,7 @@
     gram_a[...] = jnp.zeros_like(gram_a)
     x, r, p = slice(0, n), slice(n, 2 * n), slice(2 * n, 3 * n)
     kx, kp, kr = slice(0, n), slice(n, 2 * n), slice(2 * n, 3 * n)
-    ax, ap = slice(3 * n, 4 * n), slice(4 * n, 5 * n)
+    ax, ap = slice(LANES, LANES + n), slice(LANES + n, LANES + 2 * n)
     for rows, here in ((x, kx), (r, kr), (p, kp)):
         gram_a[rows, x] = old[here, ax]
         gram_a[rows, r] = turned[here, :n]
@@ -600,15 +618,15 @@
     o_ref[1 - field] = across[1]
 
 
-def gram_everywhere(vec_modes, vec_prev, residual_dir, image_r, known):
-    columns = vec_modes.shape[0]
+def gram_everywhere(split, image_r, known):
+    columns = image_r.shape[0]
     rounds = sum_rounds()
     slots = len(rounds)
     cell = (LANES // 2, LANES)
     return pl.pallas_call(
         functools.partial(gram_kernel, rounds),
         out_shape=jax.ShapeDtypeStruct((2,) + cell, jnp.float32),
-        in_specs=[VMEM] * 5,
+        in_specs=[VMEM] * 3,
         out_specs=VMEM,
         scratch_shapes=[
             pltpu.VMEM((rows_deep(columns), LANES), jnp.float32),
@@ -626,15 +644,15 @@
         compiler_params=pltpu.CompilerParams(
             collective_id=2, has_side_effects=True, vmem_limit_bytes=16 * 1024 * 1024
         ),
-    )(vec_modes, vec_prev, residual_dir, image_r, known)
-
-
-def group_rows(kind_of, lists, nbr, types, cells):
+    )(split, image_r, known)
+
+
+def group_rows(kind_of, lists, nbr, types, cells, group):
     spare = nbr + 2
     bits = 32 // types
     mask = (1 << bits) - 1
     for offset in range(3):
-        for slot in range(cells * GROUP):
+        for slot in range(cells * group):
             lists[offset, slot] = spare
         first = 2 - offset
         shifts = [kind_of(offset, row) * bits for row in range(first, nbr + 2)]
@@ -648,33 +666,32 @@
         for kind in range(types):
             starts = starts + place * (1 << bits * kind)
             here = lax.shift_right_logical(count, jnp.int32(bits * kind)) & mask
-            place = place + ((here + (GROUP - 1)) & -GROUP)
+            place = place + ((here + (group - 1)) // group) * group
         for n, (shift, rank) in enumerate(zip(shifts, ranks)):
             lists[offset, (lax.shift_right_logical(starts, shift) & mask) + rank] = n + first
 
 
-def operator_kernel(cells, with_diagonal, kinds, scales, rows_hbm, window, wet, tables, o_ref, *rest):
+def operator_kernel(cells, group, with_diagonal, kinds_hbm, scales_hbm, rows_hbm, window, wet, tables, o_ref, *rest):
     if with_diagonal:
-        jacobi, diagonal, total, rows_in, rows_out, lists, rows, loads = rest
+        jacobi, diagonal, total, rows_in, rows_out, lists, rows, kinds, scales, loads = rest
     else:
-        total, rows_in, rows_out, lists, rows, loads = rest
+        total, rows_in, rows_out, lists, rows, kinds, scales, loads = rest
     columns, wide = o_ref.shape
     nbr = wide // BS
     types = tables.shape[1]
     deep = window.shape[1]
     slots = wet.shape[0]
-    arrival = pltpu.make_async_copy(rows_hbm, rows, loads.at[0])
-    arrival.start()
+    pairs = [(rows_hbm, rows), (kinds_hbm, kinds), (scales_hbm, scales)]
+    arrivals = [pltpu.make_async_copy(source, target, loads.at[n]) for n, (source, target) in enumerate(pairs)]
+    for arrival in arrivals:
+        arrival.start()
     base = lax.axis_index("dom") * nbr - 2
-    every = kinds.shape[0] // 3
 
     def kind_of(offset, row):
-        return kinds[offset * every + jnp.maximum(base + row, 0)]
+        return kinds[offset, 0, jnp.maximum(base + row, 0)]
 
     def scale_of(offset, row):
-        return scales[offset * every + jnp.maximum(base + row, 0)]
-
-    group_rows(kind_of, lists, nbr, types, cells)
+        return scales[offset, 0, jnp.maximum(base + row, 0)]
 
     def clear(n, carry):
         total[n] = jnp.zeros(total.shape[1:], jnp.float32)
@@ -690,15 +707,16 @@
         return carry
 
     lax.fori_loop(0, slots // LANES, widen, 0, unroll=4)
-    arrival.wait()
+    for arrival in arrivals:
+        arrival.wait()
 
     def scatter(i, carry):
-        for slot in range(UNROLL):
-            at = i * UNROLL + slot
-            rows_out[pl.ds(rows[0, at], 1), :] = rows_in[pl.ds(at, 1), :]
-        return carry
-
-    lax.fori_loop(0, slots // UNROLL, scatter, 0)
+        for slot in range(LANES):
+            rows_out[pl.ds(rows[i, slot], 1), :] = rows_in[pl.ds(i * LANES + slot, 1), :]
+        return carry
+
+    lax.fori_loop(0, slots // LANES, scatter, 0)
+    group_rows(kind_of, lists, nbr, types, cells, group)
     if with_diagonal:
         eye = lax.broadcasted_iota(jnp.int32, (LANES, LANES), 0) == lax.broadcasted_iota(
             jnp.int32, (LANES, LANES), 1
@@ -713,7 +731,7 @@
 
     def step(i, carry):
         for offset in range(3):
-            found = [lists[offset, i * GROUP + u] for u in range(GROUP)]
+            found = [lists[offset, i * group + u] for u in range(group)]
             held = [jnp.minimum(row, nbr + 1) for row in found]
             kind = kind_of(offset, held[0])
             factors = [scale_of(offset, row) for row in held]
@@ -731,7 +749,7 @@
                     NT if ahead and offset else NN,
                     preferred_element_type=jnp.float32,
                 )
-                for u in range(GROUP):
+                for u in range(group):
                     total[targets[u]] += factors[u] * product[u * deep : (u + 1) * deep]
         return carry
 
@@ -754,23 +772,26 @@
     deep = window.shape[1]
     slots = wet.shape[0]
     types = tables.shape[1]
-    cells = (nbr + 2 + types * (GROUP - 1)) // GROUP
+    group = GROUP_WIDE if columns > LANES // 2 else GROUP
+    cells = (nbr + 2 + types * (group - 1)) // group
     outs = [jax.ShapeDtypeStruct((columns, wide), jnp.float32)]
     scratch = [
         pltpu.VMEM((nbr + 1, deep, BS), jnp.float32),
         pltpu.VMEM((slots, LANES), jnp.float32),
         pltpu.VMEM((wide, LANES), jnp.float32),
-        pltpu.SMEM((3, cells * GROUP), jnp.int32),
+        pltpu.SMEM((3, cells * group), jnp.int32),
         pltpu.SMEM(rows.shape, jnp.int32),
-        pltpu.SemaphoreType.DMA((1,)),
+        pltpu.SMEM(kinds.shape, jnp.int32),
+        pltpu.SMEM(scales.shape, jnp.float32),
+        pltpu.SemaphoreType.DMA((3,)),
     ]
     if with_diagonal:
         outs.append(jax.ShapeDtypeStruct((1, wide), jnp.float32))
         scratch = [pltpu.VMEM((types, 1, BS), jnp.float32)] + scratch
     return pl.pallas_call(
-        functools.partial(operator_kernel, cells, with_diagonal),
+        functools.partial(operator_kernel, cells, group, with_diagonal),
         out_shape=tuple(outs),
-        in_specs=[SMEM, SMEM, HBM, VMEM, VMEM, VMEM],
+        in_specs=[HBM, HBM, HBM, VMEM, VMEM, VMEM],
         out_specs=(VMEM,) * len(outs),
         scratch_shapes=scratch,
         cost_estimate=pl.CostEstimate(
@@ -781,22 +802,31 @@
 
 
 def shards(modes, previous, kinds, scales, tables, wet_rows, wet_counts, coupling):
-    modes, previous, tables, wet_rows, coupling = [
-        pltpu.with_memory_space_constraint(a, pltpu.HBM) for a in (modes, previous, tables, wet_rows, coupling.reshape(-1, LANES))
+    modes, previous, tables, wet_rows, coupling, kinds, scales = [
+        pltpu.with_memory_space_constraint(array, pltpu.HBM)
+        for array in (
+            modes,
+            previous,
+            tables,
+            wet_rows.reshape(-1, LANES),
+            coupling.reshape(-1, LANES),
+            jnp.swapaxes(kinds, 0, 1),
+            jnp.swapaxes(scales, 0, 1),
+        )
     ]
     _, columns, wide = modes.shape
     window, wet, vec_modes, vec_prev, field_tables, weights = exchange_first(
         modes, previous, wet_rows, wet_counts, coupling, tables
     )
-    shared = (kinds.reshape(-1), scales.reshape(-1), wet_rows, field_tables)
+    shared = (kinds, scales, wet_rows, field_tables)
     image, jacobi = operate(2 * columns, window, wet, *shared, True)
-    window, wet, residual_dir, known = exchange_second(
+    window, wet, known, split = exchange_second(
         vec_modes, vec_prev, image, jacobi, wet_rows, wet_counts, weights
     )
     (image_r,) = operate(columns, window, wet, *shared, False)
-    packed = gram_everywhere(vec_modes, vec_prev, residual_dir, image_r, known)
+    packed = gram_everywhere(split, image_r, known)
     ndof = 2.0 * lax.axis_size("dom") * wide
-    return finish(packed.reshape(LANES, LANES), vec_modes, residual_dir, vec_prev, ndof)
+    return finish(columns, packed.reshape(LANES, LANES), split, ndof)
 
 
 def solution(mesh):

time: 79.3 us -> 76.9 us (0.970)
  other arithmetic: 1.41 us -> 0 us
  Pallas kernels: 76.2 us -> 75.1 us
    pallas_call x3, Pallas kernels: 33.2 us -> 31.7 us  [the longest x2 23.2 us: operate(): pl.pallas_call(functools.partial(operator_kernel, cells, group, with_diag...]
    unnamed x2 -> x0, other arithmetic: 1.41 us -> none
where the time goes in v5:
time: 76.9 us; the launch traced here: 76.4 us
  Pallas kernels  75.1 us (98%)
  between operations  1.32 us (2%)
    pallas_call x2, Pallas kernels, operate(): pl.pallas_call(functools.partial(operator_kernel, cells, group, with_diag...  23.2 us
    pallas_call x1, Pallas kernels, exchange_second(): pl.pallas_call(functools.partial(second_kernel, rounds), out_shape=(jax.S...  18.6 us
    pallas_call x1, Pallas kernels, gram_everywhere(): pl.pallas_call(functools.partial(gram_kernel, rounds), out_shape=jax.Shap...  14 us
    pallas_call x1, Pallas kernels, exchange_first(): pl.pallas_call(first_kernel, out_shape=(jax.ShapeDtypeStruct((wide // BS...  10.8 us
    pallas_call x1, Pallas kernels, finish(): pl.pallas_call(functools.partial(finish_kernel, columns, chunk, 1.0 / ndo...  8.48 us

profile of v5, /device:TPU:0, one launch (start us, length us, event | category | flops | bytes accessed | tf_op | source)
XLA Modules:
  0.0 76.4 jit_solution(14010088534113662533)
XLA Ops:
  1.3 10.8 %shard_map.95 = (bf16[21,80,512]{2,1,0:T(8,128)(2,1)S(1)}, bf16[3072,128]{1,0:T(8,128)(2,1)S(1)}, f32[40,8192]{1,0:T(8,128)S(1)}, f32[40,8192]{1,0:T(8,128)S(1)}...) custom-call(s32[1]{0:T(128)S(6)} %copy.10.counts, s32[24,128]{1,0:T(8,128)} %bitcast.6, f32[24,128]{1,0:T(8,128)} %bitcast.10, ...), custom_call_target="tpu_custom_call" | custom-call | tf_op jit(solution)/shard_map/pallas_call | solution.py:351
  12.0 11.9 %shard_map.96 = (f32[80,8192]{1,0:T(8,128)S(1)}, f32[1,8192]{1,0:T(1,128)S(1)}) custom-call(s32[3,1,256]{2,1,0:T(1,128)} %bitcast.11, f32[3,1,256]{2,1,0:T(1,128)} %bitcast.13, s32[24,128]{1,0:T(8,128)} %bitcast.7, bf16[21,80,512]{2,1,0:T(8,128)(2,1)S(1)} %get-tuple-element.17.window, bf16[3072,128]{1,0:T(8,128)(2,1)S(1)} %get-tuple-element.18.wet, ...), custom_call_target="tpu_custom_call" | custom-call | flops 3355443200 | bytes 10485760 | tf_op jit(solution)/shard_map/pallas_call | solution.py:791
  24.0 18.6 %shard_map.97 = (bf16[21,48,512]{2,1,0:T(8,128)(2,1)S(1)}, bf16[3072,128]{1,0:T(8,128)(2,1)S(1)}, f32[128,208]{1,0:T(8,128)S(1)}, bf16[256,8192]{1,0:T(8,128)(2,1)S(1)}) custom-call(s32[1]{0:T(128)S(6)} %copy.10.counts, s32[24,128]{1,0:T(8,128)} %bitcast.8, f32[24,128]{1,0:T(8,128)S(1)} %get-tuple-element.14.coupling, ...), custom_call_target="tpu_custom_call" | custom-call | tf_op jit(solution)/shard_map/pallas_call | solution.py:520
  42.6 11.3 %shard_map.98.image_r = f32[40,8192]{1,0:T(8,128)S(1)} custom-call(s32[3,1,256]{2,1,0:T(1,128)} %bitcast.12, f32[3,1,256]{2,1,0:T(1,128)} %bitcast.14, s32[24,128]{1,0:T(8,128)} %bitcast.9, bf16[21,48,512]{2,1,0:T(8,128)(2,1)S(1)} %get-tuple-element.23.window, bf16[3072,128]{1,0:T(8,128)(2,1)S(1)} %get-tuple-element.24.wet, ...), custom_call_target="tpu_custom_call" | custom-call | flops 1677721600 | bytes 5242880 | tf_op jit(solution)/shard_map/pallas_call | solution.py:791
  53.9 14.0 %shard_map.99 = f32[2,64,128]{2,1,0:T(8,128)S(1)} custom-call(bf16[256,8192]{1,0:T(8,128)(2,1)S(1)} %get-tuple-element.22.split, f32[40,8192]{1,0:T(8,128)S(1)} %shard_map.98.image_r, f32[128,208]{1,0:T(8,128)S(1)} %get-tuple-element.25.known), custom_call_target="tpu_custom_call" | custom-call | tf_op jit(solution)/shard_map/pallas_call | solution.py:626
  67.9 8.5 %shard_map.100 = (f32[1,120,8192]{2,1,0:T(8,128)}, f32[120,120]{1,0:T(8,128)}) custom-call(f32[128,128]{1,0:T(8,128)S(1)} %bitcast.5, bf16[256,8192]{1,0:T(8,128)(2,1)S(1)} %get-tuple-element.22.split), custom_call_target="tpu_custom_call" | custom-call | flops 707788800 | bytes 7864320 | tf_op jit(solution)/shard_map/pallas_call | solution.py:130

commit v6 on v5

--- a/solution.py
+++ b/solution.py
@@ -9,7 +9,7 @@
 
 BS = 512
 LANES = 128
-GROUP = 4
+GROUP = 5
 GROUP_WIDE = 3
 PARTS = 4
 SPAN = 2048
@@ -113,7 +113,7 @@
         copy(n).start()
         return carry
 
-    lax.fori_loop(0, wide // chunk, step, 0, unroll=2)
+    lax.fori_loop(0, wide // chunk, step, 0, unroll=4)
 
     def close(n, carry):
         copy(n).wait()
@@ -277,7 +277,8 @@
 
 
 def first_kernel(
-    counts, rows_in_hbm, coupling_in, x_in, p_in, tables_in, window, wet, x_ref, p_ref, tables, coupling,
+    counts, rows_in_hbm, coupling_in, x_in, p_in, tables_in, kinds_in, scales_in,
+    window, wet, x_ref, p_ref, tables, coupling, rows_out, kinds_out, scales_out,
     rows_in, picked, spread, outgoing, side_send, side_recv, end_send, end_recv, rows, loads,
 ):
     field = lax.axis_index("field")
@@ -286,6 +287,7 @@
     columns, wide = x_ref.shape
     nbr = wide // BS
     pairs = [(x_in.at[0], x_ref), (p_in.at[0], p_ref), (rows_in_hbm, rows), (coupling_in, coupling), (tables_in.at[0], tables)]
+    pairs += [(rows_in_hbm, rows_out), (kinds_in, kinds_out), (scales_in, scales_out)]
     arrivals = [pltpu.make_async_copy(source, target, loads.at[n]) for n, (source, target) in enumerate(pairs)]
     for arrival in arrivals[:4]:
         arrival.start()
@@ -305,7 +307,8 @@
     spread_weights(counts[0], coupling, spread)
     arrivals[0].wait()
     arrivals[1].wait()
-    arrivals[4].start()
+    for arrival in arrivals[4:]:
+        arrival.start()
     lax.fori_loop(0, nbr, fill, 0, unroll=2)
     meet(dom, ends, 1)
     halos = halo_copies(window, nbr, (end_send, end_recv), field, dom)
@@ -316,7 +319,8 @@
         lambda low, high: pick_rows(low, high, rows, rows_in, picked),
         lambda cell: cell, spread, picked, outgoing, wet, (side_send, side_recv), (1 - field, dom),
     )
-    arrivals[4].wait()
+    for arrival in arrivals[4:]:
+        arrival.wait()
     finish_halos(halos, dom, ends)
     for copy in copies:
         copy.wait()
@@ -344,7 +348,7 @@
 HBM = pl.BlockSpec(memory_space=pltpu.HBM)
 
 
-def exchange_first(modes, previous, wet_rows, wet_counts, coupling, tables):
+def exchange_first(modes, previous, wet_rows, wet_counts, coupling, tables, kinds, scales):
     _, columns, wide = modes.shape
     slots = wet_rows.size
     held = jax.ShapeDtypeStruct((columns, wide), jnp.float32)
@@ -357,15 +361,18 @@
             held,
             jax.ShapeDtypeStruct(tables.shape[1:], tables.dtype),
             jax.ShapeDtypeStruct(coupling.shape, coupling.dtype),
-        ),
-        in_specs=[SMEM, HBM, HBM, HBM, HBM, HBM],
-        out_specs=(VMEM,) * 6,
+            jax.ShapeDtypeStruct(wet_rows.shape, wet_rows.dtype),
+            jax.ShapeDtypeStruct(kinds.shape, kinds.dtype),
+            jax.ShapeDtypeStruct(scales.shape, scales.dtype),
+        ),
+        in_specs=[SMEM] + [HBM] * 7,
+        out_specs=(VMEM,) * 9,
         scratch_shapes=exchange_scratch(wide, slots)
-        + [pltpu.SMEM(wet_rows.shape, jnp.int32), pltpu.SemaphoreType.DMA((5,))],
+        + [pltpu.SMEM(wet_rows.shape, jnp.int32), pltpu.SemaphoreType.DMA((8,))],
         compiler_params=pltpu.CompilerParams(
             collective_id=1, has_side_effects=True, vmem_limit_bytes=24 * 1024 * 1024
         ),
-    )(wet_counts, wet_rows, coupling, modes, previous, tables)
+    )(wet_counts, wet_rows, coupling, modes, previous, tables, kinds, scales)
 
 
 def parts_of(cell):
@@ -525,7 +532,7 @@
             jax.ShapeDtypeStruct((LANES, LANES + 2 * columns), jnp.float32),
             jax.ShapeDtypeStruct((2 * LANES, wide), jnp.bfloat16),
         ),
-        in_specs=[SMEM, HBM, VMEM, VMEM, VMEM, VMEM, VMEM],
+        in_specs=[SMEM, VMEM, VMEM, VMEM, VMEM, VMEM, VMEM],
         out_specs=(VMEM,) * 4,
         scratch_shapes=exchange_scratch(wide, slots)
         + [
@@ -710,12 +717,10 @@
     for arrival in arrivals:
         arrival.wait()
 
-    def scatter(i, carry):
+    for i in range(slots // LANES):
         for slot in range(LANES):
-            rows_out[pl.ds(rows[i, slot], 1), :] = rows_in[pl.ds(i * LANES + slot, 1), :]
-        return carry
-
-    lax.fori_loop(0, slots // LANES, scatter, 0)
+            at = i * LANES + slot
+            rows_out[pl.ds(rows[i, slot], 1), :] = rows_in[at : at + 1, :]
     group_rows(kind_of, lists, nbr, types, cells, group)
     if with_diagonal:
         eye = lax.broadcasted_iota(jnp.int32, (LANES, LANES), 0) == lax.broadcasted_iota(
@@ -729,7 +734,14 @@
         for n in range(nbr):
             jacobi[:, n * BS : (n + 1) * BS] = scale_of(0, n + 2) * diagonal[kind_of(0, n + 2)]
 
+    tiles = wide // LANES
+    share = -(-tiles // cells)
+
     def step(i, carry):
+        for part in range(share):
+            tile = jnp.minimum(i * share + part, tiles - 1)
+            span = pl.ds(pl.multiple_of(tile * LANES, LANES), LANES)
+            o_ref[:, span] = rows_out[span, :].T[:columns]
         for offset in range(3):
             found = [lists[offset, i * group + u] for u in range(group)]
             held = [jnp.minimum(row, nbr + 1) for row in found]
@@ -753,17 +765,14 @@
                     total[targets[u]] += factors[u] * product[u * deep : (u + 1) * deep]
         return carry
 
-    lax.fori_loop(0, cells, step, 0)
-    parts = BS // LANES
-
-    def turn_out(n, carry):
-        for part in range(parts):
-            span = pl.ds(pl.multiple_of(n * BS + part * LANES, LANES), LANES)
-            inner = slice(part * LANES, (part + 1) * LANES)
-            o_ref[:, span] = total[n, :columns, inner] + rows_out[span, :].T[:columns]
-        return carry
-
-    lax.fori_loop(0, nbr, turn_out, 0, unroll=4)
+    lax.fori_loop(0, cells, step, 0, unroll=2)
+
+    def close(n, carry):
+        span = pl.ds(pl.multiple_of(n * BS, BS), BS)
+        o_ref[:, span] = o_ref[:, span] + total[n, :columns]
+        return carry
+
+    lax.fori_loop(0, nbr, close, 0, unroll=2)
 
 
 def operate(columns, window, wet, kinds, scales, rows, tables, with_diagonal):
@@ -791,7 +800,7 @@
     return pl.pallas_call(
         functools.partial(operator_kernel, cells, group, with_diagonal),
         out_shape=tuple(outs),
-        in_specs=[HBM, HBM, HBM, VMEM, VMEM, VMEM],
+        in_specs=[VMEM] * 6,
         out_specs=(VMEM,) * len(outs),
         scratch_shapes=scratch,
         cost_estimate=pl.CostEstimate(
@@ -815,8 +824,8 @@
         )
     ]
     _, columns, wide = modes.shape
-    window, wet, vec_modes, vec_prev, field_tables, weights = exchange_first(
-        modes, previous, wet_rows, wet_counts, coupling, tables
+    window, wet, vec_modes, vec_prev, field_tables, weights, wet_rows, kinds, scales = exchange_first(
+        modes, previous, wet_rows, wet_counts, coupling, tables, kinds, scales
     )
     shared = (kinds, scales, wet_rows, field_tables)
     image, jacobi = operate(2 * columns, window, wet, *shared, True)

time: 76.9 us -> 70.9 us (0.922)
  Pallas kernels: 75.1 us -> 69.2 us
    pallas_call x2, Pallas kernels: 23.2 us -> 17.9 us  [operate(): pl.pallas_call(functools.partial(operator_kernel, cells, group, with_diag...]
where the time goes in v6:
time: 70.9 us; the launch traced here: 70.7 us
  Pallas kernels  69.2 us (98%)
  between operations  1.48 us (2%)
    pallas_call x1, Pallas kernels, exchange_second(): pl.pallas_call(functools.partial(second_kernel, rounds), out_shape=(jax.S...  18.6 us
    pallas_call x2, Pallas kernels, operate(): pl.pallas_call(functools.partial(operator_kernel, cells, group, with_diag...  17.9 us
    pallas_call x1, Pallas kernels, gram_everywhere(): pl.pallas_call(functools.partial(gram_kernel, rounds), out_shape=jax.Shap...  14 us
    pallas_call x1, Pallas kernels, exchange_first(): pl.pallas_call(first_kernel, out_shape=(jax.ShapeDtypeStruct((wide // BS...  10.8 us
    pallas_call x1, Pallas kernels, finish(): pl.pallas_call(functools.partial(finish_kernel, columns, chunk, 1.0 / ndo...  7.91 us

profile of v6, /device:TPU:0, one launch (start us, length us, event | category | flops | bytes accessed | tf_op | source)
XLA Modules:
  0.0 70.7 jit_solution(14181856843348720978)
XLA Ops:
  1.3 10.8 %shard_map.95 = (bf16[21,80,512]{2,1,0:T(8,128)(2,1)S(1)}, bf16[3072,128]{1,0:T(8,128)(2,1)S(1)}, f32[40,8192]{1,0:T(8,128)S(1)}, f32[40,8192]{1,0:T(8,128)S(1)}...) custom-call(s32[1]{0:T(128)S(6)} %copy.10.counts, ...), custom_call_target="tpu_custom_call" | custom-call | tf_op jit(solution)/shard_map/pallas_call | solution.py:355
  12.1 9.8 %shard_map.96 = (f32[80,8192]{1,0:T(8,128)S(1)}, f32[1,8192]{1,0:T(1,128)S(1)}) custom-call(s32[3,1,256]{2,1,0:T(1,128)S(1)} %get-tuple-element.21.kinds_hbm, f32[3,1,256]{2,1,0:T(1,128)S(1)} %get-tuple-element.22.scales_hbm, s32[24,128]{1,0:T(8,128)S(1)} %get-tuple-element.17.rows_hbm, bf16[21,80,512]{2,1,0:T(8,128)(2,1)S(1)} %get-tuple-element.23.window, ...), custom_call_target="tpu_custom_call" | custom-call | flops 3355443200 | bytes 10485760 | tf_op jit(solution)/shard_map/pallas_call | solution.py:800
  21.9 18.6 %shard_map.97 = (bf16[21,48,512]{2,1,0:T(8,128)(2,1)S(1)}, bf16[3072,128]{1,0:T(8,128)(2,1)S(1)}, f32[128,208]{1,0:T(8,128)S(1)}, bf16[256,8192]{1,0:T(8,128)(2,1)S(1)}) custom-call(s32[1]{0:T(128)S(6)} %copy.10.counts, s32[24,128]{1,0:T(8,128)S(1)} %get-tuple-element.17.rows_hbm, f32[24,128]{1,0:T(8,128)S(1)} %get-tuple-element.18.coupling, ...), custom_call_target="tpu_custom_call" | custom-call | tf_op jit(solution)/shard_map/pallas_call | solution.py:527
  40.6 8.0 %shard_map.98.image_r = f32[40,8192]{1,0:T(8,128)S(1)} custom-call(s32[3,1,256]{2,1,0:T(1,128)S(1)} %get-tuple-element.21.kinds_hbm, f32[3,1,256]{2,1,0:T(1,128)S(1)} %get-tuple-element.22.scales_hbm, s32[24,128]{1,0:T(8,128)S(1)} %get-tuple-element.17.rows_hbm, bf16[21,48,512]{2,1,0:T(8,128)(2,1)S(1)} %get-tuple-element.29.window, ...), custom_call_target="tpu_custom_call" | custom-call | flops 1677721600 | bytes 5242880 | tf_op jit(solution)/shard_map/pallas_call | solution.py:800
  48.6 14.0 %shard_map.99 = f32[2,64,128]{2,1,0:T(8,128)S(1)} custom-call(bf16[256,8192]{1,0:T(8,128)(2,1)S(1)} %get-tuple-element.28.split, f32[40,8192]{1,0:T(8,128)S(1)} %shard_map.98.image_r, f32[128,208]{1,0:T(8,128)S(1)} %get-tuple-element.31.known), custom_call_target="tpu_custom_call" | custom-call | tf_op jit(solution)/shard_map/pallas_call | solution.py:633
  62.6 7.9 %shard_map.100 = (f32[1,120,8192]{2,1,0:T(8,128)}, f32[120,120]{1,0:T(8,128)}) custom-call(f32[128,128]{1,0:T(8,128)S(1)} %bitcast.5, bf16[256,8192]{1,0:T(8,128)(2,1)S(1)} %get-tuple-element.28.split), custom_call_target="tpu_custom_call" | custom-call | flops 707788800 | bytes 7864320 | tf_op jit(solution)/shard_map/pallas_call | solution.py:130
